TPU v7x, 128 devices: a whole 4x4x4 slice. The times are simulated.
128 devices in a mesh: lon: 8 (over x, y_hi), lat: 4 (over z), tm: 4 (over y_lo, core).
Axes of the slice: x: 4, y: 4 (y_hi: 2, y_lo: 2; y = y_hi * 2 + y_lo), z: 4, core: 2. Of those that a mesh axis runs over, the one named last changes fastest.
Arguments:
- precip: float32 [128, 1024, 1024], P('tm', 'lat', 'lon'), may hold values from 0.02 to 8
- offset: float32 [128, 1024, 1024], P('tm', 'lat', 'lon'), may hold values from -3 to 3
- coefficients: float32 [32, 256, 256], P('tm', 'lat', 'lon'), may hold values from -2 to 2
- inverse_diag: float32 [32, 256, 256], P('tm', 'lat', 'lon'), may hold values from 0.02 to 0.2
Outputs:
- newton_step: float32 [32, 256, 256], P('tm', 'lat', 'lon')
- residual: float32 [32, 256, 256], P('tm', 'lat', 'lon')
All inputs are finite; a program needn't handle non-finite values.
Results may differ from a plain program's by a relative error of at most 0.0003.
Values sent between devices are 32-bit elements; how exact they have to be, the bound alone decides.
No kernel may reach another device: no remote copies, remote signals or barrier semaphores. Data moves between devices by JAX's collectives and lax.ppermute only.
A program may use at most 64 MiB of HBM per device.

v0:
```python
import jax
import jax.numpy as jnp
from jax import lax
from jax.sharding import PartitionSpec as P

SPLIT = ("tm", "lat", "lon")
tweedie_power = 1.6
smooth = 0.5
highest = lax.Precision.HIGHEST


def spline(offsets):
    distance = jnp.abs(offsets)
    near_part = (4.0 - 6.0 * distance * distance + 3.0 * distance * distance * distance) / 6.0
    far_part = jnp.maximum(2.0 - distance, 0.0) ** 3 / 6.0
    return jnp.where(distance < 1.0, near_part, far_part)


def synth_table(cell_count, knot_count):
    cell_pos = jnp.arange(cell_count, dtype=jnp.float32)[:, None]
    knot_pos = jnp.arange(knot_count + 4, dtype=jnp.float32)[None, :] - 2.0
    return spline((cell_pos - 4.0 * knot_pos - 1.5) / 4.0)


def matchings(count):
    first = [(i, i ^ 1) for i in range(count)]
    second = [(i, ((i + 1) ^ 1) - 1) for i in range(count)]
    return first, [(i, j % count) for i, j in second]


def swap_sides(to_left, to_right, axis):
    first, second = matchings(lax.axis_size(axis))
    odd = lax.axis_index(axis) % 2 == 1
    got_first = lax.ppermute(jnp.where(odd, to_left, to_right), axis, first)
    got_second = lax.ppermute(jnp.where(odd, to_right, to_left), axis, second)
    return jnp.where(odd, got_first, got_second), jnp.where(odd, got_second, got_first)


def inside(axis):
    index = lax.axis_index(axis)
    if axis == "lon":
        return 1.0, 1.0
    return (index > 0).astype(jnp.float32), (index < lax.axis_size(axis) - 1).astype(jnp.float32)


def cut(values, dim, start, stop):
    return lax.slice_in_dim(values, start, stop, axis=dim)


def expand(values):
    for dim, axis in ((1, "tm"), (2, "lat"), (3, "lon")):
        count = values.shape[dim]
        left, right = swap_sides(cut(values, dim, 0, 2), cut(values, dim, count - 2, count), axis)
        has_left, has_right = inside(axis)
        values = jnp.concatenate([left * has_left, values, right * has_right], axis=dim)
    return values


def merge(partial_sums):
    for dim, axis in ((0, "tm"), (1, "lat"), (2, "lon")):
        size = partial_sums.shape[dim]
        head, tail = cut(partial_sums, dim, 0, 4), cut(partial_sums, dim, size - 4, size)
        left, right = swap_sides(head, tail, axis)
        has_left, has_right = inside(axis)
        partial_sums = jnp.concatenate(
            [head + left * has_left, cut(partial_sums, dim, 4, size - 4), tail + right * has_right], axis=dim
        )
    return partial_sums


def evaluate(padded, tables):
    time_tab, lat_tab, lon_tab = tables
    partial_value = jnp.einsum("tae,le->tal", padded, lon_tab, precision=highest)
    partial_value = jnp.einsum("tal,ba->tbl", partial_value, lat_tab, precision=highest)
    return jnp.einsum("tbl,st->sbl", partial_value, time_tab, precision=highest)


def adjoint(cell_values, tables):
    time_tab, lat_tab, lon_tab = tables
    partial_value = jnp.einsum("sbl,st->tbl", cell_values, time_tab, precision=highest)
    partial_value = jnp.einsum("tbl,ba->tal", partial_value, lat_tab, precision=highest)
    return jnp.einsum("tal,le->tae", partial_value, lon_tab, precision=highest)


def penalty(padded):
    summed = jnp.zeros_like(padded)
    own = padded[2:-2, 2:-2, 2:-2]
    for dim, axis in ((0, "tm"), (1, "lat"), (2, "lon")):
        lines = padded[tuple(slice(None) if d == dim else slice(2, -2) for d in range(3))]
        size = lines.shape[dim]
        second = (
            cut(lines, dim, 0, size - 2) - 2.0 * cut(lines, dim, 1, size - 1) + cut(lines, dim, 2, size)
        )
        has_left, has_right = inside(axis)
        place = jnp.arange(size - 2).reshape([-1 if d == dim else 1 for d in range(3)])
        second = second * jnp.where(place == 0, 1.0 - has_left, jnp.where(place == size - 3, 1.0 - has_right, 1.0))
        spread = jnp.pad(second, [(2, 2) if d == dim else (0, 0) for d in range(3)])
        line_part = cut(spread, dim, 0, size) - 2.0 * cut(spread, dim, 1, size + 1) + cut(spread, dim, 2, size + 2)
        summed = summed + jnp.pad(line_part, [(0, 0) if d == dim else (2, 2) for d in range(3)])
    return smooth * summed


def all_sum(values):
    for axis, distances in (("tm", (1, 2, 3)), ("lat", (1, 2, 3)), ("lon", (2, 4, 6)), ("lon", (1,))):
        count = lax.axis_size(axis)
        values = values + sum(lax.ppermute(values, axis, [(i, i ^ d) for i in range(count)]) for d in distances)
    return values


def core(padded):
    return padded[2:-2, 2:-2, 2:-2]


def per_device(precip, offset, coefficients, inverse_diag):
    counts = coefficients.shape
    tables = tuple(synth_table(cells, knots) for cells, knots in zip(precip.shape, counts))
    lat_cells = precip.shape[1]
    lat_total = lat_cells * lax.axis_size("lat")
    lat_index = (lax.axis_index("lat") * lat_cells + jnp.arange(lat_cells, dtype=jnp.int32)).astype(jnp.float32)
    area_weight = jnp.cos((90.0 - (lat_index + 0.5) * 180.0 / lat_total) * (jnp.pi / 180.0))[None, :, None]

    both = expand(jnp.stack([coefficients, inverse_diag]))
    padded, diag = both[0], both[1]
    linear = offset + evaluate(padded, tables)
    rate = jnp.exp((2.0 - tweedie_power) * linear)
    weight = area_weight * rate
    slope = weight - area_weight * precip * jnp.exp((1.0 - tweedie_power) * linear)
    residual = -merge(adjoint(slope, tables) + penalty(padded))
    direction = diag * residual
    image_part = adjoint(weight * evaluate(direction, tables), tables) + penalty(direction)
    norm, curvature = all_sum(jnp.stack([jnp.sum(core(residual * direction)), jnp.sum(direction * image_part)]))
    image = merge(image_part)
    step_size = norm / curvature
    residual_next = residual - step_size * image
    scaled = diag * residual_next
    scaled_part = adjoint(weight * evaluate(scaled, tables), tables) + penalty(scaled)
    next_norm, curvature = all_sum(jnp.stack([jnp.sum(core(residual_next * scaled)), jnp.sum(scaled * scaled_part)]))
    scaled_image = core(merge(scaled_part))
    ratio = next_norm / norm
    step_next = next_norm / (curvature - ratio * next_norm / step_size)
    direction_own = core(direction)
    newton_step = step_size * direction_own + step_next * (core(scaled) + ratio * direction_own)
    last = core(residual_next) - step_next * (scaled_image + ratio * core(image))
    return newton_step, last


def solution(mesh):
    return jax.shard_map(
        per_device, mesh=mesh, in_specs=(P(*SPLIT),) * 4, out_specs=(P(*SPLIT),) * 2, check_vma=False
    )
```

profile of v0, /device:TPU:0, one launch (start us, length us, event | category | flops | bytes accessed | tf_op | source)
XLA Modules:
  0.0 183.8 jit_solution(14610448820307698269)
XLA Ops:
  3.6 2.2 %collective-permute-done.1 = f32[2,2,64,32]{2,3,1,0:T(8,128)S(1)} collective-permute-done((f32[2,2,64,32]{2,3,1,0:T(8,128)S(1)}, f32[2,2,64,32]{2,3,1,0:T(8,128)S(1)}, u32[]{:S(2)}, u32[]{:S(2)}) %collective-permute-start.1) | collective-permute-done | bytes 32800 | tf_op jit(solution)/shard_map/ppermute | solution.py:35
  7.0 2.2 %collective-permute-start.2 = (f32[2,12,2,32]{2,3,1,0:T(8,128)S(1)}, f32[2,12,2,32]{2,3,1,0:T(8,128)S(1)}, u32[]{:S(2)}, u32[]{:S(2)}) collective-permute-start(f32[2,12,2,32]{2,3,1,0:T(8,128)S(1)} %get-tuple-element.36), channel_id=1, source_target_pairs={{0,4},{4,0},{8,12},{12,8},{1,5},{5,1},{9,13},{13,9},{2,6},{6,2},{1... | collective-permute-start | bytes 18440 | tf_op jit(solution)/shard_map/ppermute | solution.py:34
  9.2 2.5 %collective-permute-start.3 = (f32[2,12,2,32]{2,3,1,0:T(8,128)S(1)}, f32[2,12,2,32]{2,3,1,0:T(8,128)S(1)}, u32[]{:S(2)}, u32[]{:S(2)}) collective-permute-start(f32[2,12,2,32]{2,3,1,0:T(8,128)S(1)} %get-tuple-element.37), channel_id=1, source_target_pairs={{0,12},{4,8},{8,4},{12,0},{1,13},{5,9},{9,5},{13,1},{2,14},{6,10},... | collective-permute-start | bytes 18440 | tf_op jit(solution)/shard_map/ppermute | solution.py:35
  11.8 6.9 %collective-permute-done.2 = f32[2,12,2,32]{2,3,1,0:T(8,128)S(1)} collective-permute-done((f32[2,12,2,32]{2,3,1,0:T(8,128)S(1)}, f32[2,12,2,32]{2,3,1,0:T(8,128)S(1)}, u32[]{:S(2)}, u32[]{:S(2)}) %collective-permute-start.2) | collective-permute-done | bytes 6176 | tf_op jit(solution)/shard_map/ppermute | solution.py:34
  18.6 2.7 %collective-permute-done.3 = f32[2,12,2,32]{2,3,1,0:T(8,128)S(1)} collective-permute-done((f32[2,12,2,32]{2,3,1,0:T(8,128)S(1)}, f32[2,12,2,32]{2,3,1,0:T(8,128)S(1)}, u32[]{:S(2)}, u32[]{:S(2)}) %collective-permute-start.3) | collective-permute-done | bytes 6176 | tf_op jit(solution)/shard_map/ppermute | solution.py:35
  21.6 5.6 %collective-permute-start.5 = (f32[2,12,68,2]{2,3,1,0:T(2,128)S(1)}, f32[2,12,68,2]{2,3,1,0:T(2,128)S(1)}, u32[]{:S(2)}, u32[]{:S(2)}) collective-permute-start(f32[2,12,68,2]{2,3,1,0:T(2,128)S(1)} %bitcast.143), channel_id=1, source_target_pairs={{0,112},{16,32},{32,16},{48,64},{64,48},{80,96},{96,80},{112,0},{1... | collective-permute-start | bytes 39176 | tf_op jit(solution)/shard_map/ppermute | solution.py:35
  29.2 3.5 %collective-permute-done.4 = f32[2,12,68,2]{2,3,1,0:T(2,128)S(1)} collective-permute-done((f32[2,12,68,2]{2,3,1,0:T(2,128)S(1)}, f32[2,12,68,2]{2,3,1,0:T(2,128)S(1)}, u32[]{:S(2)}, u32[]{:S(2)}) %collective-permute-start.4) | collective-permute-done | bytes 13088 | tf_op jit(solution)/shard_map/ppermute | solution.py:34
  35.5 6.4 %copy_add_fusion = f32[32,256,128]{2,0,1:T(8,128)S(1)} fusion(f32[32,256,128]{2,1,0:T(8,128)S(1)} %copy-done.2, f32[256,12,128]{2,0,1:T(8,128)S(1)} %fusion.97, f32[12]{0:T(128)S(1)} %add_multiply_fusion.1), kind=kOutput, calls=%fused_computation.4 | convolution fusion | flops 152050816 | bytes 9961520 | tf_op jit(solution)/shard_map/tbl,st->sbl/dot_general | solution.py:75
  41.9 5.5 %fusion.2 = f32[12,256,128]{2,0,1:T(8,128)S(1)} fusion(f32[32,256,128]{2,1,0:T(8,128)S(1)} %copy-done.3, f32[32,256,128]{2,0,1:T(8,128)S(1)} %copy_add_fusion, f32[256]{0:T(256)S(1)} %multiply_cosine_fusion, f32[12]{0:T(128)S(1)} %add_multiply_fusion.1), kind=kOutput, calls=%fused_computation.3 | convolution fusion | flops 157293696 | bytes 9962544 | tf_op jit(solution)/shard_map/sbl,st->tbl/dot_general | solution.py:80
  52.4 3.0 %collective-permute-done.7 = f32[4,68,36]{1,2,0:T(8,128)S(1)} collective-permute-done((f32[4,68,36]{1,2,0:T(8,128)S(1)}, f32[4,68,36]{1,2,0:T(8,128)S(1)}, u32[]{:S(2)}, u32[]{:S(2)}) %collective-permute-start.7) | collective-permute-done | bytes 39200 | tf_op jit(solution)/shard_map/ppermute | solution.py:35
  56.2 2.4 %collective-permute-start.9 = (f32[12,4,36]{1,2,0:T(8,128)S(1)}, f32[12,4,36]{1,2,0:T(8,128)S(1)}, u32[]{:S(2)}, u32[]{:S(2)}) collective-permute-start(f32[12,4,36]{1,2,0:T(8,128)S(1)} %get-tuple-element.49), channel_id=1, source_target_pairs={{0,12},{4,8},{8,4},{12,0},{1,13},{5,9},{9,5},{13,1},{2,14},{6,10},... | collective-permute-start | bytes 20744 | tf_op jit(solution)/shard_map/ppermute | solution.py:35
  58.7 5.2 %collective-permute-done.8 = f32[12,4,36]{1,2,0:T(8,128)S(1)} collective-permute-done((f32[12,4,36]{1,2,0:T(8,128)S(1)}, f32[12,4,36]{1,2,0:T(8,128)S(1)}, u32[]{:S(2)}, u32[]{:S(2)}) %collective-permute-start.8) | collective-permute-done | bytes 6944 | tf_op jit(solution)/shard_map/ppermute | solution.py:34
  65.7 2.1 %collective-permute-start.11 = (f32[12,68,4]{1,2,0:T(4,128)S(1)}, f32[12,68,4]{1,2,0:T(4,128)S(1)}, u32[]{:S(2)}, u32[]{:S(2)}) collective-permute-start(f32[12,68,4]{1,2,0:T(4,128)S(1)} %bitcast.145), channel_id=1, source_target_pairs={{0,112},{16,32},{32,16},{48,64},{64,48},{80,96},{96,80},{112,0},{1... | collective-permute-start | bytes 39176 | tf_op jit(solution)/shard_map/ppermute | solution.py:35
  68.5 4.7 %collective-permute-done.11 = f32[12,68,4]{1,2,0:T(4,128)S(1)} collective-permute-done((f32[12,68,4]{1,2,0:T(4,128)S(1)}, f32[12,68,4]{1,2,0:T(4,128)S(1)}, u32[]{:S(2)}, u32[]{:S(2)}) %collective-permute-start.11) | collective-permute-done | bytes 13088 | tf_op jit(solution)/shard_map/ppermute | solution.py:35
  76.6 4.2 %fusion.12 = f32[32,256,128]{2,0,1:T(8,128)S(1)} fusion(f32[256,12,128]{2,0,1:T(8,128)S(1)} %fusion.94, f32[12]{0:T(128)S(1)} %add_multiply_fusion.1), kind=kOutput, calls=%fused_computation.14 | convolution fusion | flops 151002240 | bytes 5767216 | tf_op jit(solution)/shard_map/tbl,st->sbl/dot_general | solution.py:75
  80.9 2.8 %fusion.6 = f32[12,256,128]{2,0,1:T(8,128)S(1)} fusion(f32[32,256,128]{2,0,1:T(8,128)S(1)} %fusion.12, f32[32,256,128]{2,0,1:T(8,128)S(1)} %copy_add_fusion, f32[256]{0:T(256)S(1)} %multiply_cosine_fusion, f32[12]{0:T(128)S(1)} %add_multiply_fusion.1), kind=kOutput, calls=%fused_computation.7 | convolution fusion | flops 154147968 | bytes 9962544 | tf_op jit(solution)/shard_map/sbl,st->tbl/dot_general | solution.py:80
  86.2 2.0 %multiply_reduce_fusion.1 = (f32[]{:T(128)}, f32[12,68,36]{1,2,0:T(8,128)S(1)}) fusion(f32[12,68,36]{1,2,0:T(8,128)S(1)} %get-tuple-element.11, f32[8,64,36]{1,2,0:T(8,128)S(1)} %slice_add_fusion.7, f32[8,68,32]{1,2,0:T(8,128)S(1)} %slice_add_fusion.13, f32[12,64,32]{1,2,0:T(8,128)S(1)} %fusion.51, f32[12,68,128]{2,1,0:T(8,128)S(1)} %fusion.34, ...), kind=kOutput, calls=%fused_computation.76 | convolution fusion | flops 45385344 | bytes 894612 | tf_op jit(solution)/shard_map/tal,le->tae/dot_general | solution.py:82
  95.2 3.4 %collective-permute-start.16 = (f32[2]{0:T(128)S(1)}, f32[2]{0:T(128)S(1)}, u32[]{:S(2)}, u32[]{:S(2)}) collective-permute-start(f32[2]{0:T(128)S(1)} %add_add_fusion.5), channel_id=1, source_target_pairs={{0,8},{4,12},{8,0},{12,4},{1,9},{5,13},{9,1},{13,5},{2,10},{6,14},... | collective-permute-start | bytes 32 | tf_op jit(solution)/shard_map/ppermute | solution.py:106
  100.2 3.1 %collective-permute-done.17 = f32[2]{0:T(128)S(1)} collective-permute-done((f32[2]{0:T(128)S(1)}, f32[2]{0:T(128)S(1)}, u32[]{:S(2)}, u32[]{:S(2)}) %collective-permute-start.17) | collective-permute-done | bytes 40 | tf_op jit(solution)/shard_map/ppermute | solution.py:106
  103.4 2.2 %collective-permute-start.19 = (f32[2]{0:T(128)S(1)}, f32[2]{0:T(128)S(1)}, u32[]{:S(2)}, u32[]{:S(2)}) collective-permute-start(f32[2]{0:T(128)S(1)} %add_add_fusion.4), channel_id=1, source_target_pairs={{0,64},{16,80},{32,96},{48,112},{64,0},{80,16},{96,32},{112,48},{1... | collective-permute-start | bytes 32 | tf_op jit(solution)/shard_map/ppermute | solution.py:106
  105.6 2.5 %collective-permute-start.20 = (f32[2]{0:T(128)S(1)}, f32[2]{0:T(128)S(1)}, u32[]{:S(2)}, u32[]{:S(2)}) collective-permute-start(f32[2]{0:T(128)S(1)} %add_add_fusion.4), channel_id=1, source_target_pairs={{0,96},{16,112},{32,64},{48,80},{64,32},{80,48},{96,0},{112,16},{1... | collective-permute-start | bytes 32 | tf_op jit(solution)/shard_map/ppermute | solution.py:106
  110.4 4.1 %collective-permute-start.21 = (f32[2]{0:T(128)S(1)}, f32[2]{0:T(128)S(1)}, u32[]{:S(2)}, u32[]{:S(2)}) collective-permute-start(f32[2]{0:T(128)S(1)} %add_add_fusion.3), channel_id=1, source_target_pairs={{0,16},{16,0},{32,48},{48,32},{64,80},{80,64},{96,112},{112,96},{1... | collective-permute-start | bytes 32 | tf_op jit(solution)/shard_map/ppermute | solution.py:106
  116.4 4.1 %collective-permute-start.27 = (f32[12,68,4]{1,2,0:T(4,128)S(1)}, f32[12,68,4]{1,2,0:T(4,128)S(1)}, u32[]{:S(2)}, u32[]{:S(2)}) collective-permute-start(f32[12,68,4]{1,2,0:T(4,128)S(1)} %bitcast.142), channel_id=1, source_target_pairs={{0,112},{16,32},{32,16},{48,64},{64,48},{80,96},{96,80},{112,0},{1... | collective-permute-start | bytes 39176 | tf_op jit(solution)/shard_map/ppermute | solution.py:35
  129.0 4.2 %fusion.10 = f32[32,256,128]{2,0,1:T(8,128)S(1)} fusion(f32[256,12,128]{2,0,1:T(8,128)S(1)} %fusion.91, f32[12]{0:T(128)S(1)} %add_multiply_fusion.1), kind=kOutput, calls=%fused_computation.12 | convolution fusion | flops 151002240 | bytes 5767216 | tf_op jit(solution)/shard_map/tbl,st->sbl/dot_general | solution.py:75
  133.2 2.8 %fusion.4 = f32[12,256,128]{2,0,1:T(8,128)S(1)} fusion(f32[32,256,128]{2,0,1:T(8,128)S(1)} %fusion.10, f32[32,256,128]{2,0,1:T(8,128)S(1)} %copy-done.1, f32[256]{0:T(256)S(1)} %multiply_cosine_fusion, f32[12]{0:T(128)S(1)} %add_multiply_fusion.1), kind=kOutput, calls=%fused_computation.5 | convolution fusion | flops 154147968 | bytes 9962544 | tf_op jit(solution)/shard_map/sbl,st->tbl/dot_general | solution.py:80
  138.6 2.1 %multiply_reduce_fusion = (f32[]{:T(128)}, f32[12,68,36]{1,2,0:T(8,128)S(1)}) fusion(f32[12,68,36]{1,2,0:T(8,128)S(1)} %get-tuple-element.5, f32[8,64,36]{1,2,0:T(8,128)S(1)} %slice_add_fusion.6, f32[8,68,32]{1,2,0:T(8,128)S(1)} %slice_add_fusion.12, f32[12,64,32]{1,2,0:T(8,128)S(1)} %fusion.54, f32[12,68,128]{2,1,0:T(8,128)S(1)} %fusion.37, ...), kind=kOutput, calls=%fused_computation.72 | convolution fusion | flops 45385344 | bytes 894612 | tf_op jit(solution)/shard_map/tal,le->tae/dot_general | solution.py:82
  149.7 2.1 %collective-permute-start.33 = (f32[2]{0:T(128)S(1)}, f32[2]{0:T(128)S(1)}, u32[]{:S(2)}, u32[]{:S(2)}) collective-permute-start(f32[2]{0:T(128)S(1)} %add_add_fusion.2), channel_id=1, source_target_pairs={{0,12},{4,8},{8,4},{12,0},{1,13},{5,9},{9,5},{13,1},{2,14},{6,10},... | collective-permute-start | bytes 32 | tf_op jit(solution)/shard_map/ppermute | solution.py:106
  155.6 3.6 %collective-permute-start.36 = (f32[2]{0:T(128)S(1)}, f32[2]{0:T(128)S(1)}, u32[]{:S(2)}, u32[]{:S(2)}) collective-permute-start(f32[2]{0:T(128)S(1)} %add_add_fusion.1), channel_id=1, source_target_pairs={{0,96},{16,112},{32,64},{48,80},{64,32},{80,48},{96,0},{112,16},{1... | collective-permute-start | bytes 32 | tf_op jit(solution)/shard_map/ppermute | solution.py:106
  160.7 3.3 %collective-permute-start.37 = (f32[2]{0:T(128)S(1)}, f32[2]{0:T(128)S(1)}, u32[]{:S(2)}, u32[]{:S(2)}) collective-permute-start(f32[2]{0:T(128)S(1)} %add_add_fusion), channel_id=1, source_target_pairs={{0,16},{16,0},{32,48},{48,32},{64,80},{80,64},{96,112},{112,96},{1... | collective-permute-start | bytes 32 | tf_op jit(solution)/shard_map/ppermute | solution.py:106
  166.1 2.2 %collective-permute-start.41 = (f32[12,4,36]{1,2,0:T(8,128)S(1)}, f32[12,4,36]{1,2,0:T(8,128)S(1)}, u32[]{:S(2)}, u32[]{:S(2)}) collective-permute-start(f32[12,4,36]{1,2,0:T(8,128)S(1)} %get-tuple-element.39), channel_id=1, source_target_pairs={{0,12},{4,8},{8,4},{12,0},{1,13},{5,9},{9,5},{13,1},{2,14},{6,10},... | collective-permute-start | bytes 20744 | tf_op jit(solution)/shard_map/ppermute | solution.py:35
  173.9 3.4 %collective-permute-start.43 = (f32[12,68,4]{1,2,0:T(4,128)S(1)}, f32[12,68,4]{1,2,0:T(4,128)S(1)}, u32[]{:S(2)}, u32[]{:S(2)}) collective-permute-start(f32[12,68,4]{1,2,0:T(4,128)S(1)} %bitcast.144), channel_id=1, source_target_pairs={{0,112},{16,32},{32,16},{48,64},{64,48},{80,96},{96,80},{112,0},{1... | collective-permute-start | bytes 39176 | tf_op jit(solution)/shard_map/ppermute | solution.py:35
  178.7 2.7 %collective-permute-done.43 = f32[12,68,4]{1,2,0:T(4,128)S(1)} collective-permute-done((f32[12,68,4]{1,2,0:T(4,128)S(1)}, f32[12,68,4]{1,2,0:T(4,128)S(1)}, u32[]{:S(2)}, u32[]{:S(2)}) %collective-permute-start.43) | collective-permute-done | bytes 13088 | tf_op jit(solution)/shard_map/ppermute | solution.py:35
  (168 shorter events, 66.8 us)
Async XLA Ops:
  7.0 11.6 %collective-permute-start.2 = (f32[2,12,2,32]{2,3,1,0:T(8,128)S(1)}, f32[2,12,2,32]{2,3,1,0:T(8,128)S(1)}, u32[]{:S(2)}, u32[]{:S(2)}) collective-permute-start(f32[2,12,2,32]{2,3,1,0:T(8,128)S(1)} %get-tuple-element.36), channel_id=1, source_target_pairs={{0,4},{4,0},{8,12},{12,8},{1,5},{5,1},{9,13},{13,9},{2,6},{6,2},{1... | collective-permute-start | bytes 18440 | tf_op jit(solution)/shard_map/ppermute | solution.py:34
  9.2 12.1 %collective-permute-start.3 = (f32[2,12,2,32]{2,3,1,0:T(8,128)S(1)}, f32[2,12,2,32]{2,3,1,0:T(8,128)S(1)}, u32[]{:S(2)}, u32[]{:S(2)}) collective-permute-start(f32[2,12,2,32]{2,3,1,0:T(8,128)S(1)} %get-tuple-element.37), channel_id=1, source_target_pairs={{0,12},{4,8},{8,4},{12,0},{1,13},{5,9},{9,5},{13,1},{2,14},{6,10},... | collective-permute-start | bytes 18440 | tf_op jit(solution)/shard_map/ppermute | solution.py:35
  21.6 7.5 %collective-permute-start.5 = (f32[2,12,68,2]{2,3,1,0:T(2,128)S(1)}, f32[2,12,68,2]{2,3,1,0:T(2,128)S(1)}, u32[]{:S(2)}, u32[]{:S(2)}) collective-permute-start(f32[2,12,68,2]{2,3,1,0:T(2,128)S(1)} %bitcast.143), channel_id=1, source_target_pairs={{0,112},{16,32},{32,16},{48,64},{64,48},{80,96},{96,80},{112,0},{1... | collective-permute-start | bytes 39176 | tf_op jit(solution)/shard_map/ppermute | solution.py:35
  27.2 5.5 %collective-permute-start.4 = (f32[2,12,68,2]{2,3,1,0:T(2,128)S(1)}, f32[2,12,68,2]{2,3,1,0:T(2,128)S(1)}, u32[]{:S(2)}, u32[]{:S(2)}) collective-permute-start(f32[2,12,68,2]{2,3,1,0:T(2,128)S(1)} %get-tuple-element.16), channel_id=1, source_target_pairs={{0,16},{16,0},{32,48},{48,32},{64,80},{80,64},{96,112},{112,96},{1... | collective-permute-start | bytes 39176 | tf_op jit(solution)/shard_map/ppermute | solution.py:34
  55.5 8.4 %collective-permute-start.8 = (f32[12,4,36]{1,2,0:T(8,128)S(1)}, f32[12,4,36]{1,2,0:T(8,128)S(1)}, u32[]{:S(2)}, u32[]{:S(2)}) collective-permute-start(f32[12,4,36]{1,2,0:T(8,128)S(1)} %get-tuple-element.48), channel_id=1, source_target_pairs={{0,4},{4,0},{8,12},{12,8},{1,5},{5,1},{9,13},{13,9},{2,6},{6,2},{1... | collective-permute-start | bytes 20744 | tf_op jit(solution)/shard_map/ppermute | solution.py:34
  56.2 9.2 %collective-permute-start.9 = (f32[12,4,36]{1,2,0:T(8,128)S(1)}, f32[12,4,36]{1,2,0:T(8,128)S(1)}, u32[]{:S(2)}, u32[]{:S(2)}) collective-permute-start(f32[12,4,36]{1,2,0:T(8,128)S(1)} %get-tuple-element.49), channel_id=1, source_target_pairs={{0,12},{4,8},{8,4},{12,0},{1,13},{5,9},{9,5},{13,1},{2,14},{6,10},... | collective-permute-start | bytes 20744 | tf_op jit(solution)/shard_map/ppermute | solution.py:35
  65.7 7.5 %collective-permute-start.11 = (f32[12,68,4]{1,2,0:T(4,128)S(1)}, f32[12,68,4]{1,2,0:T(4,128)S(1)}, u32[]{:S(2)}, u32[]{:S(2)}) collective-permute-start(f32[12,68,4]{1,2,0:T(4,128)S(1)} %bitcast.145), channel_id=1, source_target_pairs={{0,112},{16,32},{32,16},{48,64},{64,48},{80,96},{96,80},{112,0},{1... | collective-permute-start | bytes 39176 | tf_op jit(solution)/shard_map/ppermute | solution.py:35
  67.7 5.8 %collective-permute-start.10 = (f32[12,68,4]{1,2,0:T(4,128)S(1)}, f32[12,68,4]{1,2,0:T(4,128)S(1)}, u32[]{:S(2)}, u32[]{:S(2)}) collective-permute-start(f32[12,68,4]{1,2,0:T(4,128)S(1)} %get-tuple-element.13), channel_id=1, source_target_pairs={{0,16},{16,0},{32,48},{48,32},{64,80},{80,64},{96,112},{112,96},{1... | collective-permute-start | bytes 39176 | tf_op jit(solution)/shard_map/ppermute | solution.py:34
  91.5 16.6 %collective-permute-start.22 = (f32[4,68,36]{1,2,0:T(8,128)S(1)}, f32[4,68,36]{1,2,0:T(8,128)S(1)}, u32[]{:S(2)}, u32[]{:S(2)}) collective-permute-start(f32[4,68,36]{1,2,0:T(8,128)S(1)} %get-tuple-element.46), channel_id=1, source_target_pairs={{0,1},{1,0},{2,3},{3,2},{4,5},{5,4},{6,7},{7,6},{8,9},{9,8},{10,11... | collective-permute-start | bytes 117512 | tf_op jit(solution)/shard_map/ppermute | solution.py:34
  91.9 16.1 %collective-permute-start.23 = (f32[4,68,36]{1,2,0:T(8,128)S(1)}, f32[4,68,36]{1,2,0:T(8,128)S(1)}, u32[]{:S(2)}, u32[]{:S(2)}) collective-permute-start(f32[4,68,36]{1,2,0:T(8,128)S(1)} %get-tuple-element.47), channel_id=1, source_target_pairs={{0,3},{1,2},{2,1},{3,0},{4,7},{5,6},{6,5},{7,4},{8,11},{9,10},{10,... | collective-permute-start | bytes 117512 | tf_op jit(solution)/shard_map/ppermute | solution.py:35
  94.8 4.7 %collective-permute-start.15 = (f32[2]{0:T(128)S(1)}, f32[2]{0:T(128)S(1)}, u32[]{:S(2)}, u32[]{:S(2)}) collective-permute-start(f32[2]{0:T(128)S(1)} %add_add_fusion.5), channel_id=1, source_target_pairs={{0,4},{4,0},{8,12},{12,8},{1,5},{5,1},{9,13},{13,9},{2,6},{6,2},{1... | collective-permute-start | bytes 32 | tf_op jit(solution)/shard_map/ppermute | solution.py:106
  95.2 5.1 %collective-permute-start.16 = (f32[2]{0:T(128)S(1)}, f32[2]{0:T(128)S(1)}, u32[]{:S(2)}, u32[]{:S(2)}) collective-permute-start(f32[2]{0:T(128)S(1)} %add_add_fusion.5), channel_id=1, source_target_pairs={{0,8},{4,12},{8,0},{12,4},{1,9},{5,13},{9,1},{13,5},{2,10},{6,14},... | collective-permute-start | bytes 32 | tf_op jit(solution)/shard_map/ppermute | solution.py:106
  98.6 4.8 %collective-permute-start.17 = (f32[2]{0:T(128)S(1)}, f32[2]{0:T(128)S(1)}, u32[]{:S(2)}, u32[]{:S(2)}) collective-permute-start(f32[2]{0:T(128)S(1)} %add_add_fusion.5), channel_id=1, source_target_pairs={{0,12},{4,8},{8,4},{12,0},{1,13},{5,9},{9,5},{13,1},{2,14},{6,10},... | collective-permute-start | bytes 32 | tf_op jit(solution)/shard_map/ppermute | solution.py:106
  103.4 6.0 %collective-permute-start.18 = (f32[2]{0:T(128)S(1)}, f32[2]{0:T(128)S(1)}, u32[]{:S(2)}, u32[]{:S(2)}) collective-permute-start(f32[2]{0:T(128)S(1)} %add_add_fusion.4), channel_id=1, source_target_pairs={{0,32},{16,48},{32,0},{48,16},{64,96},{80,112},{96,64},{112,80},{1... | collective-permute-start | bytes 32 | tf_op jit(solution)/shard_map/ppermute | solution.py:106
  103.4 6.0 %collective-permute-start.19 = (f32[2]{0:T(128)S(1)}, f32[2]{0:T(128)S(1)}, u32[]{:S(2)}, u32[]{:S(2)}) collective-permute-start(f32[2]{0:T(128)S(1)} %add_add_fusion.4), channel_id=1, source_target_pairs={{0,64},{16,80},{32,96},{48,112},{64,0},{80,16},{96,32},{112,48},{1... | collective-permute-start | bytes 32 | tf_op jit(solution)/shard_map/ppermute | solution.py:106
  105.6 4.8 %collective-permute-start.20 = (f32[2]{0:T(128)S(1)}, f32[2]{0:T(128)S(1)}, u32[]{:S(2)}, u32[]{:S(2)}) collective-permute-start(f32[2]{0:T(128)S(1)} %add_add_fusion.4), channel_id=1, source_target_pairs={{0,96},{16,112},{32,64},{48,80},{64,32},{80,48},{96,0},{112,16},{1... | collective-permute-start | bytes 32 | tf_op jit(solution)/shard_map/ppermute | solution.py:106
  108.3 7.9 %collective-permute-start.24 = (f32[12,4,36]{1,2,0:T(8,128)S(1)}, f32[12,4,36]{1,2,0:T(8,128)S(1)}, u32[]{:S(2)}, u32[]{:S(2)}) collective-permute-start(f32[12,4,36]{1,2,0:T(8,128)S(1)} %get-tuple-element.43), channel_id=1, source_target_pairs={{0,4},{4,0},{8,12},{12,8},{1,5},{5,1},{9,13},{13,9},{2,6},{6,2},{1... | collective-permute-start | bytes 20744 | tf_op jit(solution)/shard_map/ppermute | solution.py:34
  108.3 7.8 %collective-permute-start.25 = (f32[12,4,36]{1,2,0:T(8,128)S(1)}, f32[12,4,36]{1,2,0:T(8,128)S(1)}, u32[]{:S(2)}, u32[]{:S(2)}) collective-permute-start(f32[12,4,36]{1,2,0:T(8,128)S(1)} %get-tuple-element.44), channel_id=1, source_target_pairs={{0,12},{4,8},{8,4},{12,0},{1,13},{5,9},{9,5},{13,1},{2,14},{6,10},... | collective-permute-start | bytes 20744 | tf_op jit(solution)/shard_map/ppermute | solution.py:35
  110.4 5.7 %collective-permute-start.21 = (f32[2]{0:T(128)S(1)}, f32[2]{0:T(128)S(1)}, u32[]{:S(2)}, u32[]{:S(2)}) collective-permute-start(f32[2]{0:T(128)S(1)} %add_add_fusion.3), channel_id=1, source_target_pairs={{0,16},{16,0},{32,48},{48,32},{64,80},{80,64},{96,112},{112,96},{1... | collective-permute-start | bytes 32 | tf_op jit(solution)/shard_map/ppermute | solution.py:106
  116.4 7.5 %collective-permute-start.27 = (f32[12,68,4]{1,2,0:T(4,128)S(1)}, f32[12,68,4]{1,2,0:T(4,128)S(1)}, u32[]{:S(2)}, u32[]{:S(2)}) collective-permute-start(f32[12,68,4]{1,2,0:T(4,128)S(1)} %bitcast.142), channel_id=1, source_target_pairs={{0,112},{16,32},{32,16},{48,64},{64,48},{80,96},{96,80},{112,0},{1... | collective-permute-start | bytes 39176 | tf_op jit(solution)/shard_map/ppermute | solution.py:35
  120.5 5.3 %collective-permute-start.26 = (f32[12,68,4]{1,2,0:T(4,128)S(1)}, f32[12,68,4]{1,2,0:T(4,128)S(1)}, u32[]{:S(2)}, u32[]{:S(2)}) collective-permute-start(f32[12,68,4]{1,2,0:T(4,128)S(1)} %get-tuple-element.8), channel_id=1, source_target_pairs={{0,16},{16,0},{32,48},{48,32},{64,80},{80,64},{96,112},{112,96},{1... | collective-permute-start | bytes 39176 | tf_op jit(solution)/shard_map/ppermute | solution.py:34
  143.9 21.9 %collective-permute-start.38 = (f32[4,68,36]{1,2,0:T(8,128)S(1)}, f32[4,68,36]{1,2,0:T(8,128)S(1)}, u32[]{:S(2)}, u32[]{:S(2)}) collective-permute-start(f32[4,68,36]{1,2,0:T(8,128)S(1)} %get-tuple-element.41), channel_id=1, source_target_pairs={{0,1},{1,0},{2,3},{3,2},{4,5},{5,4},{6,7},{7,6},{8,9},{9,8},{10,11... | collective-permute-start | bytes 117512 | tf_op jit(solution)/shard_map/ppermute | solution.py:34
  144.4 21.4 %collective-permute-start.39 = (f32[4,68,36]{1,2,0:T(8,128)S(1)}, f32[4,68,36]{1,2,0:T(8,128)S(1)}, u32[]{:S(2)}, u32[]{:S(2)}) collective-permute-start(f32[4,68,36]{1,2,0:T(8,128)S(1)} %get-tuple-element.42), channel_id=1, source_target_pairs={{0,3},{1,2},{2,1},{3,0},{4,7},{5,6},{6,5},{7,4},{8,11},{9,10},{10,... | collective-permute-start | bytes 117512 | tf_op jit(solution)/shard_map/ppermute | solution.py:35
  147.8 5.1 %collective-permute-start.32 = (f32[2]{0:T(128)S(1)}, f32[2]{0:T(128)S(1)}, u32[]{:S(2)}, u32[]{:S(2)}) collective-permute-start(f32[2]{0:T(128)S(1)} %add_add_fusion.2), channel_id=1, source_target_pairs={{0,8},{4,12},{8,0},{12,4},{1,9},{5,13},{9,1},{13,5},{2,10},{6,14},... | collective-permute-start | bytes 32 | tf_op jit(solution)/shard_map/ppermute | solution.py:106
  149.7 4.8 %collective-permute-start.33 = (f32[2]{0:T(128)S(1)}, f32[2]{0:T(128)S(1)}, u32[]{:S(2)}, u32[]{:S(2)}) collective-permute-start(f32[2]{0:T(128)S(1)} %add_add_fusion.2), channel_id=1, source_target_pairs={{0,12},{4,8},{8,4},{12,0},{1,13},{5,9},{9,5},{13,1},{2,14},{6,10},... | collective-permute-start | bytes 32 | tf_op jit(solution)/shard_map/ppermute | solution.py:106
  155.2 5.1 %collective-permute-start.35 = (f32[2]{0:T(128)S(1)}, f32[2]{0:T(128)S(1)}, u32[]{:S(2)}, u32[]{:S(2)}) collective-permute-start(f32[2]{0:T(128)S(1)} %add_add_fusion.1), channel_id=1, source_target_pairs={{0,64},{16,80},{32,96},{48,112},{64,0},{80,16},{96,32},{112,48},{1... | collective-permute-start | bytes 32 | tf_op jit(solution)/shard_map/ppermute | solution.py:106
  155.6 5.1 %collective-permute-start.36 = (f32[2]{0:T(128)S(1)}, f32[2]{0:T(128)S(1)}, u32[]{:S(2)}, u32[]{:S(2)}) collective-permute-start(f32[2]{0:T(128)S(1)} %add_add_fusion.1), channel_id=1, source_target_pairs={{0,96},{16,112},{32,64},{48,80},{64,32},{80,48},{96,0},{112,16},{1... | collective-permute-start | bytes 32 | tf_op jit(solution)/shard_map/ppermute | solution.py:106
  160.7 5.1 %collective-permute-start.37 = (f32[2]{0:T(128)S(1)}, f32[2]{0:T(128)S(1)}, u32[]{:S(2)}, u32[]{:S(2)}) collective-permute-start(f32[2]{0:T(128)S(1)} %add_add_fusion), channel_id=1, source_target_pairs={{0,16},{16,0},{32,48},{48,32},{64,80},{80,64},{96,112},{112,96},{1... | collective-permute-start | bytes 32 | tf_op jit(solution)/shard_map/ppermute | solution.py:106
  166.0 7.6 %collective-permute-start.40 = (f32[12,4,36]{1,2,0:T(8,128)S(1)}, f32[12,4,36]{1,2,0:T(8,128)S(1)}, u32[]{:S(2)}, u32[]{:S(2)}) collective-permute-start(f32[12,4,36]{1,2,0:T(8,128)S(1)} %get-tuple-element.38), channel_id=1, source_target_pairs={{0,4},{4,0},{8,12},{12,8},{1,5},{5,1},{9,13},{13,9},{2,6},{6,2},{1... | collective-permute-start | bytes 20744 | tf_op jit(solution)/shard_map/ppermute | solution.py:34
  166.1 7.5 %collective-permute-start.41 = (f32[12,4,36]{1,2,0:T(8,128)S(1)}, f32[12,4,36]{1,2,0:T(8,128)S(1)}, u32[]{:S(2)}, u32[]{:S(2)}) collective-permute-start(f32[12,4,36]{1,2,0:T(8,128)S(1)} %get-tuple-element.39), channel_id=1, source_target_pairs={{0,12},{4,8},{8,4},{12,0},{1,13},{5,9},{9,5},{13,1},{2,14},{6,10},... | collective-permute-start | bytes 20744 | tf_op jit(solution)/shard_map/ppermute | solution.py:35
  173.9 7.5 %collective-permute-start.43 = (f32[12,68,4]{1,2,0:T(4,128)S(1)}, f32[12,68,4]{1,2,0:T(4,128)S(1)}, u32[]{:S(2)}, u32[]{:S(2)}) collective-permute-start(f32[12,68,4]{1,2,0:T(4,128)S(1)} %bitcast.144), channel_id=1, source_target_pairs={{0,112},{16,32},{32,16},{48,64},{64,48},{80,96},{96,80},{112,0},{1... | collective-permute-start | bytes 39176 | tf_op jit(solution)/shard_map/ppermute | solution.py:35
  177.3 5.3 %collective-permute-start.42 = (f32[12,68,4]{1,2,0:T(4,128)S(1)}, f32[12,68,4]{1,2,0:T(4,128)S(1)}, u32[]{:S(2)}, u32[]{:S(2)}) collective-permute-start(f32[12,68,4]{1,2,0:T(4,128)S(1)} %get-tuple-element.2), channel_id=1, source_target_pairs={{0,16},{16,0},{32,48},{48,32},{64,80},{80,64},{96,112},{112,96},{1... | collective-permute-start | bytes 39176 | tf_op jit(solution)/shard_map/ppermute | solution.py:34
  (18 other events, 157.5 us)
where the time goes:
time: 186 us; the launch traced here: 184 us
  starting transfers between devices  61.7 us (33%)
  waiting for transfers between devices  54.4 us (29%)
  matrix products  43.1 us (23%)
  other arithmetic  15.5 us (8%)
  between operations  7.49 us (4%)
    ppermute x20, starting transfers between devices, all_sum(): lax.ppermute(values, axis, [(i, i ^ d) for i in range(count)])  30 us
    ppermute x12, starting transfers between devices, swap_sides(): got_second = lax.ppermute(jnp.where(odd, to_right, to_left), axis, second)  25.5 us
    ppermute x12, waiting for transfers between devices, swap_sides(): got_second = lax.ppermute(jnp.where(odd, to_right, to_left), axis, second)  20.1 us
    ppermute x12, waiting for transfers between devices, swap_sides(): got_first = lax.ppermute(jnp.where(odd, to_left, to_right), axis, first)  19.5 us
    dot_general x3, matrix products, evaluate(): return jnp.einsum('tbl,st->sbl', partial_value, time_tab, precision=highest)  14.9 us
    ppermute x20, waiting for transfers between devices, all_sum(): lax.ppermute(values, axis, [(i, i ^ d) for i in range(count)])  14.8 us
    dot_general x3, matrix products, adjoint(): jnp.einsum('sbl,st->tbl', cell_values, time_tab, precision=highest)  11.1 us
    ppermute x12, starting transfers between devices, swap_sides(): got_first = lax.ppermute(jnp.where(odd, to_left, to_right), axis, first)  6.18 us
  transfers between devices with their start and end apart: 44, of which 27 were waited for; matrix products, arithmetic and copies ran while one was open for 3% of the time, Pallas kernels for 0%

commit v1 on v0

v1 whole, which is shorter than its diff:
```python
import functools

import jax
import jax.numpy as jnp
import numpy as np
from jax import lax
from jax.experimental import pallas as pl
from jax.experimental.pallas import tpu as pltpu
from jax.sharding import PartitionSpec as P

SPLIT = ("tm", "lat", "lon")
tweedie_power = 1.6
smooth = 0.5

ROWS, LANES, SEG, LAT_OWN, LON_OWN, T_OWN = 80, 512, 40, 64, 32, 8
HOURS, LAT_CELLS, LON_CELLS, BLOCK = 32, 256, 128, 128
STEPS = LAT_CELLS // BLOCK


def spline(offsets):
    distance = np.abs(offsets)
    near_part = (4.0 - 6.0 * distance**2 + 3.0 * distance**3) / 6.0
    far_part = np.maximum(2.0 - distance, 0.0) ** 3 / 6.0
    return np.where(distance < 1.0, near_part, far_part)


def table(cell_count, knot_count):
    cell_pos = np.arange(cell_count, dtype=np.float64)[:, None]
    knot_pos = np.arange(knot_count + 4, dtype=np.float64)[None, :] - 2.0
    return spline((cell_pos - 4.0 * knot_pos - 1.5) / 4.0)


def halves(values):
    values = jnp.asarray(values, jnp.float32)
    high = values.astype(jnp.bfloat16)
    return high, (values - high.astype(jnp.float32)).astype(jnp.bfloat16)


def tables():
    lat = np.zeros((LAT_CELLS, ROWS))
    lat[:, : LAT_OWN + 4] = table(LAT_CELLS, LAT_OWN)
    high, low = halves(lat)
    lat_up = jnp.concatenate([high, low, high], axis=1)
    high, low = (part.T.reshape(ROWS, STEPS, BLOCK).transpose(1, 0, 2) for part in (high, low))
    lat_down = jnp.concatenate([high, low, high], axis=2)
    lon = np.zeros((128, 3 * LON_CELLS))
    for r in range(3):
        lon[r * SEG : r * SEG + LON_OWN + 4, r * LON_CELLS : (r + 1) * LON_CELLS] = table(LON_CELLS, LON_OWN).T
    high, low = halves(lon)
    lon_up = jnp.concatenate([high, high, low], axis=0)
    lon_down = jnp.concatenate([high.T, low.T], axis=1)
    return lat_up, lat_down, lon_up, lon_down


def hour_factors():
    near, far = ([float(spline(np.float64(x))) for x in xs] for xs in ((0.125, 0.875, 0.375, 0.625), (1.125, 1.875, 1.375, 1.625)))
    outer = ((far[0] + far[1]) / 2, (far[0] - far[1]) / 2, (far[2] + far[3]) / 2, (far[2] - far[3]) / 2)
    inner = ((near[0] + near[1]) / 2, (near[0] - near[1]) / 2, (near[2] + near[3]) / 2, (near[2] - near[3]) / 2)
    return outer, inner


class Place:
    def __init__(self):
        index = {axis: lax.axis_index(axis) for axis in SPLIT}
        self.odd = {axis: index[axis] % 2 == 1 for axis in SPLIT}
        self.left = {axis: jnp.where(index[axis] > 0, 1.0, 0.0) for axis in SPLIT}
        self.right = {axis: jnp.where(index[axis] < lax.axis_size(axis) - 1, 1.0, 0.0) for axis in SPLIT}

    def messages(self, axis, to_left, to_right):
        return jnp.where(self.odd[axis], to_left, to_right), jnp.where(self.odd[axis], to_right, to_left)

    def received(self, axis, first, second):
        left, right = jnp.where(self.odd[axis], first, second), jnp.where(self.odd[axis], second, first)
        return (left, right) if axis == "lon" else (left * self.left[axis], right * self.right[axis])


def split(values):
    high = values.astype(jnp.bfloat16)
    return high, (values - high.astype(jnp.float32)).astype(jnp.bfloat16)


def dot(left, right):
    return jnp.dot(left, right, preferred_element_type=jnp.float32)


def lane_places():
    lane = lax.broadcasted_iota(jnp.int32, (ROWS, 128), 1)
    r = (lane >= SEG).astype(jnp.int32) + (lane >= 2 * SEG).astype(jnp.int32)
    return r, lane - SEG * r, lax.broadcasted_iota(jnp.int32, (ROWS, 128), 0)


def within(place, count):
    return (place >= 2) & (place < count + 2)


def group(values, g):
    return values[:, g * 128 : (g + 1) * 128]


def penalty(values, place):
    r, lon, row = lane_places()
    own_row, own_lon = within(row, LAT_OWN), within(lon, LON_OWN)
    row_share = jnp.where(
        own_row, 1.0, jnp.where(row == 1, 1.0 - place.left["lat"], jnp.where(row == LAT_OWN + 2, 1.0 - place.right["lat"], 0.0))
    )
    parts = [group(values, g) for g in range(4)]

    def along_t(v):
        before = [pltpu.roll(v[3], SEG, 1), v[0], v[1], v[2]]
        after = [v[1], v[2], v[3], pltpu.roll(v[0], 128 - SEG, 1)]
        return [b - 2.0 * m + a for b, m, a in zip(before, v, after)]

    t_second = along_t(parts)
    t_shared = []
    summed = []
    for g in range(4):
        t = 4 * r + g
        own_t = within(t, T_OWN)
        share = jnp.where(own_t, 1.0, jnp.where(t == 1, 1.0 - place.left["tm"], jnp.where(t == T_OWN + 2, 1.0 - place.right["tm"], 0.0)))
        t_shared.append(jnp.where(own_row & own_lon, share, 0.0) * t_second[g])
        v = parts[g]
        second = pltpu.roll(v, 1, 0) - 2.0 * v + pltpu.roll(v, ROWS - 1, 0)
        second = jnp.where(own_t & own_lon, row_share, 0.0) * second
        total = pltpu.roll(second, 1, 0) - 2.0 * second + pltpu.roll(second, ROWS - 1, 0)
        second = pltpu.roll(v, 1, 1) - 2.0 * v + pltpu.roll(v, 127, 1)
        second = jnp.where(own_t & own_lon & own_row, second, 0.0)
        summed.append(total + pltpu.roll(second, 1, 1) - 2.0 * second + pltpu.roll(second, 127, 1))
    return [smooth * (a + b) for a, b in zip(summed, along_t(t_shared))]


def lane_sum(parts):
    return jnp.sum(parts[0] + parts[1] + parts[2] + parts[3], axis=0, keepdims=True)


def own_lane_sum(values):
    r, lon, row = lane_places()
    inside = within(row, LAT_OWN) & within(lon, LON_OWN)
    return lane_sum([jnp.where(inside & within(4 * r + g, T_OWN), group(values, g), 0.0) for g in range(4)])


def merge_rows(values, got_first, got_second, place):
    keep = lax.broadcasted_iota(jnp.int32, (8, LANES), 0) < 4
    left, right = place.received("lat", got_first, got_second)
    return jnp.concatenate(
        [
            values[0:8] + jnp.where(keep, left, 0.0),
            values[8:64],
            values[64:72] + jnp.where(keep, right, 0.0),
            values[72:80],
        ],
        axis=0,
    )


def cell_block(block, vec_parts, w_of, lat_up, lat_down, lon_up, lon_down, up, down, before_cells):
    outer, inner = hour_factors()
    expanded = dot(lat_up[block * BLOCK : (block + 1) * BLOCK], vec_parts)
    high, low = split(jnp.concatenate([group(expanded, g) for g in range(4)], axis=0))
    up[...] = dot(jnp.concatenate([high, low, high], axis=1), lon_up[...])

    def tile(i, carry):
        start = pl.multiple_of(i * 8, 8)
        rows = pl.ds(pl.multiple_of(block * BLOCK + start, 8), 8)

        def knot(t):
            return up[pl.ds((t % 4) * BLOCK + start, 8), (t // 4) * 128 : (t // 4 + 1) * 128]

        back = [None] * 12

        def add(t, value):
            back[t] = value if back[t] is None else back[t] + value

        x = [knot(0), knot(1), knot(2), None]
        for j in range(9):
            x[3] = knot(j + 3)
            edge_sum, edge_diff, mid_sum, mid_diff = x[0] + x[3], x[0] - x[3], x[1] + x[2], x[1] - x[2]
            sides = []
            for pair, (late, early) in enumerate(((2, 1), (3, 0))):
                even = outer[2 * pair] * edge_sum + inner[2 * pair] * mid_sum
                uneven = outer[2 * pair + 1] * edge_diff + inner[2 * pair + 1] * mid_diff
                below = w_of(4 * (j - 1) + late, rows, even + uneven) if j > 0 else None
                above = w_of(4 * j + early, rows, even - uneven) if j < 8 else None
                if below is None:
                    sides.append((above, -above))
                elif above is None:
                    sides.append((below, below))
                else:
                    sides.append((below + above, below - above))
            (both0, differ0), (both1, differ1) = sides
            edge_even, edge_odd = outer[0] * both0 + outer[2] * both1, outer[1] * differ0 + outer[3] * differ1
            mid_even, mid_odd = inner[0] * both0 + inner[2] * both1, inner[1] * differ0 + inner[3] * differ1
            add(j, edge_even + edge_odd)
            add(j + 1, mid_even + mid_odd)
            add(j + 2, mid_even - mid_odd)
            add(j + 3, edge_even - edge_odd)
            for t in (j,) if j < 8 else (8, 9, 10, 11):
                down[pl.ds((t % 4) * BLOCK + start, 8), (t // 4) * 128 : (t // 4 + 1) * 128] = back[t]
            x = [x[1], x[2], x[3], None]
        return carry

    before_cells(block)
    lax.fori_loop(0, BLOCK // 8, tile, 0)
    high, low = split(down[...])
    both = dot(high, lon_down[...])
    narrow = both[:, :128] + both[:, 128:] + dot(low, lon_down[:, :128])
    narrow = jnp.concatenate([narrow[g * BLOCK : (g + 1) * BLOCK] for g in range(4)], axis=1)
    high, low = split(narrow)
    return dot(lat_down[block], jnp.concatenate([high, high, low], axis=0))


def apply_cells(values, w_of, place, lat_up, lat_down, lon_up, lon_down, up, down, before_cells=lambda block: None):
    high, low = split(values)
    parts = jnp.concatenate([high, high, low], axis=0)
    total = 0.0
    for block in range(STEPS):
        total = total + cell_block(block, parts, w_of, lat_up, lat_down, lon_up, lon_down, up, down, before_cells)
    extra = penalty(values, place)
    sums = [group(total, g) + extra[g] for g in range(4)]
    turned = [jnp.concatenate([part, jnp.zeros((128 - ROWS, 128), jnp.float32)], axis=0).T for part in sums]
    return sums, [[turned[g][r * SEG : (r + 1) * SEG] for g in range(4)] for r in range(3)]


def write_ends(segs, place, tiles, first, second):
    lower = lax.broadcasted_iota(jnp.int32, (8, 128), 0) < 4
    for r in range(3):
        for g in range(4):
            tiles[r, g] = segs[r][g]
        for h in range(2):
            packed = [
                jnp.where(lower, segs[r][2 * h][at : at + 8], pltpu.roll(segs[r][2 * h + 1][at : at + 8], 4, 0))
                for at in (0, 32)
            ]
            first[r, h], second[r, h] = place.messages("lon", *packed)


def start_kernel(both, got_first, got_second, area, offset_far, precip_far, lat_up, lat_down, lon_up, lon_down,
                 weight, diag, tiles, first, second, offset, precip, up, down, arrived):
    place = Place()
    copies = []
    for block in range(STEPS):
        rows = slice(block * BLOCK, (block + 1) * BLOCK)
        for source, target in ((offset_far, offset), (precip_far, precip)):
            at = arrived.at[len(copies)]
            copies.append(pltpu.make_async_copy(source.at[:, rows, :], target.at[:, rows, :], at))
    for copy in copies:
        copy.start()

    row = lax.broadcasted_iota(jnp.int32, (8, LANES), 0)
    left, right = place.received("lat", got_first[...], got_second[...])

    def with_halo(own, left, right):
        head, tail = own[0:8] + jnp.where(row < 2, left, 0.0), own[64:72] + jnp.where((row >= 2) & (row < 4), right, 0.0)
        return jnp.concatenate([head, own[8:64], tail, own[72:80]], axis=0)

    values = with_halo(both[0], left, right)
    diag[...] = with_halo(both[1], pltpu.roll(left, 6, 0), pltpu.roll(right, 6, 0))

    def w_of(hour, rows, value):
        linear = offset[hour, rows, :] + value
        here = area[rows, :]
        w = here * jnp.exp((2.0 - tweedie_power) * linear)
        weight[hour, rows, :] = w
        return w - here * precip[hour, rows, :] * jnp.exp((1.0 - tweedie_power) * linear)

    def before_cells(block):
        for copy in copies[2 * block : 2 * block + 2]:
            copy.wait()

    _, segs = apply_cells(values, w_of, place, lat_up, lat_down, lon_up, lon_down, up, down, before_cells)
    write_ends(segs, place, tiles, first, second)


def hessian_kernel(partial_rows, got_first, got_second, diag, weight, lat_up, lat_down, lon_up, lon_down, *refs, again):
    if again:
        before, residual, scaled, tiles, slots, up, down = refs
    else:
        residual, scaled, tiles, first, second, sums, up, down = refs
    place = Place()
    merged = merge_rows(partial_rows[...], got_first[...], got_second[...], place)
    here = merged if again else -merged
    residual[...] = here
    values = diag[...] * here
    scaled[...] = values

    def w_of(hour, rows, value):
        return weight[hour, rows, :] * value

    image, segs = apply_cells(values, w_of, place, lat_up, lat_down, lon_up, lon_down, up, down)
    lines = [own_lane_sum(here * values), lane_sum([image[g] * group(values, g) for g in range(4)])]
    if again:
        for r in range(3):
            for g in range(4):
                tiles[r, g] = segs[r][g]
        lines = jnp.concatenate([jnp.zeros((4, 128), jnp.float32), before[0:2], *lines], axis=0)
        write_slots(image, segs, lines, slots)
    else:
        write_ends(segs, place, tiles, first, second)
        sums[...] = jnp.concatenate(lines + [jnp.zeros((6, 128), jnp.float32)], axis=0)


def slot_at(lon_step, lat_step):
    lon_count, lat_count = lax.axis_size("lon"), lax.axis_size("lat")
    lon = lax.rem(lax.axis_index("lon") + (lon_count + lon_step), lon_count)
    return lon * lat_count + lax.rem(lax.axis_index("lat") + (lat_count + lat_step), lat_count)


def rolled(values, amount, axis):
    amount %= values.shape[axis]
    return pltpu.roll(values, amount, axis) if amount else values


def row_of(shape=(8, 128)):
    return lax.broadcasted_iota(jnp.int32, shape, 0)


def write_slots(sums, segs, lines, slots):
    row = row_of()
    low = lax.broadcasted_iota(jnp.int32, (8, 128), 1) < LAT_OWN
    for j in range(slots.shape[0]):
        slots[j, 0:8] = jnp.zeros((8, 128), jnp.float32)
        slots[j, 8:16] = lines
    for step, at, skip in ((-1, 0, 0), (1, 32, 2)):
        halves_of = [jnp.zeros((8, 128), jnp.float32), lines]
        for r in range(3):
            for h in range(2):
                index = 2 * r + h
                pair = jnp.where(
                    low, pltpu.roll(segs[r][2 * h][at : at + 8], 126, 1), pltpu.roll(segs[r][2 * h + 1][at : at + 8], 62, 1)
                )
                to = 2 * (index % 4)
                part = rolled(pair, to - skip, 0)
                halves_of[index // 4] = jnp.where((row >= to) & (row < to + 2), part, halves_of[index // 4])
        slot = slot_at(step, 0)
        slots[slot, 0:8] = halves_of[0]
        slots[slot, 8:16] = halves_of[1]
    for lat_step, at, skip in ((-1, 0, 0), (1, 64, 2)):
        content = jnp.zeros((8, 128), jnp.float32)
        for g in range(4):
            part = rolled(sums[g][at : at + 8], 2 * g - skip, 0)
            content = jnp.where((row >= 2 * g) & (row < 2 * g + 2), part, content)
        for lon_step in (-1, 0, 1):
            slots[slot_at(lon_step, lat_step), 0:8] = content


def collect_kernel(tiles, slots, merged, first, second, lines):
    place = Place()
    row = row_of()
    lane = lax.broadcasted_iota(jnp.int32, (8, 128), 1)
    own_lane = within(lane, LAT_OWN)
    r_of = (lane >= SEG).astype(jnp.int32) + (lane >= 2 * SEG).astype(jnp.int32)
    lon = lane - SEG * r_of
    sides = []
    for lat_step, share in ((-1, place.left["lat"]), (1, place.right["lat"])):
        before, same, after = (slots[slot_at(lon_step, lat_step), 0:8] for lon_step in (-1, 0, 1))
        side = jnp.where(within(lon, LON_OWN), same, 0.0)
        side = side + jnp.where(within(lon, 2), pltpu.roll(before, 128 - LON_OWN, 1), 0.0)
        side = side + jnp.where((lon >= LON_OWN) & (lon < LON_OWN + 2), pltpu.roll(after, LON_OWN, 1), 0.0)
        sides.append(side * share)
    blank = jnp.zeros((56, 128), jnp.float32)
    from_lat = []
    for g in range(4):
        head = jnp.where(within(row, 2), rolled(sides[0], 2 - 2 * g, 0), 0.0)
        tail = jnp.where(row < 2, rolled(sides[1], -2 * g, 0), 0.0)
        from_lat.append(jnp.concatenate([head, blank, tail, blank], axis=0).T)
    left = [slots[slot_at(-1, 0), at : at + 8] for at in (0, 8)]
    right = [slots[slot_at(1, 0), at : at + 8] for at in (0, 8)]
    for r in range(3):
        for g in range(4):
            index = 2 * r + g // 2
            shift = 66 if g % 2 else 2
            to = 2 * (index % 4)
            head = jnp.where(within(row, 2) & own_lane, pltpu.roll(rolled(left[index // 4], 2 - to, 0), shift, 1), 0.0)
            tail = jnp.where((row < 2) & own_lane, pltpu.roll(rolled(right[index // 4], -to, 0), shift, 1), 0.0)
            seg = tiles[r, g] + from_lat[g][r * SEG : (r + 1) * SEG]
            merged[r, g] = jnp.concatenate([seg[0:8] + head, seg[8:32], seg[32:40] + tail], axis=0)
    total = slots[0, 8:16]
    for j in range(1, slots.shape[0]):
        total = total + slots[j, 8:16]
    lines[...] = total
    low = lax.broadcasted_iota(jnp.int32, (SEG, 128), 1) < LAT_OWN

    def message(r, g):
        data = jnp.where(low, pltpu.roll(merged[r, g], 126, 1), pltpu.roll(merged[r, g + 1], 62, 1))
        return jnp.concatenate([data[:32], jnp.where(row < 4, data[32:], total)], axis=0)

    first[...], second[...] = place.messages("tm", message(0, 0), message(2, 2))


def join_kernel(tiles, got_first, got_second, joined, first, second):
    place = Place()
    lower = lax.broadcasted_iota(jnp.int32, (8, 128), 0) < 4
    for r in range(3):
        for g in range(4):
            left, right = place.received("lon", got_first[r, g // 2], got_second[r, g // 2])
            if g % 2:
                left, right = pltpu.roll(left, 4, 0), pltpu.roll(right, 4, 0)
            joined[r, g, 0:8] = tiles[r, g, 0:8] + jnp.where(lower, left, 0.0)
            joined[r, g, 8:32] = tiles[r, g, 8:32]
            joined[r, g, 32:40] = tiles[r, g, 32:40] + jnp.where(lower, right, 0.0)
    for g in range(4):
        first[g], second[g] = place.messages("tm", joined[0, g], joined[2, g])


def turned_rows(tiles, g, left=0.0, right=0.0):
    parts = [tiles[0, g] + left, tiles[1, g], tiles[2, g] + right, jnp.zeros((8, 128), jnp.float32)]
    return jnp.concatenate(parts, axis=0).T


def turn_kernel(tiles, got_first, got_second, rows, first, second):
    place = Place()
    for g in range(4):
        block = turned_rows(tiles, g, *place.received("tm", got_first[g], got_second[g]))
        lanes = slice(g * 128, (g + 1) * 128)
        rows[:, lanes] = block[:ROWS]
        first[:, lanes], second[:, lanes] = place.messages("lat", block[0:8], block[64:72])


def embed_kernel(coefficients, inverse_diag, tiles, first, second):
    place = Place()
    pair = lax.broadcasted_iota(jnp.int32, (8, 128), 0) // 2
    heads, tails = [None] * 4, [None] * 4
    for t in range(12):
        for k, values in enumerate((coefficients, inverse_diag)):
            if 2 <= t < T_OWN + 2:
                own = jnp.concatenate([values[t - 2], jnp.zeros((LON_OWN, 128 - LAT_OWN), jnp.float32)], axis=1)
                own = jnp.concatenate([own, jnp.zeros((SEG - LON_OWN, 128), jnp.float32)], axis=0)
                seg = pltpu.roll(pltpu.roll(own, 2, 0), 2, 1)
                at, tile = 2 * (t % 2) + k, (t - 2) // 2
                head, tail = rolled(seg[0:8], 2 * at - 2, 0), rolled(seg[32:40], 2 * at, 0)
                heads[tile] = head if at == 0 else jnp.where(pair == at, head, heads[tile])
                tails[tile] = tail if at == 0 else jnp.where(pair == at, tail, tails[tile])
            else:
                seg = jnp.zeros((SEG, 128), jnp.float32)
            tiles[k, t // 4, t % 4] = seg
    for tile in range(4):
        first[tile], second[tile] = place.messages("lon", heads[tile], tails[tile])


def embed_join_kernel(tiles, got_first, got_second, joined, first, second):
    place = Place()
    row = lax.broadcasted_iota(jnp.int32, (8, 128), 0)
    for k in range(2):
        for t in range(12):
            r, g = t // 4, t % 4
            if 2 <= t < T_OWN + 2:
                at, tile = 2 * (t % 2) + k, (t - 2) // 2
                left, right = place.received("lon", got_first[tile], got_second[tile])
                left, right = rolled(left, -2 * at, 0), rolled(right, 2 - 2 * at, 0)
                joined[k, r, g, 0:8] = tiles[k, r, g, 0:8] + jnp.where(row < 2, left, 0.0)
                joined[k, r, g, 8:32] = tiles[k, r, g, 8:32]
                joined[k, r, g, 32:40] = tiles[k, r, g, 32:40] + jnp.where((row >= 2) & (row < 4), right, 0.0)
            else:
                joined[k, r, g] = tiles[k, r, g]
    low = lax.broadcasted_iota(jnp.int32, (SEG, 128), 1) < LAT_OWN

    def beside(r, g):
        return jnp.where(low, pltpu.roll(joined[0, r, g], 126, 1), pltpu.roll(joined[1, r, g], 62, 1))

    for i in range(2):
        first[i], second[i] = place.messages("tm", beside(0, 2 + i), beside(2, i))


def embed_turn_kernel(tiles, got_first, got_second, rows, first, second):
    place = Place()
    lane = lax.broadcasted_iota(jnp.int32, (SEG, 128), 1)
    own = (lane >= 2) & (lane < LAT_OWN + 2)
    row = lax.broadcasted_iota(jnp.int32, (8, 128), 0)
    for g in range(4):
        lanes = slice(g * 128, (g + 1) * 128)
        left, right = place.received("tm", got_first[g % 2], got_second[g % 2])
        blocks = []
        for k in range(2):
            shift = 66 if k else 2
            if g < 2:
                block = turned_rows(tiles.at[k], g, left=jnp.where(own, pltpu.roll(left, shift, 1), 0.0))
            else:
                block = turned_rows(tiles.at[k], g, right=jnp.where(own, pltpu.roll(right, shift, 1), 0.0))
            rows[k, :, lanes] = block[:ROWS]
            blocks.append(block)
        head = jnp.where(row < 4, blocks[0][0:8], pltpu.roll(blocks[1][0:8], 2, 0))
        tail = jnp.where(row < 2, blocks[0][64:72], pltpu.roll(blocks[1][64:72], 2, 0))
        first[:, lanes], second[:, lanes] = place.messages("lat", head, tail)


def last_kernel(tiles, got_first, got_second, lines, got_lines, residual, scaled, image, image_scaled, step_out, residual_out):
    place = Place()
    left, right = place.received("tm", got_first[...], got_second[...])
    lane = lax.broadcasted_iota(jnp.int32, (SEG, 128), 1)
    own = within(lane, LAT_OWN)
    merged = []
    for g in range(4):
        side = right if g < 2 else left
        side = jnp.where(own, pltpu.roll(side, 66 if g % 2 else 2, 1), 0.0)
        block = turned_rows(tiles, g, right=side) if g < 2 else turned_rows(tiles, g, left=side)
        merged.append(block[:ROWS])
    merged = jnp.concatenate(merged, axis=1)
    total = lines[...] + got_lines[...] + got_first[32:40] + got_second[32:40]
    norm, curvature, image_norm, image_curvature = (jnp.sum(total[i : i + 1], axis=1, keepdims=True) for i in range(4, 8))
    step_size = norm / curvature
    next_norm = step_size * step_size * image_norm - norm
    ratio = next_norm / norm
    next_curvature = curvature - 2.0 * step_size * image_norm + step_size * step_size * image_curvature
    step_next = next_norm / (next_curvature - ratio * next_norm / step_size)
    direction = scaled[...] - step_size * image_scaled[...] + ratio * scaled[...]
    newton = step_size * scaled[...] + step_next * direction
    left_over = residual[...] - step_size * image[...] - step_next * (image[...] - step_size * merged + ratio * image[...])
    for values, out in ((newton, step_out), (left_over, residual_out)):
        for g in range(4):
            turned = jnp.concatenate([group(values, g), jnp.zeros((128 - ROWS, 128), jnp.float32)], axis=0).T
            turned = pltpu.roll(turned, 126, 1)
            for r in range(3):
                t = 4 * r + g - 2
                if 0 <= t < T_OWN:
                    out[t] = pltpu.roll(turned[r * SEG : (r + 1) * SEG], SEG - 2, 0)[:LON_OWN, :LAT_OWN]


def matchings(count):
    first = [(i, i ^ 1) for i in range(count)]
    return first, [(i, (((i + 1) ^ 1) - 1) % count) for i in range(count)]


def swap(first, second, axis):
    first_pairs, second_pairs = matchings(lax.axis_size(axis))
    return lax.ppermute(first, axis, first_pairs), lax.ppermute(second, axis, second_pairs)


def shaped(*shape):
    return jax.ShapeDtypeStruct(shape, jnp.float32)


def call(kernel, out_shape, name, *args, scratch=(), far=(), limit=24):
    vmem = pl.BlockSpec(memory_space=pltpu.VMEM)
    hbm = pl.BlockSpec(memory_space=pltpu.HBM)
    return pl.pallas_call(
        kernel,
        in_specs=[hbm if i in far else vmem for i in range(len(args))],
        out_specs=[vmem] * len(out_shape),
        out_shape=out_shape,
        scratch_shapes=scratch,
        compiler_params=pltpu.CompilerParams(vmem_limit_bytes=limit * 1024 * 1024),
        cost_estimate=pl.CostEstimate(flops=10**9, bytes_accessed=20 * 10**6, transcendentals=0),
        name=name,
    )(*args)


LON_MESSAGE, TM_MESSAGE, LAT_MESSAGE = (3, 2, 8, 128), (4, SEG, 128), (8, LANES)
TILES = (3, 4, SEG, 128)
VECTOR = (ROWS, LANES)
SCRATCH = [pltpu.VMEM((4 * BLOCK, 384), jnp.float32)] * 2
CELLS = (HOURS, LAT_CELLS, LON_CELLS)


def exchange(tiles, first, second):
    first, second = swap(first, second, "lon")
    tiles, first, second = call(
        join_kernel, (shaped(*TILES), shaped(*TM_MESSAGE), shaped(*TM_MESSAGE)), "join", tiles, first, second
    )
    first, second = swap(first, second, "tm")
    rows, first, second = call(
        turn_kernel, (shaped(*VECTOR), shaped(*LAT_MESSAGE), shaped(*LAT_MESSAGE)), "turn", tiles, first, second
    )
    return rows, *swap(first, second, "lat")


def fold_and_sum(tiles, slots, lines_shape):
    slots = lax.all_to_all(slots, ("lon", "lat"), 0, 0, tiled=True)
    message = shaped(SEG, 128)
    tiles, first, second, lines = call(
        collect_kernel, (shaped(*TILES), message, message, lines_shape), "collect", tiles, slots
    )
    first, second = swap(first, second, "tm")
    count = lax.axis_size("tm")
    return tiles, first, second, lines, lax.ppermute(lines, "tm", [(i, (i + 2) % count) for i in range(count)])


def expand(coefficients, inverse_diag):
    tiles, message = shaped(2, *TILES), shaped(4, 8, 128)
    tiles_here, first, second = call(
        embed_kernel, (tiles, message, message), "embed", coefficients, inverse_diag
    )
    first, second = swap(first, second, "lon")
    message = shaped(2, SEG, 128)
    tiles_here, first, second = call(embed_join_kernel, (tiles, message, message), "embed_join", tiles_here, first, second)
    first, second = swap(first, second, "tm")
    shapes = (shaped(2, *VECTOR), shaped(*LAT_MESSAGE), shaped(*LAT_MESSAGE))
    both, first, second = call(embed_turn_kernel, shapes, "embed_turn", tiles_here, first, second)
    return both, *swap(first, second, "lat")


def per_device(precip, offset, coefficients, inverse_diag):
    lat_total = LAT_CELLS * lax.axis_size("lat")
    lat_index = (lax.axis_index("lat") * LAT_CELLS + jnp.arange(LAT_CELLS, dtype=jnp.int32)).astype(jnp.float32)
    area = jnp.cos((90.0 - (lat_index + 0.5) * 180.0 / lat_total) * (jnp.pi / 180.0))
    area = jnp.broadcast_to(area[:, None], (LAT_CELLS, LON_CELLS))
    tabs = tables()
    ends = (shaped(*TILES), shaped(*LON_MESSAGE), shaped(*LON_MESSAGE))
    vector = shaped(*VECTOR)

    both = expand(coefficients.transpose(0, 2, 1), inverse_diag.transpose(0, 2, 1))
    weight, diag, tiles, first, second = call(
        start_kernel, (shaped(*CELLS), vector, *ends), "start", *both, area, offset, precip, *tabs,
        scratch=[pltpu.VMEM(CELLS, jnp.float32)] * 2 + SCRATCH + [pltpu.SemaphoreType.DMA((2 * STEPS,))],
        far=(4, 5), limit=47,
    )
    lines = shaped(8, 128)
    residual, scaled, tiles, first, second, sums = call(
        functools.partial(hessian_kernel, again=False), (vector, vector, *ends, lines), "hessian",
        *exchange(tiles, first, second), diag, weight, *tabs, scratch=SCRATCH,
    )
    slots = shaped(lax.axis_size("lon") * lax.axis_size("lat"), 16, 128)
    image, image_scaled, tiles, slots = call(
        functools.partial(hessian_kernel, again=True), (vector, vector, ends[0], slots), "hessian_again",
        *exchange(tiles, first, second), diag, weight, *tabs, sums, scratch=SCRATCH,
    )
    out = shaped(T_OWN, LON_OWN, LAT_OWN)
    outs = call(
        last_kernel, (out, out), "last", *fold_and_sum(tiles, slots, lines), residual, scaled, image, image_scaled
    )
    return tuple(v.transpose(0, 2, 1) for v in outs)


def solution(mesh):
    return jax.shard_map(
        per_device, mesh=mesh, in_specs=(P(*SPLIT),) * 4, out_specs=(P(*SPLIT),) * 2, check_vma=False
    )
```

time: 186 us -> 101 us (0.54); the launches traced: 184 us -> 101 us
  matrix products: 43.1 us -> 0 us
  starting transfers between devices: 61.7 us -> 31.4 us
  waiting for transfers between devices: 54.4 us -> 31.4 us
  Pallas kernels: 0 us -> 17.9 us
  blocking collectives: 0 us -> 17.3 us
  other arithmetic: 15.5 us -> 0.05 us
  between operations: 7.49 us -> 0.85 us
    dot_general x18 -> x0, matrix products: 43.1 us -> none  [the longest x3 14.9 us: evaluate(): return jnp.einsum('tbl,st->sbl', partial_value, time_tab, precision=highest)]
    ppermute x44 -> x21, starting transfers between devices: 61.7 us -> 31.4 us  [the longest x10 21.2 us: swap(): lax.ppermute(second, axis, second_pairs)]
    ppermute x44 -> x21, waiting for transfers between devices: 54.4 us -> 31.4 us  [the longest x10 25.1 us: swap(): lax.ppermute(second, axis, second_pairs)]
    pallas_call x0 -> x12, Pallas kernels: none -> 17.9 us  [call(): pl.pallas_call(kernel, in_specs=[hbm if i in far else vmem for i in range...]
    all_to_all x0 -> x1, blocking collectives: none -> 17.3 us  [fold_and_sum(): slots = lax.all_to_all(slots, ('lon', 'lat'), 0, 0, tiled=True)]
    add x27 -> x0, other arithmetic: 4.67 us -> none  [the longest x8 2.72 us: all_sum(): values + sum((lax.ppermute(values, axis, [(i, i ^ d) for i in range(count...]
    another operation x2 -> x0, other arithmetic: 2.69 us -> none  [the longest x1 1.37 us: per_device(): jnp.stack([jnp.sum(core(residual * direction)), jnp.sum(direction * image...]
    mul x16 -> x0, other arithmetic: 2.14 us -> none  [the longest x9 1.64 us: penalty(): second * jnp.where(place == 0, 1.0 - has_left, jnp.where(place == size -...]
  transfers between devices with their start and end apart: 44 -> 21, of which waited for: 27 -> 16; matrix products, arithmetic and copies ran while one was open for 3% -> 0% of each run, Pallas kernels for 0% -> 0%
where the time goes in v1:
time: 101 us
  starting transfers between devices  31.4 us (31%)
  waiting for transfers between devices  31.4 us (31%)
  Pallas kernels  17.9 us (18%)
  blocking collectives  17.3 us (17%)
  local copies, waits for them, and re-layouts  1.92 us (2%)
    ppermute x10, waiting for transfers between devices, swap(): lax.ppermute(second, axis, second_pairs)  25.1 us
    ppermute x10, starting transfers between devices, swap(): lax.ppermute(second, axis, second_pairs)  21.2 us
    pallas_call x12, Pallas kernels, call(): pl.pallas_call(kernel, in_specs=[hbm if i in far else vmem for i in range...  17.9 us
    all_to_all x1, blocking collectives, fold_and_sum(): slots = lax.all_to_all(slots, ('lon', 'lat'), 0, 0, tiled=True)  17.3 us
    ppermute x10, starting transfers between devices, swap(): lax.ppermute(first, axis, first_pairs)  9.1 us
    ppermute x10, waiting for transfers between devices, swap(): lax.ppermute(first, axis, first_pairs)  3.77 us
    ppermute x1, waiting for transfers between devices, fold_and_sum(): lax.ppermute(lines, 'tm', [(i, (i + 2) % count) for i in range(count)])  2.53 us
  transfers between devices with their start and end apart: 21, of which 16 were waited for; matrix products, arithmetic and copies ran while one was open for 0% of the time, Pallas kernels for 0%

profile of v1, /device:TPU:0, one launch (start us, length us, event | category | flops | bytes accessed | tf_op | source)
XLA Modules:
  0.0 100.9 jit_solution(7439629687763535099)
XLA Ops:
  0.6 0.9 copy-done.4
  1.5 0.9 copy-done.5
  2.6 3.4 %collective-permute-start = (f32[4,8,128]{2,1,0:T(8,128)S(1)}, f32[4,8,128]{2,1,0:T(8,128)S(1)}, u32[]{:S(2)}, u32[]{:S(2)}) collective-permute-start(f32[4,8,128]{2,1,0:T(8,128)S(1)} %get-tuple-element.45), channel_id=1, source_target_pairs={{0,16},{16,0},{32,48},{48,32},{64,80},{80,64},{96,112},{112,96},{1... | collective-permute-start | bytes 49160 | tf_op jit(solution)/shard_map/ppermute | solution.py:524
  6.0 2.5 %collective-permute-start.1 = (f32[4,8,128]{2,1,0:T(8,128)S(1)}, f32[4,8,128]{2,1,0:T(8,128)S(1)}, u32[]{:S(2)}, u32[]{:S(2)}) collective-permute-start(f32[4,8,128]{2,1,0:T(8,128)S(1)} %get-tuple-element.46), channel_id=1, source_target_pairs={{0,112},{16,32},{32,16},{48,64},{64,48},{80,96},{96,80},{112,0},{1... | collective-permute-start | bytes 49160 | tf_op jit(solution)/shard_map/ppermute | solution.py:524
  8.6 4.8 %collective-permute-done.1.got_second = f32[4,8,128]{2,1,0:T(8,128)S(1)} collective-permute-done((f32[4,8,128]{2,1,0:T(8,128)S(1)}, f32[4,8,128]{2,1,0:T(8,128)S(1)}, u32[]{:S(2)}, u32[]{:S(2)}) %collective-permute-start.1) | collective-permute-done | bytes 16416 | tf_op jit(solution)/shard_map/ppermute | solution.py:524
  13.6 0.8 collective-permute-start.3
  14.8 2.3 %collective-permute-done.3.got_second = f32[2,40,128]{2,1,0:T(8,128)S(1)} collective-permute-done((f32[2,40,128]{2,1,0:T(8,128)S(1)}, f32[2,40,128]{2,1,0:T(8,128)S(1)}, u32[]{:S(2)}, u32[]{:S(2)}) %collective-permute-start.3) | collective-permute-done | bytes 40992 | tf_op jit(solution)/shard_map/ppermute | solution.py:524
  17.4 2.0 %collective-permute-start.4 = (f32[8,512]{1,0:T(8,128)S(1)}, f32[8,512]{1,0:T(8,128)S(1)}, u32[]{:S(2)}, u32[]{:S(2)}) collective-permute-start(f32[8,512]{1,0:T(8,128)S(1)} %get-tuple-element.51), channel_id=1, source_target_pairs={{0,4},{4,0},{8,12},{12,8},{1,5},{5,1},{9,13},{13,9},{2,6},{6,2},{1... | collective-permute-start | bytes 49160 | tf_op jit(solution)/shard_map/ppermute | solution.py:524
  19.4 2.5 %collective-permute-start.5 = (f32[8,512]{1,0:T(8,128)S(1)}, f32[8,512]{1,0:T(8,128)S(1)}, u32[]{:S(2)}, u32[]{:S(2)}) collective-permute-start(f32[8,512]{1,0:T(8,128)S(1)} %get-tuple-element.52), channel_id=1, source_target_pairs={{0,12},{4,8},{8,4},{12,0},{1,13},{5,9},{9,5},{13,1},{2,14},{6,10},... | collective-permute-start | bytes 49160 | tf_op jit(solution)/shard_map/ppermute | solution.py:524
  21.9 2.4 %collective-permute-done.5.got_second = f32[8,512]{1,0:T(8,128)S(1)} collective-permute-done((f32[8,512]{1,0:T(8,128)S(1)}, f32[8,512]{1,0:T(8,128)S(1)}, u32[]{:S(2)}, u32[]{:S(2)}) %collective-permute-start.5) | collective-permute-done | bytes 16416 | tf_op jit(solution)/shard_map/ppermute | solution.py:524
  24.5 7.2 %start.1 = (f32[32,256,128]{2,1,0:T(8,128)S(1)}, f32[80,512]{1,0:T(8,128)S(1)}, f32[3,4,40,128]{3,2,1,0:T(8,128)S(1)}, f32[3,2,8,128]{3,2,1,0:T(8,128)S(1)}, f32[3,2,8,128]{3,2,1,0:T(8,128)S(1)}) custom-call(f32[2,80,512]{2,1,0:T(8,128)S(1)} %get-tuple-element.50.both, f32[8,512]{1,0:T(8,128)S(1)} %collective-permute-done.4.got_first, ...), custom_call_target="tpu_custom_call" | custom-call | flops 1000000000 | bytes 20000000 | tf_op jit(solution)/shard_map/start/pallas_call | solution.py:534
  31.8 4.5 %collective-permute-start.7 = (f32[3,2,8,128]{3,2,1,0:T(8,128)S(1)}, f32[3,2,8,128]{3,2,1,0:T(8,128)S(1)}, u32[]{:S(2)}, u32[]{:S(2)}) collective-permute-start(f32[3,2,8,128]{3,2,1,0:T(8,128)S(1)} %get-tuple-element.55), channel_id=1, source_target_pairs={{0,112},{16,32},{32,16},{48,64},{64,48},{80,96},{96,80},{112,0},{1... | collective-permute-start | bytes 73736 | tf_op jit(solution)/shard_map/ppermute | solution.py:524
  36.3 0.8 collective-permute-done.6.got_first
  37.1 2.2 %collective-permute-done.7.got_second = f32[3,2,8,128]{3,2,1,0:T(8,128)S(1)} collective-permute-done((f32[3,2,8,128]{3,2,1,0:T(8,128)S(1)}, f32[3,2,8,128]{3,2,1,0:T(8,128)S(1)}, u32[]{:S(2)}, u32[]{:S(2)}) %collective-permute-start.7) | collective-permute-done | bytes 24608 | tf_op jit(solution)/shard_map/ppermute | solution.py:524
  40.7 3.0 %collective-permute-done.9.got_second = f32[4,40,128]{2,1,0:T(8,128)S(1)} collective-permute-done((f32[4,40,128]{2,1,0:T(8,128)S(1)}, f32[4,40,128]{2,1,0:T(8,128)S(1)}, u32[]{:S(2)}, u32[]{:S(2)}) %collective-permute-start.9) | collective-permute-done | bytes 81952 | tf_op jit(solution)/shard_map/ppermute | solution.py:524
  44.2 2.6 %collective-permute-start.11 = (f32[8,512]{1,0:T(8,128)S(1)}, f32[8,512]{1,0:T(8,128)S(1)}, u32[]{:S(2)}, u32[]{:S(2)}) collective-permute-start(f32[8,512]{1,0:T(8,128)S(1)} %get-tuple-element.61), channel_id=1, source_target_pairs={{0,12},{4,8},{8,4},{12,0},{1,13},{5,9},{9,5},{13,1},{2,14},{6,10},... | collective-permute-start | bytes 49160 | tf_op jit(solution)/shard_map/ppermute | solution.py:524
  46.8 0.8 collective-permute-done.10.got_first
  47.6 1.5 %collective-permute-done.11.got_second = f32[8,512]{1,0:T(8,128)S(1)} collective-permute-done((f32[8,512]{1,0:T(8,128)S(1)}, f32[8,512]{1,0:T(8,128)S(1)}, u32[]{:S(2)}, u32[]{:S(2)}) %collective-permute-start.11) | collective-permute-done | bytes 16416 | tf_op jit(solution)/shard_map/ppermute | solution.py:524
  49.1 4.2 %hessian.1 = (f32[80,512]{1,0:T(8,128)S(1)}, f32[80,512]{1,0:T(8,128)S(1)}, f32[3,4,40,128]{3,2,1,0:T(8,128)S(1)}, f32[3,2,8,128]{3,2,1,0:T(8,128)S(1)}, f32[3,2...) custom-call(f32[80,512]{1,0:T(8,128)S(1)} %get-tuple-element.59.partial_rows, ...), custom_call_target="tpu_custom_call" | custom-call | flops 1000000000 | bytes 20000000 | tf_op jit(solution)/shard_map/hessian/pallas_call | solution.py:534
  53.3 2.3 %collective-permute-start.12 = (f32[3,2,8,128]{3,2,1,0:T(8,128)S(1)}, f32[3,2,8,128]{3,2,1,0:T(8,128)S(1)}, u32[]{:S(2)}, u32[]{:S(2)}) collective-permute-start(f32[3,2,8,128]{3,2,1,0:T(8,128)S(1)} %get-tuple-element.65), channel_id=1, source_target_pairs={{0,16},{16,0},{32,48},{48,32},{64,80},{80,64},{96,112},{112,96},{1... | collective-permute-start | bytes 73736 | tf_op jit(solution)/shard_map/ppermute | solution.py:524
  55.6 3.2 %collective-permute-start.13 = (f32[3,2,8,128]{3,2,1,0:T(8,128)S(1)}, f32[3,2,8,128]{3,2,1,0:T(8,128)S(1)}, u32[]{:S(2)}, u32[]{:S(2)}) collective-permute-start(f32[3,2,8,128]{3,2,1,0:T(8,128)S(1)} %get-tuple-element.66), channel_id=1, source_target_pairs={{0,112},{16,32},{32,16},{48,64},{64,48},{80,96},{96,80},{112,0},{1... | collective-permute-start | bytes 73736 | tf_op jit(solution)/shard_map/ppermute | solution.py:524
  58.8 4.3 %collective-permute-done.13.got_second = f32[3,2,8,128]{3,2,1,0:T(8,128)S(1)} collective-permute-done((f32[3,2,8,128]{3,2,1,0:T(8,128)S(1)}, f32[3,2,8,128]{3,2,1,0:T(8,128)S(1)}, u32[]{:S(2)}, u32[]{:S(2)}) %collective-permute-start.13) | collective-permute-done | bytes 24608 | tf_op jit(solution)/shard_map/ppermute | solution.py:524
  63.2 0.8 collective-permute-start.15
  64.4 3.0 %collective-permute-done.15.got_second = f32[4,40,128]{2,1,0:T(8,128)S(1)} collective-permute-done((f32[4,40,128]{2,1,0:T(8,128)S(1)}, f32[4,40,128]{2,1,0:T(8,128)S(1)}, u32[]{:S(2)}, u32[]{:S(2)}) %collective-permute-start.15) | collective-permute-done | bytes 81952 | tf_op jit(solution)/shard_map/ppermute | solution.py:524
  68.1 2.5 %collective-permute-start.17 = (f32[8,512]{1,0:T(8,128)S(1)}, f32[8,512]{1,0:T(8,128)S(1)}, u32[]{:S(2)}, u32[]{:S(2)}) collective-permute-start(f32[8,512]{1,0:T(8,128)S(1)} %get-tuple-element.72), channel_id=1, source_target_pairs={{0,12},{4,8},{8,4},{12,0},{1,13},{5,9},{9,5},{13,1},{2,14},{6,10},... | collective-permute-start | bytes 49160 | tf_op jit(solution)/shard_map/ppermute | solution.py:524
  71.3 1.7 %collective-permute-done.17.got_second = f32[8,512]{1,0:T(8,128)S(1)} collective-permute-done((f32[8,512]{1,0:T(8,128)S(1)}, f32[8,512]{1,0:T(8,128)S(1)}, u32[]{:S(2)}, u32[]{:S(2)}) %collective-permute-start.17) | collective-permute-done | bytes 16416 | tf_op jit(solution)/shard_map/ppermute | solution.py:524
  73.1 4.3 %hessian_again.1 = (f32[80,512]{1,0:T(8,128)S(1)}, f32[80,512]{1,0:T(8,128)S(1)}, f32[3,4,40,128]{3,2,1,0:T(8,128)S(1)}, f32[32,16,128]{2,1,0:T(8,128)S(1)}) custom-call(f32[80,512]{1,0:T(8,128)S(1)} %get-tuple-element.70.partial_rows, f32[8,512]{1,0:T(8,128)S(1)} %collective-permute-done.16.got_first, f32[8,512]{1,0:T(8,128)S(1)} %collective-permute-done.17.got_second, ...), custom_call_target="tpu_custom_call" | custom-call | flops 1000000000 | bytes 20000000 | tf_op jit(solution)/shard_map/hessian_again/pallas_call | solution.py:534
  77.4 17.3 %all_to_all.5.slots = f32[32,16,128]{2,1,0:T(8,128)S(1)} all-to-all(f32[32,16,128]{2,1,0:T(8,128)S(1)} %get-tuple-element.75), channel_id=1, replica_groups=mesh['lon'=8,'lat'=4,'tm'=4] {'lon','lat'}, dimensions={0} | all-to-all | bytes 524288 | tf_op jit(solution)/shard_map/all_to_all | solution.py:566
  95.0 1.1 %collective-permute-start.19 = (f32[40,128]{1,0:T(8,128)S(1)}, f32[40,128]{1,0:T(8,128)S(1)}, u32[]{:S(2)}, u32[]{:S(2)}) collective-permute-start(f32[40,128]{1,0:T(8,128)S(1)} %get-tuple-element.78), channel_id=1, source_target_pairs={{0,3},{1,2},{2,1},{3,0},{4,7},{5,6},{6,5},{7,4},{8,11},{9,10},{10,... | collective-permute-start | bytes 61448 | tf_op jit(solution)/shard_map/ppermute | solution.py:524
  96.1 1.1 %collective-permute-start.20 = (f32[8,128]{1,0:T(8,128)S(1)}, f32[8,128]{1,0:T(8,128)S(1)}, u32[]{:S(2)}, u32[]{:S(2)}) collective-permute-start(f32[8,128]{1,0:T(8,128)S(1)} %get-tuple-element.79.lines), channel_id=1, source_target_pairs={{0,2},{1,3},{2,0},{3,1},{4,6},{5,7},{6,4},{7,5},{8,10},{9,11},{10,... | collective-permute-start | bytes 12296 | tf_op jit(solution)/shard_map/ppermute | solution.py:573
  97.2 2.5 %collective-permute-done.20.got_lines = f32[8,128]{1,0:T(8,128)S(1)} collective-permute-done((f32[8,128]{1,0:T(8,128)S(1)}, f32[8,128]{1,0:T(8,128)S(1)}, u32[]{:S(2)}, u32[]{:S(2)}) %collective-permute-start.20) | collective-permute-done | bytes 4128 | tf_op jit(solution)/shard_map/ppermute | solution.py:573
  99.7 1.2 %last.1 = (f32[8,32,64]{2,1,0:T(8,128)}, f32[8,32,64]{2,1,0:T(8,128)}) custom-call(f32[3,4,40,128]{3,2,1,0:T(8,128)S(1)} %get-tuple-element.76.tiles, f32[40,128]{1,0:T(8,128)S(1)} %collective-permute-done.18.got_first, f32[40,128]{1,0:T(8,128)S(1)} %collective-permute-done.19.got_second, f32[8,128]{1,0:T(8,128)S(1)} %get-tuple-element.79.lines, ...), custom_call_target="tpu_custom_call" | custom-call | flops 1000000000 | bytes 20000000 | tf_op jit(solution)/shard_map/last/pallas_call | solution.py:534
  (37 shorter events, 5.6 us)
Async XLA Ops:
  0.6 0.9 copy-start.4
  1.5 0.9 copy-start.5
  2.6 21.8 %copy-start = (bf16[384,384]{1,0:T(8,128)(2,1)S(1)}, bf16[384,384]{1,0:T(8,128)(2,1)}, u32[]{:S(2)}) copy-start(bf16[384,384]{1,0:T(8,128)(2,1)} %constant.40.lon_up) | copy-start | bytes 884740
  2.6 21.8 %copy-start.1 = (bf16[384,256]{1,0:T(8,128)(2,1)S(1)}, bf16[384,256]{1,0:T(8,128)(2,1)}, u32[]{:S(2)}) copy-start(bf16[384,256]{1,0:T(8,128)(2,1)} %constant.43.lon_down) | copy-start | bytes 589828
  2.6 21.8 %copy-start.2 = (bf16[256,240]{1,0:T(8,128)(2,1)S(1)}, bf16[256,240]{1,0:T(8,128)(2,1)}, u32[]{:S(2)}) copy-start(bf16[256,240]{1,0:T(8,128)(2,1)} %constant.28.lat_up) | copy-start | bytes 368644
  2.6 21.8 %copy-start.3 = (bf16[2,80,384]{2,1,0:T(8,128)(2,1)S(1)}, bf16[2,80,384]{2,1,0:T(8,128)(2,1)}, u32[]{:S(2)}) copy-start(bf16[2,80,384]{2,1,0:T(8,128)(2,1)} %constant.35.lat_down) | copy-start | bytes 368644
  2.6 5.9 %collective-permute-start = (f32[4,8,128]{2,1,0:T(8,128)S(1)}, f32[4,8,128]{2,1,0:T(8,128)S(1)}, u32[]{:S(2)}, u32[]{:S(2)}) collective-permute-start(f32[4,8,128]{2,1,0:T(8,128)S(1)} %get-tuple-element.45), channel_id=1, source_target_pairs={{0,16},{16,0},{32,48},{48,32},{64,80},{80,64},{96,112},{112,96},{1... | collective-permute-start | bytes 49160 | tf_op jit(solution)/shard_map/ppermute | solution.py:524
  6.0 7.4 %collective-permute-start.1 = (f32[4,8,128]{2,1,0:T(8,128)S(1)}, f32[4,8,128]{2,1,0:T(8,128)S(1)}, u32[]{:S(2)}, u32[]{:S(2)}) collective-permute-start(f32[4,8,128]{2,1,0:T(8,128)S(1)} %get-tuple-element.46), channel_id=1, source_target_pairs={{0,112},{16,32},{32,16},{48,64},{64,48},{80,96},{96,80},{112,0},{1... | collective-permute-start | bytes 49160 | tf_op jit(solution)/shard_map/ppermute | solution.py:524
  13.5 1.3 %collective-permute-start.2 = (f32[2,40,128]{2,1,0:T(8,128)S(1)}, f32[2,40,128]{2,1,0:T(8,128)S(1)}, u32[]{:S(2)}, u32[]{:S(2)}) collective-permute-start(f32[2,40,128]{2,1,0:T(8,128)S(1)} %get-tuple-element.48), channel_id=1, source_target_pairs={{0,1},{1,0},{2,3},{3,2},{4,5},{5,4},{6,7},{7,6},{8,9},{9,8},{10,11... | collective-permute-start | bytes 122888 | tf_op jit(solution)/shard_map/ppermute | solution.py:524
  13.6 3.5 %collective-permute-start.3 = (f32[2,40,128]{2,1,0:T(8,128)S(1)}, f32[2,40,128]{2,1,0:T(8,128)S(1)}, u32[]{:S(2)}, u32[]{:S(2)}) collective-permute-start(f32[2,40,128]{2,1,0:T(8,128)S(1)} %get-tuple-element.49), channel_id=1, source_target_pairs={{0,3},{1,2},{2,1},{3,0},{4,7},{5,6},{6,5},{7,4},{8,11},{9,10},{10,... | collective-permute-start | bytes 122888 | tf_op jit(solution)/shard_map/ppermute | solution.py:524
  17.4 4.6 %collective-permute-start.4 = (f32[8,512]{1,0:T(8,128)S(1)}, f32[8,512]{1,0:T(8,128)S(1)}, u32[]{:S(2)}, u32[]{:S(2)}) collective-permute-start(f32[8,512]{1,0:T(8,128)S(1)} %get-tuple-element.51), channel_id=1, source_target_pairs={{0,4},{4,0},{8,12},{12,8},{1,5},{5,1},{9,13},{13,9},{2,6},{6,2},{1... | collective-permute-start | bytes 49160 | tf_op jit(solution)/shard_map/ppermute | solution.py:524
  19.4 4.9 %collective-permute-start.5 = (f32[8,512]{1,0:T(8,128)S(1)}, f32[8,512]{1,0:T(8,128)S(1)}, u32[]{:S(2)}, u32[]{:S(2)}) collective-permute-start(f32[8,512]{1,0:T(8,128)S(1)} %get-tuple-element.52), channel_id=1, source_target_pairs={{0,12},{4,8},{8,4},{12,0},{1,13},{5,9},{9,5},{13,1},{2,14},{6,10},... | collective-permute-start | bytes 49160 | tf_op jit(solution)/shard_map/ppermute | solution.py:524
  31.7 5.4 %collective-permute-start.6 = (f32[3,2,8,128]{3,2,1,0:T(8,128)S(1)}, f32[3,2,8,128]{3,2,1,0:T(8,128)S(1)}, u32[]{:S(2)}, u32[]{:S(2)}) collective-permute-start(f32[3,2,8,128]{3,2,1,0:T(8,128)S(1)} %get-tuple-element.54), channel_id=1, source_target_pairs={{0,16},{16,0},{32,48},{48,32},{64,80},{80,64},{96,112},{112,96},{1... | collective-permute-start | bytes 73736 | tf_op jit(solution)/shard_map/ppermute | solution.py:524
  31.8 7.5 %collective-permute-start.7 = (f32[3,2,8,128]{3,2,1,0:T(8,128)S(1)}, f32[3,2,8,128]{3,2,1,0:T(8,128)S(1)}, u32[]{:S(2)}, u32[]{:S(2)}) collective-permute-start(f32[3,2,8,128]{3,2,1,0:T(8,128)S(1)} %get-tuple-element.55), channel_id=1, source_target_pairs={{0,112},{16,32},{32,16},{48,64},{64,48},{80,96},{96,80},{112,0},{1... | collective-permute-start | bytes 73736 | tf_op jit(solution)/shard_map/ppermute | solution.py:524
  39.3 1.4 %collective-permute-start.8 = (f32[4,40,128]{2,1,0:T(8,128)S(1)}, f32[4,40,128]{2,1,0:T(8,128)S(1)}, u32[]{:S(2)}, u32[]{:S(2)}) collective-permute-start(f32[4,40,128]{2,1,0:T(8,128)S(1)} %get-tuple-element.57), channel_id=1, source_target_pairs={{0,1},{1,0},{2,3},{3,2},{4,5},{5,4},{6,7},{7,6},{8,9},{9,8},{10,11... | collective-permute-start | bytes 245768 | tf_op jit(solution)/shard_map/ppermute | solution.py:524
  39.4 4.2 %collective-permute-start.9 = (f32[4,40,128]{2,1,0:T(8,128)S(1)}, f32[4,40,128]{2,1,0:T(8,128)S(1)}, u32[]{:S(2)}, u32[]{:S(2)}) collective-permute-start(f32[4,40,128]{2,1,0:T(8,128)S(1)} %get-tuple-element.58), channel_id=1, source_target_pairs={{0,3},{1,2},{2,1},{3,0},{4,7},{5,6},{6,5},{7,4},{8,11},{9,10},{10,... | collective-permute-start | bytes 245768 | tf_op jit(solution)/shard_map/ppermute | solution.py:524
  43.8 3.8 %collective-permute-start.10 = (f32[8,512]{1,0:T(8,128)S(1)}, f32[8,512]{1,0:T(8,128)S(1)}, u32[]{:S(2)}, u32[]{:S(2)}) collective-permute-start(f32[8,512]{1,0:T(8,128)S(1)} %get-tuple-element.60), channel_id=1, source_target_pairs={{0,4},{4,0},{8,12},{12,8},{1,5},{5,1},{9,13},{13,9},{2,6},{6,2},{1... | collective-permute-start | bytes 49160 | tf_op jit(solution)/shard_map/ppermute | solution.py:524
  44.2 4.9 %collective-permute-start.11 = (f32[8,512]{1,0:T(8,128)S(1)}, f32[8,512]{1,0:T(8,128)S(1)}, u32[]{:S(2)}, u32[]{:S(2)}) collective-permute-start(f32[8,512]{1,0:T(8,128)S(1)} %get-tuple-element.61), channel_id=1, source_target_pairs={{0,12},{4,8},{8,4},{12,0},{1,13},{5,9},{9,5},{13,1},{2,14},{6,10},... | collective-permute-start | bytes 49160 | tf_op jit(solution)/shard_map/ppermute | solution.py:524
  53.3 5.5 %collective-permute-start.12 = (f32[3,2,8,128]{3,2,1,0:T(8,128)S(1)}, f32[3,2,8,128]{3,2,1,0:T(8,128)S(1)}, u32[]{:S(2)}, u32[]{:S(2)}) collective-permute-start(f32[3,2,8,128]{3,2,1,0:T(8,128)S(1)} %get-tuple-element.65), channel_id=1, source_target_pairs={{0,16},{16,0},{32,48},{48,32},{64,80},{80,64},{96,112},{112,96},{1... | collective-permute-start | bytes 73736 | tf_op jit(solution)/shard_map/ppermute | solution.py:524
  55.6 7.4 %collective-permute-start.13 = (f32[3,2,8,128]{3,2,1,0:T(8,128)S(1)}, f32[3,2,8,128]{3,2,1,0:T(8,128)S(1)}, u32[]{:S(2)}, u32[]{:S(2)}) collective-permute-start(f32[3,2,8,128]{3,2,1,0:T(8,128)S(1)} %get-tuple-element.66), channel_id=1, source_target_pairs={{0,112},{16,32},{32,16},{48,64},{64,48},{80,96},{96,80},{112,0},{1... | collective-permute-start | bytes 73736 | tf_op jit(solution)/shard_map/ppermute | solution.py:524
  63.1 1.4 %collective-permute-start.14 = (f32[4,40,128]{2,1,0:T(8,128)S(1)}, f32[4,40,128]{2,1,0:T(8,128)S(1)}, u32[]{:S(2)}, u32[]{:S(2)}) collective-permute-start(f32[4,40,128]{2,1,0:T(8,128)S(1)} %get-tuple-element.68), channel_id=1, source_target_pairs={{0,1},{1,0},{2,3},{3,2},{4,5},{5,4},{6,7},{7,6},{8,9},{9,8},{10,11... | collective-permute-start | bytes 245768 | tf_op jit(solution)/shard_map/ppermute | solution.py:524
  63.2 4.2 %collective-permute-start.15 = (f32[4,40,128]{2,1,0:T(8,128)S(1)}, f32[4,40,128]{2,1,0:T(8,128)S(1)}, u32[]{:S(2)}, u32[]{:S(2)}) collective-permute-start(f32[4,40,128]{2,1,0:T(8,128)S(1)} %get-tuple-element.69), channel_id=1, source_target_pairs={{0,3},{1,2},{2,1},{3,0},{4,7},{5,6},{6,5},{7,4},{8,11},{9,10},{10,... | collective-permute-start | bytes 245768 | tf_op jit(solution)/shard_map/ppermute | solution.py:524
  67.5 3.8 %collective-permute-start.16 = (f32[8,512]{1,0:T(8,128)S(1)}, f32[8,512]{1,0:T(8,128)S(1)}, u32[]{:S(2)}, u32[]{:S(2)}) collective-permute-start(f32[8,512]{1,0:T(8,128)S(1)} %get-tuple-element.71), channel_id=1, source_target_pairs={{0,4},{4,0},{8,12},{12,8},{1,5},{5,1},{9,13},{13,9},{2,6},{6,2},{1... | collective-permute-start | bytes 49160 | tf_op jit(solution)/shard_map/ppermute | solution.py:524
  68.1 4.9 %collective-permute-start.17 = (f32[8,512]{1,0:T(8,128)S(1)}, f32[8,512]{1,0:T(8,128)S(1)}, u32[]{:S(2)}, u32[]{:S(2)}) collective-permute-start(f32[8,512]{1,0:T(8,128)S(1)} %get-tuple-element.72), channel_id=1, source_target_pairs={{0,12},{4,8},{8,4},{12,0},{1,13},{5,9},{9,5},{13,1},{2,14},{6,10},... | collective-permute-start | bytes 49160 | tf_op jit(solution)/shard_map/ppermute | solution.py:524
  94.9 4.8 %collective-permute-start.18 = (f32[40,128]{1,0:T(8,128)S(1)}, f32[40,128]{1,0:T(8,128)S(1)}, u32[]{:S(2)}, u32[]{:S(2)}) collective-permute-start(f32[40,128]{1,0:T(8,128)S(1)} %get-tuple-element.77), channel_id=1, source_target_pairs={{0,1},{1,0},{2,3},{3,2},{4,5},{5,4},{6,7},{7,6},{8,9},{9,8},{10,11... | collective-permute-start | bytes 61448 | tf_op jit(solution)/shard_map/ppermute | solution.py:524
  95.0 4.7 %collective-permute-start.19 = (f32[40,128]{1,0:T(8,128)S(1)}, f32[40,128]{1,0:T(8,128)S(1)}, u32[]{:S(2)}, u32[]{:S(2)}) collective-permute-start(f32[40,128]{1,0:T(8,128)S(1)} %get-tuple-element.78), channel_id=1, source_target_pairs={{0,3},{1,2},{2,1},{3,0},{4,7},{5,6},{6,5},{7,4},{8,11},{9,10},{10,... | collective-permute-start | bytes 61448 | tf_op jit(solution)/shard_map/ppermute | solution.py:524
  96.1 3.6 %collective-permute-start.20 = (f32[8,128]{1,0:T(8,128)S(1)}, f32[8,128]{1,0:T(8,128)S(1)}, u32[]{:S(2)}, u32[]{:S(2)}) collective-permute-start(f32[8,128]{1,0:T(8,128)S(1)} %get-tuple-element.79.lines), channel_id=1, source_target_pairs={{0,2},{1,3},{2,0},{3,1},{4,6},{5,7},{6,4},{7,5},{8,10},{9,11},{10,... | collective-permute-start | bytes 12296 | tf_op jit(solution)/shard_map/ppermute | solution.py:573

commit v2 on v1

--- a/solution.py
+++ b/solution.py
@@ -13,8 +13,10 @@
 smooth = 0.5
 
 ROWS, LANES, SEG, LAT_OWN, LON_OWN, T_OWN = 80, 512, 40, 64, 32, 8
-HOURS, LAT_CELLS, LON_CELLS, BLOCK = 32, 256, 128, 128
-STEPS = LAT_CELLS // BLOCK
+HOURS, LAT_CELLS, LON_CELLS = 32, 256, 128
+EDGE, CHUNK = 16, 32
+MID_CELLS, EDGE_CELLS = LAT_CELLS - 2 * EDGE, 2 * EDGE
+CHUNKS = MID_CELLS // CHUNK
 
 
 def spline(offsets):
@@ -36,20 +38,30 @@
     return high, (values - high.astype(jnp.float32)).astype(jnp.bfloat16)
 
 
+def middle(cells, axis=0):
+    return lax.slice_in_dim(cells, EDGE, LAT_CELLS - EDGE, axis=axis)
+
+
+def edges(cells, axis=0):
+    ends = (lax.slice_in_dim(cells, at, at + EDGE, axis=axis) for at in (0, LAT_CELLS - EDGE))
+    return jnp.concatenate(list(ends), axis=axis)
+
+
 def tables():
     lat = np.zeros((LAT_CELLS, ROWS))
     lat[:, : LAT_OWN + 4] = table(LAT_CELLS, LAT_OWN)
     high, low = halves(lat)
-    lat_up = jnp.concatenate([high, low, high], axis=1)
-    high, low = (part.T.reshape(ROWS, STEPS, BLOCK).transpose(1, 0, 2) for part in (high, low))
-    lat_down = jnp.concatenate([high, low, high], axis=2)
+    lat_tables = []
+    for part in (middle, edges):
+        up = jnp.concatenate([part(high), part(low), part(high)], axis=1)
+        lat_tables += [up, jnp.concatenate([part(high).T, part(low).T, part(high).T], axis=1)]
     lon = np.zeros((128, 3 * LON_CELLS))
     for r in range(3):
         lon[r * SEG : r * SEG + LON_OWN + 4, r * LON_CELLS : (r + 1) * LON_CELLS] = table(LON_CELLS, LON_OWN).T
     high, low = halves(lon)
     lon_up = jnp.concatenate([high, high, low], axis=0)
     lon_down = jnp.concatenate([high.T, low.T], axis=1)
-    return lat_up, lat_down, lon_up, lon_down
+    return lat_tables[:2] + [lon_up, lon_down], lat_tables[2:] + [lon_up, lon_down]
 
 
 def hour_factors():
@@ -62,15 +74,15 @@
 class Place:
     def __init__(self):
         index = {axis: lax.axis_index(axis) for axis in SPLIT}
-        self.odd = {axis: index[axis] % 2 == 1 for axis in SPLIT}
+        self.even = {axis: index[axis] % 2 == 0 for axis in SPLIT}
         self.left = {axis: jnp.where(index[axis] > 0, 1.0, 0.0) for axis in SPLIT}
         self.right = {axis: jnp.where(index[axis] < lax.axis_size(axis) - 1, 1.0, 0.0) for axis in SPLIT}
 
     def messages(self, axis, to_left, to_right):
-        return jnp.where(self.odd[axis], to_left, to_right), jnp.where(self.odd[axis], to_right, to_left)
+        return jnp.where(self.even[axis], to_left, to_right), jnp.where(self.even[axis], to_right, to_left)
 
     def received(self, axis, first, second):
-        left, right = jnp.where(self.odd[axis], first, second), jnp.where(self.odd[axis], second, first)
+        left, right = jnp.where(self.even[axis], first, second), jnp.where(self.even[axis], second, first)
         return (left, right) if axis == "lon" else (left * self.left[axis], right * self.right[axis])
 
 
@@ -152,18 +164,20 @@
     )
 
 
-def cell_block(block, vec_parts, w_of, lat_up, lat_down, lon_up, lon_down, up, down, before_cells):
+def apply_cells(values, w_of, lat_up, lat_down, lon_up, lon_down, up, down, before_chunk=None):
     outer, inner = hour_factors()
-    expanded = dot(lat_up[block * BLOCK : (block + 1) * BLOCK], vec_parts)
+    cells = lat_up.shape[0]
+    high, low = split(values)
+    expanded = dot(lat_up[...], jnp.concatenate([high, high, low], axis=0))
     high, low = split(jnp.concatenate([group(expanded, g) for g in range(4)], axis=0))
     up[...] = dot(jnp.concatenate([high, low, high], axis=1), lon_up[...])
 
     def tile(i, carry):
         start = pl.multiple_of(i * 8, 8)
-        rows = pl.ds(pl.multiple_of(block * BLOCK + start, 8), 8)
+        rows = pl.ds(start, 8)
 
         def knot(t):
-            return up[pl.ds((t % 4) * BLOCK + start, 8), (t // 4) * 128 : (t // 4 + 1) * 128]
+            return up[pl.ds((t % 4) * cells + start, 8), (t // 4) * 128 : (t // 4 + 1) * 128]
 
         back = [None] * 12
 
@@ -194,26 +208,25 @@
             add(j + 2, mid_even - mid_odd)
             add(j + 3, edge_even - edge_odd)
             for t in (j,) if j < 8 else (8, 9, 10, 11):
-                down[pl.ds((t % 4) * BLOCK + start, 8), (t // 4) * 128 : (t // 4 + 1) * 128] = back[t]
+                down[pl.ds((t % 4) * cells + start, 8), (t // 4) * 128 : (t // 4 + 1) * 128] = back[t]
             x = [x[1], x[2], x[3], None]
         return carry
 
-    before_cells(block)
-    lax.fori_loop(0, BLOCK // 8, tile, 0)
+    if before_chunk is None:
+        lax.fori_loop(0, cells // 8, tile, 0)
+    else:
+        for chunk in range(cells // CHUNK):
+            before_chunk(chunk)
+            lax.fori_loop(chunk * CHUNK // 8, (chunk + 1) * CHUNK // 8, tile, 0)
     high, low = split(down[...])
     both = dot(high, lon_down[...])
     narrow = both[:, :128] + both[:, 128:] + dot(low, lon_down[:, :128])
-    narrow = jnp.concatenate([narrow[g * BLOCK : (g + 1) * BLOCK] for g in range(4)], axis=1)
+    narrow = jnp.concatenate([narrow[g * cells : (g + 1) * cells] for g in range(4)], axis=1)
     high, low = split(narrow)
-    return dot(lat_down[block], jnp.concatenate([high, high, low], axis=0))
-
-
-def apply_cells(values, w_of, place, lat_up, lat_down, lon_up, lon_down, up, down, before_cells=lambda block: None):
-    high, low = split(values)
-    parts = jnp.concatenate([high, high, low], axis=0)
-    total = 0.0
-    for block in range(STEPS):
-        total = total + cell_block(block, parts, w_of, lat_up, lat_down, lon_up, lon_down, up, down, before_cells)
+    return dot(lat_down[...], jnp.concatenate([high, high, low], axis=0))
+
+
+def finish(total, values, place):
     extra = penalty(values, place)
     sums = [group(total, g) + extra[g] for g in range(4)]
     turned = [jnp.concatenate([part, jnp.zeros((128 - ROWS, 128), jnp.float32)], axis=0).T for part in sums]
@@ -233,28 +246,7 @@
             first[r, h], second[r, h] = place.messages("lon", *packed)
 
 
-def start_kernel(both, got_first, got_second, area, offset_far, precip_far, lat_up, lat_down, lon_up, lon_down,
-                 weight, diag, tiles, first, second, offset, precip, up, down, arrived):
-    place = Place()
-    copies = []
-    for block in range(STEPS):
-        rows = slice(block * BLOCK, (block + 1) * BLOCK)
-        for source, target in ((offset_far, offset), (precip_far, precip)):
-            at = arrived.at[len(copies)]
-            copies.append(pltpu.make_async_copy(source.at[:, rows, :], target.at[:, rows, :], at))
-    for copy in copies:
-        copy.start()
-
-    row = lax.broadcasted_iota(jnp.int32, (8, LANES), 0)
-    left, right = place.received("lat", got_first[...], got_second[...])
-
-    def with_halo(own, left, right):
-        head, tail = own[0:8] + jnp.where(row < 2, left, 0.0), own[64:72] + jnp.where((row >= 2) & (row < 4), right, 0.0)
-        return jnp.concatenate([head, own[8:64], tail, own[72:80]], axis=0)
-
-    values = with_halo(both[0], left, right)
-    diag[...] = with_halo(both[1], pltpu.roll(left, 6, 0), pltpu.roll(right, 6, 0))
-
+def start_of(area, offset, precip, weight):
     def w_of(hour, rows, value):
         linear = offset[hour, rows, :] + value
         here = area[rows, :]
@@ -262,15 +254,64 @@
         weight[hour, rows, :] = w
         return w - here * precip[hour, rows, :] * jnp.exp((1.0 - tweedie_power) * linear)
 
-    def before_cells(block):
-        for copy in copies[2 * block : 2 * block + 2]:
+    return w_of
+
+
+def start_middle_kernel(both, area, offset_far, precip_far, lat_up, lat_down, lon_up, lon_down,
+                        weight, total, offset_edges, precip_edges, offset, precip, up, down, arrived):
+    copies = []
+
+    def bring(source, source_at, target, target_at, count):
+        source, target = source.at[:, pl.ds(source_at, count), :], target.at[:, pl.ds(target_at, count), :]
+        copies.append(pltpu.make_async_copy(source, target, arrived.at[len(copies)]))
+
+    for chunk in range(CHUNKS):
+        for source, target in ((offset_far, offset), (precip_far, precip)):
+            bring(source, EDGE + chunk * CHUNK, target, chunk * CHUNK, CHUNK)
+    for source, target in ((offset_far, offset_edges), (precip_far, precip_edges)):
+        bring(source, 0, target, 0, EDGE)
+        bring(source, LAT_CELLS - EDGE, target, EDGE, EDGE)
+    for copy in copies:
+        copy.start()
+
+    def before_chunk(chunk):
+        for copy in copies[2 * chunk : 2 * chunk + 2]:
             copy.wait()
 
-    _, segs = apply_cells(values, w_of, place, lat_up, lat_down, lon_up, lon_down, up, down, before_cells)
+    w_of = start_of(area, offset, precip, weight)
+    total[...] = apply_cells(both[0], w_of, lat_up, lat_down, lon_up, lon_down, up, down, before_chunk)
+    for copy in copies[2 * CHUNKS :]:
+        copy.wait()
+
+
+def start_kernel(both, got_first, got_second, total, area, offset, precip, lat_up, lat_down, lon_up, lon_down,
+                 weight, diag, tiles, first, second, up, down):
+    place = Place()
+    row = lax.broadcasted_iota(jnp.int32, (8, LANES), 0)
+    left, right = place.received("lat", got_first[...], got_second[...])
+
+    def with_halo(own, left, right):
+        head, tail = own[0:8] + jnp.where(row < 2, left, 0.0), own[64:72] + jnp.where((row >= 2) & (row < 4), right, 0.0)
+        return jnp.concatenate([head, own[8:64], tail, own[72:80]], axis=0)
+
+    values = with_halo(both[0], left, right)
+    diag[...] = with_halo(both[1], pltpu.roll(left, 6, 0), pltpu.roll(right, 6, 0))
+    w_of = start_of(area, offset, precip, weight)
+    part = apply_cells(values, w_of, lat_up, lat_down, lon_up, lon_down, up, down)
+    _, segs = finish(total[...] + part, values, place)
     write_ends(segs, place, tiles, first, second)
 
 
-def hessian_kernel(partial_rows, got_first, got_second, diag, weight, lat_up, lat_down, lon_up, lon_down, *refs, again):
+def weigh(weight):
+    return lambda hour, rows, value: weight[hour, rows, :] * value
+
+
+def hessian_middle_kernel(partial_rows, diag, weight, lat_up, lat_down, lon_up, lon_down, total, up, down, *, again):
+    here = partial_rows[...] if again else -partial_rows[...]
+    total[...] = apply_cells(diag[...] * here, weigh(weight), lat_up, lat_down, lon_up, lon_down, up, down)
+
+
+def hessian_kernel(partial_rows, got_first, got_second, total, diag, weight, lat_up, lat_down, lon_up, lon_down, *refs, again):
     if again:
         before, residual, scaled, tiles, slots, up, down = refs
     else:
@@ -281,11 +322,8 @@
     residual[...] = here
     values = diag[...] * here
     scaled[...] = values
-
-    def w_of(hour, rows, value):
-        return weight[hour, rows, :] * value
-
-    image, segs = apply_cells(values, w_of, place, lat_up, lat_down, lon_up, lon_down, up, down)
+    part = apply_cells(values, weigh(weight), lat_up, lat_down, lon_up, lon_down, up, down)
+    image, segs = finish(total[...] + part, values, place)
     lines = [own_lane_sum(here * values), lane_sum([image[g] * group(values, g) for g in range(4)])]
     if again:
         for r in range(3):
@@ -515,8 +553,7 @@
 
 
 def matchings(count):
-    first = [(i, i ^ 1) for i in range(count)]
-    return first, [(i, (((i + 1) ^ 1) - 1) % count) for i in range(count)]
+    return [(i, (((i + 1) ^ 1) - 1) % count) for i in range(count)], [(i, i ^ 1) for i in range(count)]
 
 
 def swap(first, second, axis):
@@ -546,8 +583,8 @@
 LON_MESSAGE, TM_MESSAGE, LAT_MESSAGE = (3, 2, 8, 128), (4, SEG, 128), (8, LANES)
 TILES = (3, 4, SEG, 128)
 VECTOR = (ROWS, LANES)
-SCRATCH = [pltpu.VMEM((4 * BLOCK, 384), jnp.float32)] * 2
-CELLS = (HOURS, LAT_CELLS, LON_CELLS)
+MID_SCRATCH, EDGE_SCRATCH = ([pltpu.VMEM((4 * n, 384), jnp.float32)] * 2 for n in (MID_CELLS, EDGE_CELLS))
+MID, ENDS = ((HOURS, n, LON_CELLS) for n in (MID_CELLS, EDGE_CELLS))
 
 
 def exchange(tiles, first, second):
@@ -592,26 +629,38 @@
     lat_index = (lax.axis_index("lat") * LAT_CELLS + jnp.arange(LAT_CELLS, dtype=jnp.int32)).astype(jnp.float32)
     area = jnp.cos((90.0 - (lat_index + 0.5) * 180.0 / lat_total) * (jnp.pi / 180.0))
     area = jnp.broadcast_to(area[:, None], (LAT_CELLS, LON_CELLS))
-    tabs = tables()
+    mid_tabs, edge_tabs = tables()
     ends = (shaped(*TILES), shaped(*LON_MESSAGE), shaped(*LON_MESSAGE))
     vector = shaped(*VECTOR)
 
-    both = expand(coefficients.transpose(0, 2, 1), inverse_diag.transpose(0, 2, 1))
-    weight, diag, tiles, first, second = call(
-        start_kernel, (shaped(*CELLS), vector, *ends), "start", *both, area, offset, precip, *tabs,
-        scratch=[pltpu.VMEM(CELLS, jnp.float32)] * 2 + SCRATCH + [pltpu.SemaphoreType.DMA((2 * STEPS,))],
-        far=(4, 5), limit=47,
-    )
+    both, *got = expand(coefficients.transpose(0, 2, 1), inverse_diag.transpose(0, 2, 1))
+    weight, total, offset_edges, precip_edges = call(
+        start_middle_kernel, (shaped(*MID), vector, shaped(*ENDS), shaped(*ENDS)), "start_middle",
+        both, middle(area), offset, precip, *mid_tabs,
+        scratch=[pltpu.VMEM(MID, jnp.float32)] * 2 + MID_SCRATCH + [pltpu.SemaphoreType.DMA((2 * CHUNKS + 4,))],
+        far=(2, 3), limit=47,
+    )
+    edge_weight, diag, *sent = call(
+        start_kernel, (shaped(*ENDS), vector, *ends), "start", both, *got, total, edges(area), offset_edges, precip_edges,
+        *edge_tabs, scratch=EDGE_SCRATCH,
+    )
+
+    def hessian(again, rows, got, outs, *more):
+        total, = call(
+            functools.partial(hessian_middle_kernel, again=again), (vector,), "hessian_middle", rows, diag, weight, *mid_tabs,
+            scratch=MID_SCRATCH,
+        )
+        return call(
+            functools.partial(hessian_kernel, again=again), (vector, vector, *outs), "hessian", rows, *got, total, diag,
+            edge_weight, *edge_tabs, *more, scratch=EDGE_SCRATCH,
+        )
+
     lines = shaped(8, 128)
-    residual, scaled, tiles, first, second, sums = call(
-        functools.partial(hessian_kernel, again=False), (vector, vector, *ends, lines), "hessian",
-        *exchange(tiles, first, second), diag, weight, *tabs, scratch=SCRATCH,
-    )
+    rows, *got = exchange(*sent)
+    residual, scaled, *sent, sums = hessian(False, rows, got, (*ends, lines))
     slots = shaped(lax.axis_size("lon") * lax.axis_size("lat"), 16, 128)
-    image, image_scaled, tiles, slots = call(
-        functools.partial(hessian_kernel, again=True), (vector, vector, ends[0], slots), "hessian_again",
-        *exchange(tiles, first, second), diag, weight, *tabs, sums, scratch=SCRATCH,
-    )
+    rows, *got = exchange(*sent)
+    image, image_scaled, tiles, slots = hessian(True, rows, got, (ends[0], slots), sums)
     out = shaped(T_OWN, LON_OWN, LAT_OWN)
     outs = call(
         last_kernel, (out, out), "last", *fold_and_sum(tiles, slots, lines), residual, scaled, image, image_scaled

time: 101 us -> 90.9 us (0.900)
  starting transfers between devices: 31.4 us -> 25.4 us
  waiting for transfers between devices: 31.4 us -> 27.1 us
    ppermute x10, waiting for transfers between devices: 25.1 us -> 5.7 us  [swap(): lax.ppermute(second, axis, second_pairs)]
    ppermute x10, starting transfers between devices: 21.2 us -> 4.07 us  [swap(): lax.ppermute(second, axis, second_pairs)]
    ppermute x10, waiting for transfers between devices: 3.77 us -> 19.5 us  [swap(): lax.ppermute(first, axis, first_pairs)]
    ppermute x10, starting transfers between devices: 9.1 us -> 19.6 us  [swap(): lax.ppermute(first, axis, first_pairs)]
    pallas_call x12 -> x15, Pallas kernels: 17.9 us -> 18.6 us  [call(): pl.pallas_call(kernel, in_specs=[hbm if i in far else vmem for i in range...]
  transfers between devices with their start and end apart: 21 -> 21, of which waited for: 16 -> 11; matrix products, arithmetic and copies ran while one was open for 0% -> 0% of each run, Pallas kernels for 0% -> 14%
where the time goes in v2:
time: 90.9 us; the launch traced here: 90.5 us
  waiting for transfers between devices  27.1 us (30%)
  starting transfers between devices  25.4 us (28%)
  Pallas kernels  18.6 us (20%)
  blocking collectives  16.3 us (18%)
  local copies, waits for them, and re-layouts  2.14 us (2%)
  between operations  0.91 us (1%)
    ppermute x10, starting transfers between devices, swap(): lax.ppermute(first, axis, first_pairs)  19.6 us
    ppermute x10, waiting for transfers between devices, swap(): lax.ppermute(first, axis, first_pairs)  19.5 us
    pallas_call x15, Pallas kernels, call(): pl.pallas_call(kernel, in_specs=[hbm if i in far else vmem for i in range...  18.6 us
    all_to_all x1, blocking collectives, fold_and_sum(): slots = lax.all_to_all(slots, ('lon', 'lat'), 0, 0, tiled=True)  16.3 us
    ppermute x10, waiting for transfers between devices, swap(): lax.ppermute(second, axis, second_pairs)  5.7 us
    ppermute x10, starting transfers between devices, swap(): lax.ppermute(second, axis, second_pairs)  4.07 us
    ppermute x1, waiting for transfers between devices, fold_and_sum(): lax.ppermute(lines, 'tm', [(i, (i + 2) % count) for i in range(count)])  1.89 us
    unnamed x16, local copies, waits for them, and re-layouts  1.84 us
  transfers between devices with their start and end apart: 21, of which 11 were waited for; matrix products, arithmetic and copies ran while one was open for 0% of the time, Pallas kernels for 14%

profile of v2, /device:TPU:0, one launch (start us, length us, event | category | flops | bytes accessed | tf_op | source)
XLA Modules:
  0.0 90.5 jit_solution(15757025788862744752)
XLA Ops:
  0.6 0.9 copy-done.4
  1.5 0.9 copy-done.5
  2.6 5.6 %collective-permute-start = (f32[4,8,128]{2,1,0:T(8,128)S(1)}, f32[4,8,128]{2,1,0:T(8,128)S(1)}, u32[]{:S(2)}, u32[]{:S(2)}) collective-permute-start(f32[4,8,128]{2,1,0:T(8,128)S(1)} %get-tuple-element.49), channel_id=1, source_target_pairs={{0,112},{16,32},{32,16},{48,64},{64,48},{80,96},{96,80},{112,0},{1... | collective-permute-start | bytes 49160 | tf_op jit(solution)/shard_map/ppermute | solution.py:561
  8.4 1.7 %collective-permute-done.got_first = f32[4,8,128]{2,1,0:T(8,128)S(1)} collective-permute-done((f32[4,8,128]{2,1,0:T(8,128)S(1)}, f32[4,8,128]{2,1,0:T(8,128)S(1)}, u32[]{:S(2)}, u32[]{:S(2)}) %collective-permute-start) | collective-permute-done | bytes 16416 | tf_op jit(solution)/shard_map/ppermute | solution.py:561
  10.1 3.4 %collective-permute-done.1.got_second = f32[4,8,128]{2,1,0:T(8,128)S(1)} collective-permute-done((f32[4,8,128]{2,1,0:T(8,128)S(1)}, f32[4,8,128]{2,1,0:T(8,128)S(1)}, u32[]{:S(2)}, u32[]{:S(2)}) %collective-permute-start.1) | collective-permute-done | bytes 16416 | tf_op jit(solution)/shard_map/ppermute | solution.py:561
  13.7 0.8 collective-permute-start.3
  14.6 2.5 %collective-permute-done.2.got_first = f32[2,40,128]{2,1,0:T(8,128)S(1)} collective-permute-done((f32[2,40,128]{2,1,0:T(8,128)S(1)}, f32[2,40,128]{2,1,0:T(8,128)S(1)}, u32[]{:S(2)}, u32[]{:S(2)}) %collective-permute-start.2) | collective-permute-done | bytes 40992 | tf_op jit(solution)/shard_map/ppermute | solution.py:561
  17.4 4.1 %collective-permute-start.4 = (f32[8,512]{1,0:T(8,128)S(1)}, f32[8,512]{1,0:T(8,128)S(1)}, u32[]{:S(2)}, u32[]{:S(2)}) collective-permute-start(f32[8,512]{1,0:T(8,128)S(1)} %get-tuple-element.55), channel_id=1, source_target_pairs={{0,12},{4,8},{8,4},{12,0},{1,13},{5,9},{9,5},{13,1},{2,14},{6,10},... | collective-permute-start | bytes 49160 | tf_op jit(solution)/shard_map/ppermute | solution.py:561
  21.6 5.5 %start_middle.1 = (f32[32,224,128]{2,1,0:T(8,128)S(1)}, f32[80,512]{1,0:T(8,128)S(1)}, f32[32,32,128]{2,1,0:T(8,128)S(1)}, f32[32,32,128]{2,1,0:T(8,128)S(1)}) custom-call(f32[2,80,512]{2,1,0:T(8,128)S(1)} %get-tuple-element.54.both, f32[224,128]{1,0:T(8,128)S(1)} %broadcast_in_dim.10.area, f32[32,256,128]{2,1,0:T(8,128)} %offset_far.1, ...), custom_call_target="tpu_custom_call" | custom-call | flops 1000000000 | bytes 20000000 | tf_op jit(solution)/shard_map/start_middle/pallas_call | solution.py:571
  27.3 1.4 %start.1 = (f32[32,32,128]{2,1,0:T(8,128)S(1)}, f32[80,512]{1,0:T(8,128)S(1)}, f32[3,4,40,128]{3,2,1,0:T(8,128)S(1)}, f32[3,2,8,128]{3,2,1,0:T(8,128)S(1)}, f32[3,2,8,128]{3,2,1,0:T(8,128)S(1)}) custom-call(f32[2,80,512]{2,1,0:T(8,128)S(1)} %get-tuple-element.54.both, f32[8,512]{1,0:T(8,128)S(1)} %collective-permute-done.4.got_first, ...), custom_call_target="tpu_custom_call" | custom-call | flops 1000000000 | bytes 20000000 | tf_op jit(solution)/shard_map/start/pallas_call | solution.py:571
  28.7 2.5 %collective-permute-start.6 = (f32[3,2,8,128]{3,2,1,0:T(8,128)S(1)}, f32[3,2,8,128]{3,2,1,0:T(8,128)S(1)}, u32[]{:S(2)}, u32[]{:S(2)}) collective-permute-start(f32[3,2,8,128]{3,2,1,0:T(8,128)S(1)} %get-tuple-element.61), channel_id=1, source_target_pairs={{0,112},{16,32},{32,16},{48,64},{64,48},{80,96},{96,80},{112,0},{1... | collective-permute-start | bytes 73736 | tf_op jit(solution)/shard_map/ppermute | solution.py:561
  31.2 5.0 %collective-permute-done.6.got_first = f32[3,2,8,128]{3,2,1,0:T(8,128)S(1)} collective-permute-done((f32[3,2,8,128]{3,2,1,0:T(8,128)S(1)}, f32[3,2,8,128]{3,2,1,0:T(8,128)S(1)}, u32[]{:S(2)}, u32[]{:S(2)}) %collective-permute-start.6) | collective-permute-done | bytes 24608 | tf_op jit(solution)/shard_map/ppermute | solution.py:561
  36.6 0.8 collective-permute-start.9
  37.5 3.2 %collective-permute-done.8.got_first = f32[4,40,128]{2,1,0:T(8,128)S(1)} collective-permute-done((f32[4,40,128]{2,1,0:T(8,128)S(1)}, f32[4,40,128]{2,1,0:T(8,128)S(1)}, u32[]{:S(2)}, u32[]{:S(2)}) %collective-permute-start.8) | collective-permute-done | bytes 81952 | tf_op jit(solution)/shard_map/ppermute | solution.py:561
  40.8 0.6 collective-permute-start.10
  41.4 1.6 %collective-permute-start.11 = (f32[8,512]{1,0:T(8,128)S(1)}, f32[8,512]{1,0:T(8,128)S(1)}, u32[]{:S(2)}, u32[]{:S(2)}) collective-permute-start(f32[8,512]{1,0:T(8,128)S(1)} %get-tuple-element.68), channel_id=1, source_target_pairs={{0,4},{4,0},{8,12},{12,8},{1,5},{5,1},{9,13},{13,9},{2,6},{6,2},{1... | collective-permute-start | bytes 49160 | tf_op jit(solution)/shard_map/ppermute | solution.py:561
  43.0 3.4 %hessian_middle.2.total = f32[80,512]{1,0:T(8,128)S(1)} custom-call(f32[80,512]{1,0:T(8,128)S(1)} %get-tuple-element.66.partial_rows, f32[80,512]{1,0:T(8,128)S(1)} %get-tuple-element.69.diag, f32[32,224,128]{2,1,0:T(8,128)S(1)} %get-tuple-element.70.weight, bf16[224,240]{1,0:T(8,128)(2,1)S(1)} %copy-done.3, bf16[80,672]{1,0:T(8,128)(2,1)S(1)} %copy-done.2, ...), custom_call_target="tpu_custom_call" | custom-call | flops 1000000000 | bytes 20000000 | tf_op jit(solution)/shard_map/hessian_middle/pallas_call | solution.py:571
  46.4 1.3 %hessian.2 = (f32[80,512]{1,0:T(8,128)S(1)}, f32[80,512]{1,0:T(8,128)S(1)}, f32[3,4,40,128]{3,2,1,0:T(8,128)S(1)}, f32[3,2,8,128]{3,2,1,0:T(8,128)S(1)}, f32[3,2...) custom-call(f32[80,512]{1,0:T(8,128)S(1)} %get-tuple-element.66.partial_rows, ...), custom_call_target="tpu_custom_call" | custom-call | flops 1000000000 | bytes 20000000 | tf_op jit(solution)/shard_map/hessian/pallas_call | solution.py:571
  47.7 3.9 %collective-permute-start.12 = (f32[3,2,8,128]{3,2,1,0:T(8,128)S(1)}, f32[3,2,8,128]{3,2,1,0:T(8,128)S(1)}, u32[]{:S(2)}, u32[]{:S(2)}) collective-permute-start(f32[3,2,8,128]{3,2,1,0:T(8,128)S(1)} %get-tuple-element.73), channel_id=1, source_target_pairs={{0,112},{16,32},{32,16},{48,64},{64,48},{80,96},{96,80},{112,0},{1... | collective-permute-start | bytes 73736 | tf_op jit(solution)/shard_map/ppermute | solution.py:561
  51.5 3.7 %collective-permute-done.12.got_first = f32[3,2,8,128]{3,2,1,0:T(8,128)S(1)} collective-permute-done((f32[3,2,8,128]{3,2,1,0:T(8,128)S(1)}, f32[3,2,8,128]{3,2,1,0:T(8,128)S(1)}, u32[]{:S(2)}, u32[]{:S(2)}) %collective-permute-start.12) | collective-permute-done | bytes 24608 | tf_op jit(solution)/shard_map/ppermute | solution.py:561
  55.2 1.7 %collective-permute-done.13.got_second = f32[3,2,8,128]{3,2,1,0:T(8,128)S(1)} collective-permute-done((f32[3,2,8,128]{3,2,1,0:T(8,128)S(1)}, f32[3,2,8,128]{3,2,1,0:T(8,128)S(1)}, u32[]{:S(2)}, u32[]{:S(2)}) %collective-permute-start.13) | collective-permute-done | bytes 24608 | tf_op jit(solution)/shard_map/ppermute | solution.py:561
  57.0 0.4 collective-permute-start.15
  57.4 3.4 %collective-permute-done.14.got_first = f32[4,40,128]{2,1,0:T(8,128)S(1)} collective-permute-done((f32[4,40,128]{2,1,0:T(8,128)S(1)}, f32[4,40,128]{2,1,0:T(8,128)S(1)}, u32[]{:S(2)}, u32[]{:S(2)}) %collective-permute-start.14) | collective-permute-done | bytes 81952 | tf_op jit(solution)/shard_map/ppermute | solution.py:561
  61.0 2.6 %collective-permute-start.16 = (f32[8,512]{1,0:T(8,128)S(1)}, f32[8,512]{1,0:T(8,128)S(1)}, u32[]{:S(2)}, u32[]{:S(2)}) collective-permute-start(f32[8,512]{1,0:T(8,128)S(1)} %get-tuple-element.79), channel_id=1, source_target_pairs={{0,12},{4,8},{8,4},{12,0},{1,13},{5,9},{9,5},{13,1},{2,14},{6,10},... | collective-permute-start | bytes 49160 | tf_op jit(solution)/shard_map/ppermute | solution.py:561
  63.6 3.4 %hessian_middle.3.total = f32[80,512]{1,0:T(8,128)S(1)} custom-call(f32[80,512]{1,0:T(8,128)S(1)} %get-tuple-element.78.partial_rows, f32[80,512]{1,0:T(8,128)S(1)} %get-tuple-element.69.diag, f32[32,224,128]{2,1,0:T(8,128)S(1)} %get-tuple-element.70.weight, bf16[224,240]{1,0:T(8,128)(2,1)S(1)} %copy-done.3, bf16[80,672]{1,0:T(8,128)(2,1)S(1)} %copy-done.2, ...), custom_call_target="tpu_custom_call" | custom-call | flops 1000000000 | bytes 20000000 | tf_op jit(solution)/shard_map/hessian_middle/pallas_call | solution.py:571
  67.0 0.3 collective-permute-done.17.got_second
  67.3 1.3 %hessian.3 = (f32[80,512]{1,0:T(8,128)S(1)}, f32[80,512]{1,0:T(8,128)S(1)}, f32[3,4,40,128]{3,2,1,0:T(8,128)S(1)}, f32[32,16,128]{2,1,0:T(8,128)S(1)}) custom-call(f32[80,512]{1,0:T(8,128)S(1)} %get-tuple-element.78.partial_rows, f32[8,512]{1,0:T(8,128)S(1)} %collective-permute-done.16.got_first, f32[8,512]{1,0:T(8,128)S(1)} %collective-permute-done.17.got_second, ...), custom_call_target="tpu_custom_call" | custom-call | flops 1000000000 | bytes 20000000 | tf_op jit(solution)/shard_map/hessian/pallas_call | solution.py:571
  68.7 16.3 %all_to_all.5.slots = f32[32,16,128]{2,1,0:T(8,128)S(1)} all-to-all(f32[32,16,128]{2,1,0:T(8,128)S(1)} %get-tuple-element.83), channel_id=1, replica_groups=mesh['lon'=8,'lat'=4,'tm'=4] {'lon','lat'}, dimensions={0} | all-to-all | bytes 524288 | tf_op jit(solution)/shard_map/all_to_all | solution.py:603
  85.4 0.4 collective-permute-start.19
  85.8 1.7 %collective-permute-start.20 = (f32[8,128]{1,0:T(8,128)S(1)}, f32[8,128]{1,0:T(8,128)S(1)}, u32[]{:S(2)}, u32[]{:S(2)}) collective-permute-start(f32[8,128]{1,0:T(8,128)S(1)} %get-tuple-element.87.lines), channel_id=1, source_target_pairs={{0,2},{1,3},{2,0},{3,1},{4,6},{5,7},{6,4},{7,5},{8,10},{9,11},{10,... | collective-permute-start | bytes 12296 | tf_op jit(solution)/shard_map/ppermute | solution.py:610
  87.5 1.9 %collective-permute-done.20.got_lines = f32[8,128]{1,0:T(8,128)S(1)} collective-permute-done((f32[8,128]{1,0:T(8,128)S(1)}, f32[8,128]{1,0:T(8,128)S(1)}, u32[]{:S(2)}, u32[]{:S(2)}) %collective-permute-start.20) | collective-permute-done | bytes 4128 | tf_op jit(solution)/shard_map/ppermute | solution.py:610
  89.4 1.2 %last.1 = (f32[8,32,64]{2,1,0:T(8,128)}, f32[8,32,64]{2,1,0:T(8,128)}) custom-call(f32[3,4,40,128]{3,2,1,0:T(8,128)S(1)} %get-tuple-element.84.tiles, f32[40,128]{1,0:T(8,128)S(1)} %collective-permute-done.18.got_first, f32[40,128]{1,0:T(8,128)S(1)} %collective-permute-done.19.got_second, f32[8,128]{1,0:T(8,128)S(1)} %get-tuple-element.87.lines, ...), custom_call_target="tpu_custom_call" | custom-call | flops 1000000000 | bytes 20000000 | tf_op jit(solution)/shard_map/last/pallas_call | solution.py:571
  (48 shorter events, 2.2 us)
Async XLA Ops:
  0.6 0.9 copy-start.4
  1.5 0.9 copy-start.5
  2.6 19.0 %copy-start = (bf16[384,384]{1,0:T(8,128)(2,1)S(1)}, bf16[384,384]{1,0:T(8,128)(2,1)}, u32[]{:S(2)}) copy-start(bf16[384,384]{1,0:T(8,128)(2,1)} %constant.38.lon_up) | copy-start | bytes 884740
  2.6 19.0 %copy-start.1 = (bf16[384,256]{1,0:T(8,128)(2,1)S(1)}, bf16[384,256]{1,0:T(8,128)(2,1)}, u32[]{:S(2)}) copy-start(bf16[384,256]{1,0:T(8,128)(2,1)} %constant.41.lon_down) | copy-start | bytes 589828
  2.6 19.0 %copy-start.2 = (bf16[80,672]{1,0:T(8,128)(2,1)S(1)}, bf16[80,672]{1,0:T(8,128)(2,1)}, u32[]{:S(2)}) copy-start(bf16[80,672]{1,0:T(8,128)(2,1)} %constant.33.lat_down) | copy-start | bytes 322564
  2.6 19.0 %copy-start.3 = (bf16[224,240]{1,0:T(8,128)(2,1)S(1)}, bf16[224,240]{1,0:T(8,128)(2,1)}, u32[]{:S(2)}) copy-start(bf16[224,240]{1,0:T(8,128)(2,1)} %constant.30.lat_up) | copy-start | bytes 322564
  2.6 7.4 %collective-permute-start = (f32[4,8,128]{2,1,0:T(8,128)S(1)}, f32[4,8,128]{2,1,0:T(8,128)S(1)}, u32[]{:S(2)}, u32[]{:S(2)}) collective-permute-start(f32[4,8,128]{2,1,0:T(8,128)S(1)} %get-tuple-element.49), channel_id=1, source_target_pairs={{0,112},{16,32},{32,16},{48,64},{64,48},{80,96},{96,80},{112,0},{1... | collective-permute-start | bytes 49160 | tf_op jit(solution)/shard_map/ppermute | solution.py:561
  8.2 5.2 %collective-permute-start.1 = (f32[4,8,128]{2,1,0:T(8,128)S(1)}, f32[4,8,128]{2,1,0:T(8,128)S(1)}, u32[]{:S(2)}, u32[]{:S(2)}) collective-permute-start(f32[4,8,128]{2,1,0:T(8,128)S(1)} %get-tuple-element.50), channel_id=1, source_target_pairs={{0,16},{16,0},{32,48},{48,32},{64,80},{80,64},{96,112},{112,96},{1... | collective-permute-start | bytes 49160 | tf_op jit(solution)/shard_map/ppermute | solution.py:561
  13.6 3.5 %collective-permute-start.2 = (f32[2,40,128]{2,1,0:T(8,128)S(1)}, f32[2,40,128]{2,1,0:T(8,128)S(1)}, u32[]{:S(2)}, u32[]{:S(2)}) collective-permute-start(f32[2,40,128]{2,1,0:T(8,128)S(1)} %get-tuple-element.52), channel_id=1, source_target_pairs={{0,3},{1,2},{2,1},{3,0},{4,7},{5,6},{6,5},{7,4},{8,11},{9,10},{10,... | collective-permute-start | bytes 122888 | tf_op jit(solution)/shard_map/ppermute | solution.py:561
  13.7 3.4 %collective-permute-start.3 = (f32[2,40,128]{2,1,0:T(8,128)S(1)}, f32[2,40,128]{2,1,0:T(8,128)S(1)}, u32[]{:S(2)}, u32[]{:S(2)}) collective-permute-start(f32[2,40,128]{2,1,0:T(8,128)S(1)} %get-tuple-element.53), channel_id=1, source_target_pairs={{0,1},{1,0},{2,3},{3,2},{4,5},{5,4},{6,7},{7,6},{8,9},{9,8},{10,11... | collective-permute-start | bytes 122888 | tf_op jit(solution)/shard_map/ppermute | solution.py:561
  17.4 9.8 %collective-permute-start.4 = (f32[8,512]{1,0:T(8,128)S(1)}, f32[8,512]{1,0:T(8,128)S(1)}, u32[]{:S(2)}, u32[]{:S(2)}) collective-permute-start(f32[8,512]{1,0:T(8,128)S(1)} %get-tuple-element.55), channel_id=1, source_target_pairs={{0,12},{4,8},{8,4},{12,0},{1,13},{5,9},{9,5},{13,1},{2,14},{6,10},... | collective-permute-start | bytes 49160 | tf_op jit(solution)/shard_map/ppermute | solution.py:561
  21.5 5.7 %collective-permute-start.5 = (f32[8,512]{1,0:T(8,128)S(1)}, f32[8,512]{1,0:T(8,128)S(1)}, u32[]{:S(2)}, u32[]{:S(2)}) collective-permute-start(f32[8,512]{1,0:T(8,128)S(1)} %get-tuple-element.56), channel_id=1, source_target_pairs={{0,4},{4,0},{8,12},{12,8},{1,5},{5,1},{9,13},{13,9},{2,6},{6,2},{1... | collective-permute-start | bytes 49160 | tf_op jit(solution)/shard_map/ppermute | solution.py:561
  21.6 5.7 %copy-start.6 = (bf16[80,96]{1,0:T(8,128)(2,1)S(1)}, bf16[80,96]{1,0:T(8,128)(2,1)}, u32[]{:S(2)}) copy-start(bf16[80,96]{1,0:T(8,128)(2,1)} %constant.51.lat_down) | copy-start | bytes 46084
  21.6 5.7 %copy-start.7 = (bf16[32,240]{1,0:T(8,128)(2,1)S(1)}, bf16[32,240]{1,0:T(8,128)(2,1)}, u32[]{:S(2)}) copy-start(bf16[32,240]{1,0:T(8,128)(2,1)} %constant.48.lat_up) | copy-start | bytes 46084
  28.7 7.5 %collective-permute-start.6 = (f32[3,2,8,128]{3,2,1,0:T(8,128)S(1)}, f32[3,2,8,128]{3,2,1,0:T(8,128)S(1)}, u32[]{:S(2)}, u32[]{:S(2)}) collective-permute-start(f32[3,2,8,128]{3,2,1,0:T(8,128)S(1)} %get-tuple-element.61), channel_id=1, source_target_pairs={{0,112},{16,32},{32,16},{48,64},{64,48},{80,96},{96,80},{112,0},{1... | collective-permute-start | bytes 73736 | tf_op jit(solution)/shard_map/ppermute | solution.py:561
  31.2 5.3 %collective-permute-start.7 = (f32[3,2,8,128]{3,2,1,0:T(8,128)S(1)}, f32[3,2,8,128]{3,2,1,0:T(8,128)S(1)}, u32[]{:S(2)}, u32[]{:S(2)}) collective-permute-start(f32[3,2,8,128]{3,2,1,0:T(8,128)S(1)} %get-tuple-element.62), channel_id=1, source_target_pairs={{0,16},{16,0},{32,48},{48,32},{64,80},{80,64},{96,112},{112,96},{1... | collective-permute-start | bytes 73736 | tf_op jit(solution)/shard_map/ppermute | solution.py:561
  36.6 4.1 %collective-permute-start.8 = (f32[4,40,128]{2,1,0:T(8,128)S(1)}, f32[4,40,128]{2,1,0:T(8,128)S(1)}, u32[]{:S(2)}, u32[]{:S(2)}) collective-permute-start(f32[4,40,128]{2,1,0:T(8,128)S(1)} %get-tuple-element.64), channel_id=1, source_target_pairs={{0,3},{1,2},{2,1},{3,0},{4,7},{5,6},{6,5},{7,4},{8,11},{9,10},{10,... | collective-permute-start | bytes 245768 | tf_op jit(solution)/shard_map/ppermute | solution.py:561
  36.6 4.0 %collective-permute-start.9 = (f32[4,40,128]{2,1,0:T(8,128)S(1)}, f32[4,40,128]{2,1,0:T(8,128)S(1)}, u32[]{:S(2)}, u32[]{:S(2)}) collective-permute-start(f32[4,40,128]{2,1,0:T(8,128)S(1)} %get-tuple-element.65), channel_id=1, source_target_pairs={{0,1},{1,0},{2,3},{3,2},{4,5},{5,4},{6,7},{7,6},{8,9},{9,8},{10,11... | collective-permute-start | bytes 245768 | tf_op jit(solution)/shard_map/ppermute | solution.py:561
  40.8 5.6 %collective-permute-start.10 = (f32[8,512]{1,0:T(8,128)S(1)}, f32[8,512]{1,0:T(8,128)S(1)}, u32[]{:S(2)}, u32[]{:S(2)}) collective-permute-start(f32[8,512]{1,0:T(8,128)S(1)} %get-tuple-element.67), channel_id=1, source_target_pairs={{0,12},{4,8},{8,4},{12,0},{1,13},{5,9},{9,5},{13,1},{2,14},{6,10},... | collective-permute-start | bytes 49160 | tf_op jit(solution)/shard_map/ppermute | solution.py:561
  41.4 5.0 %collective-permute-start.11 = (f32[8,512]{1,0:T(8,128)S(1)}, f32[8,512]{1,0:T(8,128)S(1)}, u32[]{:S(2)}, u32[]{:S(2)}) collective-permute-start(f32[8,512]{1,0:T(8,128)S(1)} %get-tuple-element.68), channel_id=1, source_target_pairs={{0,4},{4,0},{8,12},{12,8},{1,5},{5,1},{9,13},{13,9},{2,6},{6,2},{1... | collective-permute-start | bytes 49160 | tf_op jit(solution)/shard_map/ppermute | solution.py:561
  47.7 7.5 %collective-permute-start.12 = (f32[3,2,8,128]{3,2,1,0:T(8,128)S(1)}, f32[3,2,8,128]{3,2,1,0:T(8,128)S(1)}, u32[]{:S(2)}, u32[]{:S(2)}) collective-permute-start(f32[3,2,8,128]{3,2,1,0:T(8,128)S(1)} %get-tuple-element.73), channel_id=1, source_target_pairs={{0,112},{16,32},{32,16},{48,64},{64,48},{80,96},{96,80},{112,0},{1... | collective-permute-start | bytes 73736 | tf_op jit(solution)/shard_map/ppermute | solution.py:561
  51.5 5.3 %collective-permute-start.13 = (f32[3,2,8,128]{3,2,1,0:T(8,128)S(1)}, f32[3,2,8,128]{3,2,1,0:T(8,128)S(1)}, u32[]{:S(2)}, u32[]{:S(2)}) collective-permute-start(f32[3,2,8,128]{3,2,1,0:T(8,128)S(1)} %get-tuple-element.74), channel_id=1, source_target_pairs={{0,16},{16,0},{32,48},{48,32},{64,80},{80,64},{96,112},{112,96},{1... | collective-permute-start | bytes 73736 | tf_op jit(solution)/shard_map/ppermute | solution.py:561
  56.9 3.9 %collective-permute-start.14 = (f32[4,40,128]{2,1,0:T(8,128)S(1)}, f32[4,40,128]{2,1,0:T(8,128)S(1)}, u32[]{:S(2)}, u32[]{:S(2)}) collective-permute-start(f32[4,40,128]{2,1,0:T(8,128)S(1)} %get-tuple-element.76), channel_id=1, source_target_pairs={{0,3},{1,2},{2,1},{3,0},{4,7},{5,6},{6,5},{7,4},{8,11},{9,10},{10,... | collective-permute-start | bytes 245768 | tf_op jit(solution)/shard_map/ppermute | solution.py:561
  57.0 3.9 %collective-permute-start.15 = (f32[4,40,128]{2,1,0:T(8,128)S(1)}, f32[4,40,128]{2,1,0:T(8,128)S(1)}, u32[]{:S(2)}, u32[]{:S(2)}) collective-permute-start(f32[4,40,128]{2,1,0:T(8,128)S(1)} %get-tuple-element.77), channel_id=1, source_target_pairs={{0,1},{1,0},{2,3},{3,2},{4,5},{5,4},{6,7},{7,6},{8,9},{9,8},{10,11... | collective-permute-start | bytes 245768 | tf_op jit(solution)/shard_map/ppermute | solution.py:561
  61.0 6.0 %collective-permute-start.16 = (f32[8,512]{1,0:T(8,128)S(1)}, f32[8,512]{1,0:T(8,128)S(1)}, u32[]{:S(2)}, u32[]{:S(2)}) collective-permute-start(f32[8,512]{1,0:T(8,128)S(1)} %get-tuple-element.79), channel_id=1, source_target_pairs={{0,12},{4,8},{8,4},{12,0},{1,13},{5,9},{9,5},{13,1},{2,14},{6,10},... | collective-permute-start | bytes 49160 | tf_op jit(solution)/shard_map/ppermute | solution.py:561
  63.6 3.7 %collective-permute-start.17 = (f32[8,512]{1,0:T(8,128)S(1)}, f32[8,512]{1,0:T(8,128)S(1)}, u32[]{:S(2)}, u32[]{:S(2)}) collective-permute-start(f32[8,512]{1,0:T(8,128)S(1)} %get-tuple-element.80), channel_id=1, source_target_pairs={{0,4},{4,0},{8,12},{12,8},{1,5},{5,1},{9,13},{13,9},{2,6},{6,2},{1... | collective-permute-start | bytes 49160 | tf_op jit(solution)/shard_map/ppermute | solution.py:561
  85.3 4.1 %collective-permute-start.18 = (f32[40,128]{1,0:T(8,128)S(1)}, f32[40,128]{1,0:T(8,128)S(1)}, u32[]{:S(2)}, u32[]{:S(2)}) collective-permute-start(f32[40,128]{1,0:T(8,128)S(1)} %get-tuple-element.85), channel_id=1, source_target_pairs={{0,3},{1,2},{2,1},{3,0},{4,7},{5,6},{6,5},{7,4},{8,11},{9,10},{10,... | collective-permute-start | bytes 61448 | tf_op jit(solution)/shard_map/ppermute | solution.py:561
  85.4 4.0 %collective-permute-start.19 = (f32[40,128]{1,0:T(8,128)S(1)}, f32[40,128]{1,0:T(8,128)S(1)}, u32[]{:S(2)}, u32[]{:S(2)}) collective-permute-start(f32[40,128]{1,0:T(8,128)S(1)} %get-tuple-element.86), channel_id=1, source_target_pairs={{0,1},{1,0},{2,3},{3,2},{4,5},{5,4},{6,7},{7,6},{8,9},{9,8},{10,11... | collective-permute-start | bytes 61448 | tf_op jit(solution)/shard_map/ppermute | solution.py:561
  85.8 3.6 %collective-permute-start.20 = (f32[8,128]{1,0:T(8,128)S(1)}, f32[8,128]{1,0:T(8,128)S(1)}, u32[]{:S(2)}, u32[]{:S(2)}) collective-permute-start(f32[8,128]{1,0:T(8,128)S(1)} %get-tuple-element.87.lines), channel_id=1, source_target_pairs={{0,2},{1,3},{2,0},{3,1},{4,6},{5,7},{6,4},{7,5},{8,10},{9,11},{10,... | collective-permute-start | bytes 12296 | tf_op jit(solution)/shard_map/ppermute | solution.py:610

commit v3 on v2

--- a/solution.py
+++ b/solution.py
@@ -14,9 +14,8 @@
 
 ROWS, LANES, SEG, LAT_OWN, LON_OWN, T_OWN = 80, 512, 40, 64, 32, 8
 HOURS, LAT_CELLS, LON_CELLS = 32, 256, 128
-EDGE, CHUNK = 16, 32
+EDGE, CHUNK = 16, 112
 MID_CELLS, EDGE_CELLS = LAT_CELLS - 2 * EDGE, 2 * EDGE
-CHUNKS = MID_CELLS // CHUNK
 
 
 def spline(offsets):
@@ -54,7 +53,9 @@
     lat_tables = []
     for part in (middle, edges):
         up = jnp.concatenate([part(high), part(low), part(high)], axis=1)
-        lat_tables += [up, jnp.concatenate([part(high).T, part(low).T, part(high).T], axis=1)]
+        cells = CHUNK if part is middle else EDGE_CELLS
+        down = [p.reshape(-1, cells, ROWS).transpose(0, 2, 1) for p in (part(high), part(low))]
+        lat_tables += [up, jnp.concatenate([down[0], down[1], down[0]], axis=2)]
     lon = np.zeros((128, 3 * LON_CELLS))
     for r in range(3):
         lon[r * SEG : r * SEG + LON_OWN + 4, r * LON_CELLS : (r + 1) * LON_CELLS] = table(LON_CELLS, LON_OWN).T
@@ -164,66 +165,78 @@
     )
 
 
-def apply_cells(values, w_of, lat_up, lat_down, lon_up, lon_down, up, down, before_chunk=None):
-    outer, inner = hour_factors()
-    cells = lat_up.shape[0]
-    high, low = split(values)
-    expanded = dot(lat_up[...], jnp.concatenate([high, high, low], axis=0))
+def expand_cells(parts, lat_up, lon_up, up):
+    expanded = dot(lat_up, parts)
     high, low = split(jnp.concatenate([group(expanded, g) for g in range(4)], axis=0))
     up[...] = dot(jnp.concatenate([high, low, high], axis=1), lon_up[...])
 
-    def tile(i, carry):
-        start = pl.multiple_of(i * 8, 8)
-        rows = pl.ds(start, 8)
-
-        def knot(t):
-            return up[pl.ds((t % 4) * cells + start, 8), (t // 4) * 128 : (t // 4 + 1) * 128]
-
-        back = [None] * 12
-
-        def add(t, value):
-            back[t] = value if back[t] is None else back[t] + value
-
-        x = [knot(0), knot(1), knot(2), None]
-        for j in range(9):
-            x[3] = knot(j + 3)
-            edge_sum, edge_diff, mid_sum, mid_diff = x[0] + x[3], x[0] - x[3], x[1] + x[2], x[1] - x[2]
-            sides = []
-            for pair, (late, early) in enumerate(((2, 1), (3, 0))):
-                even = outer[2 * pair] * edge_sum + inner[2 * pair] * mid_sum
-                uneven = outer[2 * pair + 1] * edge_diff + inner[2 * pair + 1] * mid_diff
-                below = w_of(4 * (j - 1) + late, rows, even + uneven) if j > 0 else None
-                above = w_of(4 * j + early, rows, even - uneven) if j < 8 else None
-                if below is None:
-                    sides.append((above, -above))
-                elif above is None:
-                    sides.append((below, below))
-                else:
-                    sides.append((below + above, below - above))
-            (both0, differ0), (both1, differ1) = sides
-            edge_even, edge_odd = outer[0] * both0 + outer[2] * both1, outer[1] * differ0 + outer[3] * differ1
-            mid_even, mid_odd = inner[0] * both0 + inner[2] * both1, inner[1] * differ0 + inner[3] * differ1
-            add(j, edge_even + edge_odd)
-            add(j + 1, mid_even + mid_odd)
-            add(j + 2, mid_even - mid_odd)
-            add(j + 3, edge_even - edge_odd)
-            for t in (j,) if j < 8 else (8, 9, 10, 11):
-                down[pl.ds((t % 4) * cells + start, 8), (t // 4) * 128 : (t // 4 + 1) * 128] = back[t]
-            x = [x[1], x[2], x[3], None]
-        return carry
-
-    if before_chunk is None:
-        lax.fori_loop(0, cells // 8, tile, 0)
-    else:
-        for chunk in range(cells // CHUNK):
-            before_chunk(chunk)
-            lax.fori_loop(chunk * CHUNK // 8, (chunk + 1) * CHUNK // 8, tile, 0)
+
+def cells_tile(w_of, first_row, start, cells, up, down):
+    outer, inner = hour_factors()
+    rows = pl.ds(first_row + start, 8)
+
+    def knot(t):
+        return up[pl.ds((t % 4) * cells + start, 8), (t // 4) * 128 : (t // 4 + 1) * 128]
+
+    back = [None] * 12
+
+    def add(t, value):
+        back[t] = value if back[t] is None else back[t] + value
+
+    x = [knot(0), knot(1), knot(2), None]
+    for j in range(9):
+        x[3] = knot(j + 3)
+        edge_sum, edge_diff, mid_sum, mid_diff = x[0] + x[3], x[0] - x[3], x[1] + x[2], x[1] - x[2]
+        sides = []
+        for pair, (late, early) in enumerate(((2, 1), (3, 0))):
+            even = outer[2 * pair] * edge_sum + inner[2 * pair] * mid_sum
+            uneven = outer[2 * pair + 1] * edge_diff + inner[2 * pair + 1] * mid_diff
+            below = w_of(4 * (j - 1) + late, rows, even + uneven) if j > 0 else None
+            above = w_of(4 * j + early, rows, even - uneven) if j < 8 else None
+            if below is None:
+                sides.append((above, -above))
+            elif above is None:
+                sides.append((below, below))
+            else:
+                sides.append((below + above, below - above))
+        (both0, differ0), (both1, differ1) = sides
+        edge_even, edge_odd = outer[0] * both0 + outer[2] * both1, outer[1] * differ0 + outer[3] * differ1
+        mid_even, mid_odd = inner[0] * both0 + inner[2] * both1, inner[1] * differ0 + inner[3] * differ1
+        add(j, edge_even + edge_odd)
+        add(j + 1, mid_even + mid_odd)
+        add(j + 2, mid_even - mid_odd)
+        add(j + 3, edge_even - edge_odd)
+        for t in (j,) if j < 8 else (8, 9, 10, 11):
+            down[pl.ds((t % 4) * cells + start, 8), (t // 4) * 128 : (t // 4 + 1) * 128] = back[t]
+        x = [x[1], x[2], x[3], None]
+
+
+def fold_cells(down, cells, lat_down, lon_down):
     high, low = split(down[...])
     both = dot(high, lon_down[...])
     narrow = both[:, :128] + both[:, 128:] + dot(low, lon_down[:, :128])
     narrow = jnp.concatenate([narrow[g * cells : (g + 1) * cells] for g in range(4)], axis=1)
     high, low = split(narrow)
-    return dot(lat_down[...], jnp.concatenate([high, high, low], axis=0))
+    return dot(lat_down, jnp.concatenate([high, high, low], axis=0))
+
+
+def apply_cells(values, w_of, lat_up, lat_down, lon_up, lon_down, *scratch):
+    high, low = split(values)
+    parts = jnp.concatenate([high, high, low], axis=0)
+    chunks, _, _ = lat_down.shape
+    cells = lat_up.shape[0] // chunks
+    buffers = scratch[:2], scratch[2:]
+    expand_cells(parts, lat_up[0:cells], lon_up, buffers[0][0])
+    total = None
+    for chunk in range(chunks):
+        up, down = buffers[chunk % 2]
+        if chunk + 1 < chunks:
+            expand_cells(parts, lat_up[(chunk + 1) * cells : (chunk + 2) * cells], lon_up, buffers[(chunk + 1) % 2][0])
+        for start in range(0, cells, 8):
+            cells_tile(w_of, chunk * cells, start, cells, up, down)
+        part = fold_cells(down, cells, lat_down[chunk], lon_down)
+        total = part if total is None else total + part
+    return total
 
 
 def finish(total, values, place):
@@ -257,35 +270,30 @@
     return w_of
 
 
-def start_middle_kernel(both, area, offset_far, precip_far, lat_up, lat_down, lon_up, lon_down,
-                        weight, total, offset_edges, precip_edges, offset, precip, up, down, arrived):
+def load_kernel(_, offset_far, precip_far, offset, precip, offset_edges, precip_edges, arrived):
     copies = []
 
     def bring(source, source_at, target, target_at, count):
         source, target = source.at[:, pl.ds(source_at, count), :], target.at[:, pl.ds(target_at, count), :]
         copies.append(pltpu.make_async_copy(source, target, arrived.at[len(copies)]))
 
-    for chunk in range(CHUNKS):
-        for source, target in ((offset_far, offset), (precip_far, precip)):
-            bring(source, EDGE + chunk * CHUNK, target, chunk * CHUNK, CHUNK)
-    for source, target in ((offset_far, offset_edges), (precip_far, precip_edges)):
-        bring(source, 0, target, 0, EDGE)
-        bring(source, LAT_CELLS - EDGE, target, EDGE, EDGE)
+    for source, target, ends in ((offset_far, offset, offset_edges), (precip_far, precip, precip_edges)):
+        bring(source, EDGE, target, 0, MID_CELLS)
+        bring(source, 0, ends, 0, EDGE)
+        bring(source, LAT_CELLS - EDGE, ends, EDGE, EDGE)
     for copy in copies:
         copy.start()
-
-    def before_chunk(chunk):
-        for copy in copies[2 * chunk : 2 * chunk + 2]:
-            copy.wait()
-
+    for copy in copies:
+        copy.wait()
+
+
+def start_middle_kernel(both, area, offset, precip, lat_up, lat_down, lon_up, lon_down, weight, total, *scratch):
     w_of = start_of(area, offset, precip, weight)
-    total[...] = apply_cells(both[0], w_of, lat_up, lat_down, lon_up, lon_down, up, down, before_chunk)
-    for copy in copies[2 * CHUNKS :]:
-        copy.wait()
+    total[...] = apply_cells(both[0], w_of, lat_up, lat_down, lon_up, lon_down, *scratch)
 
 
 def start_kernel(both, got_first, got_second, total, area, offset, precip, lat_up, lat_down, lon_up, lon_down,
-                 weight, diag, tiles, first, second, up, down):
+                 weight, diag, tiles, first, second, *scratch):
     place = Place()
     row = lax.broadcasted_iota(jnp.int32, (8, LANES), 0)
     left, right = place.received("lat", got_first[...], got_second[...])
@@ -297,7 +305,7 @@
     values = with_halo(both[0], left, right)
     diag[...] = with_halo(both[1], pltpu.roll(left, 6, 0), pltpu.roll(right, 6, 0))
     w_of = start_of(area, offset, precip, weight)
-    part = apply_cells(values, w_of, lat_up, lat_down, lon_up, lon_down, up, down)
+    part = apply_cells(values, w_of, lat_up, lat_down, lon_up, lon_down, *scratch)
     _, segs = finish(total[...] + part, values, place)
     write_ends(segs, place, tiles, first, second)
 
@@ -306,23 +314,23 @@
     return lambda hour, rows, value: weight[hour, rows, :] * value
 
 
-def hessian_middle_kernel(partial_rows, diag, weight, lat_up, lat_down, lon_up, lon_down, total, up, down, *, again):
+def hessian_middle_kernel(partial_rows, diag, weight, lat_up, lat_down, lon_up, lon_down, total, *scratch, again):
     here = partial_rows[...] if again else -partial_rows[...]
-    total[...] = apply_cells(diag[...] * here, weigh(weight), lat_up, lat_down, lon_up, lon_down, up, down)
+    total[...] = apply_cells(diag[...] * here, weigh(weight), lat_up, lat_down, lon_up, lon_down, *scratch)
 
 
 def hessian_kernel(partial_rows, got_first, got_second, total, diag, weight, lat_up, lat_down, lon_up, lon_down, *refs, again):
     if again:
-        before, residual, scaled, tiles, slots, up, down = refs
+        before, residual, scaled, tiles, slots, *scratch = refs
     else:
-        residual, scaled, tiles, first, second, sums, up, down = refs
+        residual, scaled, tiles, first, second, sums, *scratch = refs
     place = Place()
     merged = merge_rows(partial_rows[...], got_first[...], got_second[...], place)
     here = merged if again else -merged
     residual[...] = here
     values = diag[...] * here
     scaled[...] = values
-    part = apply_cells(values, weigh(weight), lat_up, lat_down, lon_up, lon_down, up, down)
+    part = apply_cells(values, weigh(weight), lat_up, lat_down, lon_up, lon_down, *scratch)
     image, segs = finish(total[...] + part, values, place)
     lines = [own_lane_sum(here * values), lane_sum([image[g] * group(values, g) for g in range(4)])]
     if again:
@@ -435,8 +443,16 @@
             joined[r, g, 0:8] = tiles[r, g, 0:8] + jnp.where(lower, left, 0.0)
             joined[r, g, 8:32] = tiles[r, g, 8:32]
             joined[r, g, 32:40] = tiles[r, g, 32:40] + jnp.where(lower, right, 0.0)
-    for g in range(4):
-        first[g], second[g] = place.messages("tm", joined[0, g], joined[2, g])
+    lane = lax.broadcasted_iota(jnp.int32, (SEG, 128), 1)
+
+    def packed(r):
+        rest = pltpu.roll(joined[r, 0], 64, 1)
+        for g in range(1, 4):
+            rest = jnp.where(lane < 4 * g, rest, pltpu.roll(joined[r, g], 64 + 4 * g, 1))
+        return [jnp.where(lane < 64, joined[r, g], pltpu.roll(joined[r, g + 1], 64, 1)) for g in (0, 2)] + [rest]
+
+    for i, (low_side, high_side) in enumerate(zip(packed(0), packed(2))):
+        first[i], second[i] = place.messages("tm", low_side, high_side)
 
 
 def turned_rows(tiles, g, left=0.0, right=0.0):
@@ -446,21 +462,29 @@
 
 def turn_kernel(tiles, got_first, got_second, rows, first, second):
     place = Place()
+    lane = lax.broadcasted_iota(jnp.int32, (SEG, 128), 1)
+    sides = [place.received("tm", got_first[i], got_second[i]) for i in range(3)]
+
+    def unpacked(g, side):
+        main = rolled(sides[g // 2][side], -64 * (g % 2), 1)
+        rest = rolled(sides[2][side], 64 - 4 * g, 1)
+        return jnp.where(lane < 64, main, jnp.where(lane < LAT_OWN + 4, rest, 0.0))
+
     for g in range(4):
-        block = turned_rows(tiles, g, *place.received("tm", got_first[g], got_second[g]))
+        block = turned_rows(tiles, g, unpacked(g, 0), unpacked(g, 1))
         lanes = slice(g * 128, (g + 1) * 128)
         rows[:, lanes] = block[:ROWS]
         first[:, lanes], second[:, lanes] = place.messages("lat", block[0:8], block[64:72])
 
 
-def embed_kernel(coefficients, inverse_diag, tiles, first, second):
+def embed_kernel(own_both, tiles, first, second):
     place = Place()
     pair = lax.broadcasted_iota(jnp.int32, (8, 128), 0) // 2
     heads, tails = [None] * 4, [None] * 4
     for t in range(12):
-        for k, values in enumerate((coefficients, inverse_diag)):
+        for k in range(2):
             if 2 <= t < T_OWN + 2:
-                own = jnp.concatenate([values[t - 2], jnp.zeros((LON_OWN, 128 - LAT_OWN), jnp.float32)], axis=1)
+                own = jnp.concatenate([own_both[k, t - 2], jnp.zeros((LON_OWN, 128 - LAT_OWN), jnp.float32)], axis=1)
                 own = jnp.concatenate([own, jnp.zeros((SEG - LON_OWN, 128), jnp.float32)], axis=0)
                 seg = pltpu.roll(pltpu.roll(own, 2, 0), 2, 1)
                 at, tile = 2 * (t % 2) + k, (t - 2) // 2
@@ -474,7 +498,7 @@
         first[tile], second[tile] = place.messages("lon", heads[tile], tails[tile])
 
 
-def embed_join_kernel(tiles, got_first, got_second, joined, first, second):
+def embed_join_kernel(tiles, got_first, got_second, _, joined, first, second):
     place = Place()
     row = lax.broadcasted_iota(jnp.int32, (8, 128), 0)
     for k in range(2):
@@ -520,18 +544,19 @@
         first[:, lanes], second[:, lanes] = place.messages("lat", head, tail)
 
 
+def ready_kernel(_, *refs):
+    for source, target in zip(refs[:4], refs[4:]):
+        for g in range(4):
+            turned = jnp.concatenate([source[:, g * 128 : (g + 1) * 128], jnp.zeros((128 - ROWS, 128), jnp.float32)], axis=0).T
+            turned = pltpu.roll(turned, 126, 1)
+            for r in range(3):
+                t = 4 * r + g - 2
+                if 0 <= t < T_OWN:
+                    target[t] = pltpu.roll(turned[r * SEG : (r + 1) * SEG], SEG - 2, 0)[:LON_OWN]
+
+
 def last_kernel(tiles, got_first, got_second, lines, got_lines, residual, scaled, image, image_scaled, step_out, residual_out):
     place = Place()
-    left, right = place.received("tm", got_first[...], got_second[...])
-    lane = lax.broadcasted_iota(jnp.int32, (SEG, 128), 1)
-    own = within(lane, LAT_OWN)
-    merged = []
-    for g in range(4):
-        side = right if g < 2 else left
-        side = jnp.where(own, pltpu.roll(side, 66 if g % 2 else 2, 1), 0.0)
-        block = turned_rows(tiles, g, right=side) if g < 2 else turned_rows(tiles, g, left=side)
-        merged.append(block[:ROWS])
-    merged = jnp.concatenate(merged, axis=1)
     total = lines[...] + got_lines[...] + got_first[32:40] + got_second[32:40]
     norm, curvature, image_norm, image_curvature = (jnp.sum(total[i : i + 1], axis=1, keepdims=True) for i in range(4, 8))
     step_size = norm / curvature
@@ -539,17 +564,16 @@
     ratio = next_norm / norm
     next_curvature = curvature - 2.0 * step_size * image_norm + step_size * step_size * image_curvature
     step_next = next_norm / (next_curvature - ratio * next_norm / step_size)
-    direction = scaled[...] - step_size * image_scaled[...] + ratio * scaled[...]
-    newton = step_size * scaled[...] + step_next * direction
-    left_over = residual[...] - step_size * image[...] - step_next * (image[...] - step_size * merged + ratio * image[...])
-    for values, out in ((newton, step_out), (left_over, residual_out)):
-        for g in range(4):
-            turned = jnp.concatenate([group(values, g), jnp.zeros((128 - ROWS, 128), jnp.float32)], axis=0).T
-            turned = pltpu.roll(turned, 126, 1)
-            for r in range(3):
-                t = 4 * r + g - 2
-                if 0 <= t < T_OWN:
-                    out[t] = pltpu.roll(turned[r * SEG : (r + 1) * SEG], SEG - 2, 0)[:LON_OWN, :LAT_OWN]
+    left, right = place.received("tm", got_first[...], got_second[...])
+    for t in range(T_OWN):
+        merged = pltpu.roll(tiles[(t + 2) // 4, (t + 2) % 4], 126, 1)
+        if t in (0, 1, T_OWN - 2, T_OWN - 1):
+            merged = merged + rolled(left if t < 2 else right, 64 * (t % 2), 1)
+        merged = pltpu.roll(merged, SEG - 2, 0)[:LON_OWN]
+        s, y = scaled[t], image[t]
+        step_out[t] = (step_size * s + step_next * (s - step_size * image_scaled[t] + ratio * s))[:, :LAT_OWN]
+        left_over = residual[t] - step_size * y - step_next * (y - step_size * merged + ratio * y)
+        residual_out[t] = left_over[:, :LAT_OWN]
 
 
 def matchings(count):
@@ -574,16 +598,17 @@
         out_specs=[vmem] * len(out_shape),
         out_shape=out_shape,
         scratch_shapes=scratch,
-        compiler_params=pltpu.CompilerParams(vmem_limit_bytes=limit * 1024 * 1024),
+        compiler_params=pltpu.CompilerParams(vmem_limit_bytes=int(limit * 1024) * 1024),
         cost_estimate=pl.CostEstimate(flops=10**9, bytes_accessed=20 * 10**6, transcendentals=0),
         name=name,
     )(*args)
 
 
-LON_MESSAGE, TM_MESSAGE, LAT_MESSAGE = (3, 2, 8, 128), (4, SEG, 128), (8, LANES)
+LON_MESSAGE, TM_MESSAGE, LAT_MESSAGE = (3, 2, 8, 128), (3, SEG, 128), (8, LANES)
 TILES = (3, 4, SEG, 128)
 VECTOR = (ROWS, LANES)
-MID_SCRATCH, EDGE_SCRATCH = ([pltpu.VMEM((4 * n, 384), jnp.float32)] * 2 for n in (MID_CELLS, EDGE_CELLS))
+MID_SCRATCH, EDGE_SCRATCH = ([pltpu.VMEM((4 * n, 384), jnp.float32)] * m for n, m in ((CHUNK, 4), (EDGE_CELLS, 2)))
+LOAD_LIMIT = 42
 MID, ENDS = ((HOURS, n, LON_CELLS) for n in (MID_CELLS, EDGE_CELLS))
 
 
@@ -610,18 +635,22 @@
     return tiles, first, second, lines, lax.ppermute(lines, "tm", [(i, (i + 2) % count) for i in range(count)])
 
 
-def expand(coefficients, inverse_diag):
+def expand(coefficients, inverse_diag, offset, precip):
     tiles, message = shaped(2, *TILES), shaped(4, 8, 128)
     tiles_here, first, second = call(
-        embed_kernel, (tiles, message, message), "embed", coefficients, inverse_diag
+        embed_kernel, (tiles, message, message), "embed", jnp.stack([coefficients, inverse_diag])
+    )
+    cells = call(
+        load_kernel, (shaped(*MID), shaped(*MID), shaped(*ENDS), shaped(*ENDS)), "load", first, offset, precip,
+        scratch=[pltpu.SemaphoreType.DMA((6,))], far=(1, 2), limit=LOAD_LIMIT,
     )
     first, second = swap(first, second, "lon")
     message = shaped(2, SEG, 128)
-    tiles_here, first, second = call(embed_join_kernel, (tiles, message, message), "embed_join", tiles_here, first, second)
+    tiles_here, first, second = call(embed_join_kernel, (tiles, message, message), "embed_join", tiles_here, first, second, cells[2])
     first, second = swap(first, second, "tm")
     shapes = (shaped(2, *VECTOR), shaped(*LAT_MESSAGE), shaped(*LAT_MESSAGE))
     both, first, second = call(embed_turn_kernel, shapes, "embed_turn", tiles_here, first, second)
-    return both, *swap(first, second, "lat")
+    return both, *swap(first, second, "lat"), cells
 
 
 def per_device(precip, offset, coefficients, inverse_diag):
@@ -633,15 +662,12 @@
     ends = (shaped(*TILES), shaped(*LON_MESSAGE), shaped(*LON_MESSAGE))
     vector = shaped(*VECTOR)
 
-    both, *got = expand(coefficients.transpose(0, 2, 1), inverse_diag.transpose(0, 2, 1))
-    weight, total, offset_edges, precip_edges = call(
-        start_middle_kernel, (shaped(*MID), vector, shaped(*ENDS), shaped(*ENDS)), "start_middle",
-        both, middle(area), offset, precip, *mid_tabs,
-        scratch=[pltpu.VMEM(MID, jnp.float32)] * 2 + MID_SCRATCH + [pltpu.SemaphoreType.DMA((2 * CHUNKS + 4,))],
-        far=(2, 3), limit=47,
+    both, *got, cells = expand(coefficients.transpose(0, 2, 1), inverse_diag.transpose(0, 2, 1), offset, precip)
+    weight, total = call(
+        start_middle_kernel, (shaped(*MID), vector), "start_middle", both, middle(area), *cells[:2], *mid_tabs, scratch=MID_SCRATCH
     )
     edge_weight, diag, *sent = call(
-        start_kernel, (shaped(*ENDS), vector, *ends), "start", both, *got, total, edges(area), offset_edges, precip_edges,
+        start_kernel, (shaped(*ENDS), vector, *ends), "start", both, *got, total, edges(area), *cells[2:],
         *edge_tabs, scratch=EDGE_SCRATCH,
     )
 
@@ -662,9 +688,11 @@
     rows, *got = exchange(*sent)
     image, image_scaled, tiles, slots = hessian(True, rows, got, (ends[0], slots), sums)
     out = shaped(T_OWN, LON_OWN, LAT_OWN)
-    outs = call(
-        last_kernel, (out, out), "last", *fold_and_sum(tiles, slots, lines), residual, scaled, image, image_scaled
-    )
+    folded = fold_and_sum(tiles, slots, lines)
+    ready = call(
+        ready_kernel, (shaped(T_OWN, LON_OWN, 128),) * 4, "ready", folded[3], residual, scaled, image, image_scaled
+    )
+    outs = call(last_kernel, (out, out), "last", *folded, *ready)
     return tuple(v.transpose(0, 2, 1) for v in outs)
 
 

time: 90.9 us -> 86.5 us (0.952)
  waiting for transfers between devices: 27.1 us -> 22.3 us
  local copies, waits for them, and re-layouts: 2.14 us -> 0.33 us
  Pallas kernels: 18.6 us -> 19.6 us
  other arithmetic: 0.13 us -> 1.12 us
    ppermute x10, waiting for transfers between devices: 19.5 us -> 16.6 us  [swap(): lax.ppermute(first, axis, first_pairs)]
    unnamed x16 -> x12, local copies, waits for them, and re-layouts: 1.84 us -> 0.03 us
    ppermute x10, waiting for transfers between devices: 5.7 us -> 4.18 us  [swap(): lax.ppermute(second, axis, second_pairs)]
    ppermute x10, starting transfers between devices: 4.07 us -> 5.22 us  [swap(): lax.ppermute(second, axis, second_pairs)]
    another operation x0 -> x1, other arithmetic: none -> 0.99 us  [expand(): jnp.stack([coefficients, inverse_diag])]
    pallas_call x15 -> x17, Pallas kernels: 18.6 us -> 19.6 us  [call(): pl.pallas_call(kernel, in_specs=[hbm if i in far else vmem for i in range...]
  transfers between devices with their start and end apart: 21 -> 21, of which waited for: 11 -> 10; matrix products, arithmetic and copies ran while one was open for 0% -> 0% of each run, Pallas kernels for 14% -> 16%
where the time goes in v3:
time: 86.5 us; the launch traced here: 86.4 us
  starting transfers between devices  26.2 us (30%)
  waiting for transfers between devices  22.3 us (26%)
  Pallas kernels  19.6 us (23%)
  blocking collectives  15.9 us (18%)
  other arithmetic  1.12 us (1%)
  between operations  0.9 us (1%)
    pallas_call x17, Pallas kernels, call(): pl.pallas_call(kernel, in_specs=[hbm if i in far else vmem for i in range...  19.6 us
    ppermute x10, starting transfers between devices, swap(): lax.ppermute(first, axis, first_pairs)  19.5 us
    ppermute x10, waiting for transfers between devices, swap(): lax.ppermute(first, axis, first_pairs)  16.6 us
    all_to_all x1, blocking collectives, fold_and_sum(): slots = lax.all_to_all(slots, ('lon', 'lat'), 0, 0, tiled=True)  15.9 us
    ppermute x10, starting transfers between devices, swap(): lax.ppermute(second, axis, second_pairs)  5.22 us
    ppermute x10, waiting for transfers between devices, swap(): lax.ppermute(second, axis, second_pairs)  4.18 us
  transfers between devices with their start and end apart: 21, of which 10 were waited for; matrix products, arithmetic and copies ran while one was open for 0% of the time, Pallas kernels for 16%

profile of v3, /device:TPU:0, one launch (start us, length us, event | category | flops | bytes accessed | tf_op | source)
XLA Modules:
  0.0 86.4 jit_solution(5333661302330876908)
XLA Ops:
  0.6 1.0 %pad_maximum_fusion.own_both = f32[2,8,32,64]{3,2,1,0:T(8,128)S(1)} fusion(f32[1,8,32,64]{3,2,1,0:T(8,128)} %bitcast.13, f32[1,8,32,64]{3,2,1,0:T(8,128)} %bitcast.14), kind=kLoop, calls=%fused_computation | loop fusion | flops 32768 | bytes 262144 | tf_op jit(solution)/shard_map/stack | solution.py:641
  1.8 5.6 %collective-permute-start = (f32[4,8,128]{2,1,0:T(8,128)S(1)}, f32[4,8,128]{2,1,0:T(8,128)S(1)}, u32[]{:S(2)}, u32[]{:S(2)}) collective-permute-start(f32[4,8,128]{2,1,0:T(8,128)S(1)} %get-tuple-element.55._), channel_id=1, source_target_pairs={{0,112},{16,32},{32,16},{48,64},{64,48},{80,96},{96,80},{112,0},{1... | collective-permute-start | bytes 49160 | tf_op jit(solution)/shard_map/ppermute | solution.py:585
  7.5 3.4 %load.1 = (f32[32,224,128]{2,1,0:T(8,128)S(1)}, f32[32,224,128]{2,1,0:T(8,128)S(1)}, f32[32,32,128]{2,1,0:T(8,128)S(1)}, f32[32,32,128]{2,1,0:T(8,128)S(1)}) custom-call(f32[4,8,128]{2,1,0:T(8,128)S(1)} %get-tuple-element.55._, f32[32,256,128]{2,1,0:T(8,128)} %offset_far.1, f32[32,256,128]{2,1,0:T(8,128)} %precip_far.1), custom_call_target="tpu_custom_call" | custom-call | flops 1000000000 | bytes 20000000 | tf_op jit(solution)/shard_map/load/pallas_call | solution.py:595
  10.9 1.7 %collective-permute-done.1.got_second = f32[4,8,128]{2,1,0:T(8,128)S(1)} collective-permute-done((f32[4,8,128]{2,1,0:T(8,128)S(1)}, f32[4,8,128]{2,1,0:T(8,128)S(1)}, u32[]{:S(2)}, u32[]{:S(2)}) %collective-permute-start.1) | collective-permute-done | bytes 16416 | tf_op jit(solution)/shard_map/ppermute | solution.py:585
  12.8 0.8 collective-permute-start.3
  13.8 2.5 %collective-permute-done.2.got_first = f32[2,40,128]{2,1,0:T(8,128)S(1)} collective-permute-done((f32[2,40,128]{2,1,0:T(8,128)S(1)}, f32[2,40,128]{2,1,0:T(8,128)S(1)}, u32[]{:S(2)}, u32[]{:S(2)}) %collective-permute-start.2) | collective-permute-done | bytes 40992 | tf_op jit(solution)/shard_map/ppermute | solution.py:585
  16.5 4.1 %collective-permute-start.4 = (f32[8,512]{1,0:T(8,128)S(1)}, f32[8,512]{1,0:T(8,128)S(1)}, u32[]{:S(2)}, u32[]{:S(2)}) collective-permute-start(f32[8,512]{1,0:T(8,128)S(1)} %get-tuple-element.62), channel_id=1, source_target_pairs={{0,12},{4,8},{8,4},{12,0},{1,13},{5,9},{9,5},{13,1},{2,14},{6,10},... | collective-permute-start | bytes 49160 | tf_op jit(solution)/shard_map/ppermute | solution.py:585
  20.8 4.1 %start_middle.1 = (f32[32,224,128]{2,1,0:T(8,128)S(1)}, f32[80,512]{1,0:T(8,128)S(1)}) custom-call(f32[2,80,512]{2,1,0:T(8,128)S(1)} %get-tuple-element.61.both, f32[224,128]{1,0:T(8,128)S(1)} %broadcast_in_dim.10.area, f32[32,224,128]{2,1,0:T(8,128)S(1)} %get-tuple-element.64.offset, f32[32,224,128]{2,1,0:T(8,128)S(1)} %get-tuple-element.65.precip, ...), custom_call_target="tpu_custom_call" | custom-call | flops 1000000000 | bytes 20000000 | tf_op jit(solution)/shard_map/start_middle/pallas_call | solution.py:595
  25.0 1.2 %start.1 = (f32[32,32,128]{2,1,0:T(8,128)S(1)}, f32[80,512]{1,0:T(8,128)S(1)}, f32[3,4,40,128]{3,2,1,0:T(8,128)S(1)}, f32[3,2,8,128]{3,2,1,0:T(8,128)S(1)}, f32[3,2,8,128]{3,2,1,0:T(8,128)S(1)}) custom-call(f32[2,80,512]{2,1,0:T(8,128)S(1)} %get-tuple-element.61.both, f32[8,512]{1,0:T(8,128)S(1)} %collective-permute-done.4.got_first, ...), custom_call_target="tpu_custom_call" | custom-call | flops 1000000000 | bytes 20000000 | tf_op jit(solution)/shard_map/start/pallas_call | solution.py:595
  26.2 2.5 %collective-permute-start.6 = (f32[3,2,8,128]{3,2,1,0:T(8,128)S(1)}, f32[3,2,8,128]{3,2,1,0:T(8,128)S(1)}, u32[]{:S(2)}, u32[]{:S(2)}) collective-permute-start(f32[3,2,8,128]{3,2,1,0:T(8,128)S(1)} %get-tuple-element.69), channel_id=1, source_target_pairs={{0,112},{16,32},{32,16},{48,64},{64,48},{80,96},{96,80},{112,0},{1... | collective-permute-start | bytes 73736 | tf_op jit(solution)/shard_map/ppermute | solution.py:585
  28.8 5.0 %collective-permute-done.6.got_first = f32[3,2,8,128]{3,2,1,0:T(8,128)S(1)} collective-permute-done((f32[3,2,8,128]{3,2,1,0:T(8,128)S(1)}, f32[3,2,8,128]{3,2,1,0:T(8,128)S(1)}, u32[]{:S(2)}, u32[]{:S(2)}) %collective-permute-start.6) | collective-permute-done | bytes 24608 | tf_op jit(solution)/shard_map/ppermute | solution.py:585
  34.3 0.8 collective-permute-start.9
  35.1 2.8 %collective-permute-done.8.got_first = f32[3,40,128]{2,1,0:T(8,128)S(1)} collective-permute-done((f32[3,40,128]{2,1,0:T(8,128)S(1)}, f32[3,40,128]{2,1,0:T(8,128)S(1)}, u32[]{:S(2)}, u32[]{:S(2)}) %collective-permute-start.8) | collective-permute-done | bytes 61472 | tf_op jit(solution)/shard_map/ppermute | solution.py:585
  38.2 0.7 collective-permute-start.10
  38.9 1.7 %collective-permute-start.11 = (f32[8,512]{1,0:T(8,128)S(1)}, f32[8,512]{1,0:T(8,128)S(1)}, u32[]{:S(2)}, u32[]{:S(2)}) collective-permute-start(f32[8,512]{1,0:T(8,128)S(1)} %get-tuple-element.76), channel_id=1, source_target_pairs={{0,4},{4,0},{8,12},{12,8},{1,5},{5,1},{9,13},{13,9},{2,6},{6,2},{1... | collective-permute-start | bytes 49160 | tf_op jit(solution)/shard_map/ppermute | solution.py:585
  40.6 2.9 %hessian_middle.2.total = f32[80,512]{1,0:T(8,128)S(1)} custom-call(f32[80,512]{1,0:T(8,128)S(1)} %get-tuple-element.74.partial_rows, f32[80,512]{1,0:T(8,128)S(1)} %get-tuple-element.77.diag, f32[32,224,128]{2,1,0:T(8,128)S(1)} %get-tuple-element.78.weight, bf16[224,240]{1,0:T(8,128)(2,1)S(1)} %copy-done.3, bf16[2,80,336]{2,1,0:T(8,128)(2,1)S(1)} %copy-done.2, ...), custom_call_target="tpu_custom_call" | custom-call | flops 1000000000 | bytes 20000000 | tf_op jit(solution)/shard_map/hessian_middle/pallas_call | solution.py:595
  43.5 1.1 %hessian.2 = (f32[80,512]{1,0:T(8,128)S(1)}, f32[80,512]{1,0:T(8,128)S(1)}, f32[3,4,40,128]{3,2,1,0:T(8,128)S(1)}, f32[3,2,8,128]{3,2,1,0:T(8,128)S(1)}, f32[3,2...) custom-call(f32[80,512]{1,0:T(8,128)S(1)} %get-tuple-element.74.partial_rows, ...), custom_call_target="tpu_custom_call" | custom-call | flops 1000000000 | bytes 20000000 | tf_op jit(solution)/shard_map/hessian/pallas_call | solution.py:595
  44.5 3.7 %collective-permute-start.12 = (f32[3,2,8,128]{3,2,1,0:T(8,128)S(1)}, f32[3,2,8,128]{3,2,1,0:T(8,128)S(1)}, u32[]{:S(2)}, u32[]{:S(2)}) collective-permute-start(f32[3,2,8,128]{3,2,1,0:T(8,128)S(1)} %get-tuple-element.81), channel_id=1, source_target_pairs={{0,112},{16,32},{32,16},{48,64},{64,48},{80,96},{96,80},{112,0},{1... | collective-permute-start | bytes 73736 | tf_op jit(solution)/shard_map/ppermute | solution.py:585
  48.3 0.5 collective-permute-start.13
  48.8 3.3 %collective-permute-done.12.got_first = f32[3,2,8,128]{3,2,1,0:T(8,128)S(1)} collective-permute-done((f32[3,2,8,128]{3,2,1,0:T(8,128)S(1)}, f32[3,2,8,128]{3,2,1,0:T(8,128)S(1)}, u32[]{:S(2)}, u32[]{:S(2)}) %collective-permute-start.12) | collective-permute-done | bytes 24608 | tf_op jit(solution)/shard_map/ppermute | solution.py:585
  52.1 1.5 %collective-permute-done.13.got_second = f32[3,2,8,128]{3,2,1,0:T(8,128)S(1)} collective-permute-done((f32[3,2,8,128]{3,2,1,0:T(8,128)S(1)}, f32[3,2,8,128]{3,2,1,0:T(8,128)S(1)}, u32[]{:S(2)}, u32[]{:S(2)}) %collective-permute-start.13) | collective-permute-done | bytes 24608 | tf_op jit(solution)/shard_map/ppermute | solution.py:585
  53.9 0.7 collective-permute-start.15
  54.5 3.0 %collective-permute-done.14.got_first = f32[3,40,128]{2,1,0:T(8,128)S(1)} collective-permute-done((f32[3,40,128]{2,1,0:T(8,128)S(1)}, f32[3,40,128]{2,1,0:T(8,128)S(1)}, u32[]{:S(2)}, u32[]{:S(2)}) %collective-permute-start.14) | collective-permute-done | bytes 61472 | tf_op jit(solution)/shard_map/ppermute | solution.py:585
  57.7 2.4 %collective-permute-start.16 = (f32[8,512]{1,0:T(8,128)S(1)}, f32[8,512]{1,0:T(8,128)S(1)}, u32[]{:S(2)}, u32[]{:S(2)}) collective-permute-start(f32[8,512]{1,0:T(8,128)S(1)} %get-tuple-element.87), channel_id=1, source_target_pairs={{0,12},{4,8},{8,4},{12,0},{1,13},{5,9},{9,5},{13,1},{2,14},{6,10},... | collective-permute-start | bytes 49160 | tf_op jit(solution)/shard_map/ppermute | solution.py:585
  60.4 2.9 %hessian_middle.3.total = f32[80,512]{1,0:T(8,128)S(1)} custom-call(f32[80,512]{1,0:T(8,128)S(1)} %get-tuple-element.86.partial_rows, f32[80,512]{1,0:T(8,128)S(1)} %get-tuple-element.77.diag, f32[32,224,128]{2,1,0:T(8,128)S(1)} %get-tuple-element.78.weight, bf16[224,240]{1,0:T(8,128)(2,1)S(1)} %copy-done.3, bf16[2,80,336]{2,1,0:T(8,128)(2,1)S(1)} %copy-done.2, ...), custom_call_target="tpu_custom_call" | custom-call | flops 1000000000 | bytes 20000000 | tf_op jit(solution)/shard_map/hessian_middle/pallas_call | solution.py:595
  63.3 0.6 collective-permute-done.17.got_second
  63.9 1.1 %hessian.3 = (f32[80,512]{1,0:T(8,128)S(1)}, f32[80,512]{1,0:T(8,128)S(1)}, f32[3,4,40,128]{3,2,1,0:T(8,128)S(1)}, f32[32,16,128]{2,1,0:T(8,128)S(1)}) custom-call(f32[80,512]{1,0:T(8,128)S(1)} %get-tuple-element.86.partial_rows, f32[8,512]{1,0:T(8,128)S(1)} %collective-permute-done.16.got_first, f32[8,512]{1,0:T(8,128)S(1)} %collective-permute-done.17.got_second, ...), custom_call_target="tpu_custom_call" | custom-call | flops 1000000000 | bytes 20000000 | tf_op jit(solution)/shard_map/hessian/pallas_call | solution.py:595
  65.0 15.9 %all_to_all.5.slots = f32[32,16,128]{2,1,0:T(8,128)S(1)} all-to-all(f32[32,16,128]{2,1,0:T(8,128)S(1)} %get-tuple-element.91), channel_id=1, replica_groups=mesh['lon'=8,'lat'=4,'tm'=4] {'lon','lat'}, dimensions={0} | all-to-all | bytes 524288 | tf_op jit(solution)/shard_map/all_to_all | solution.py:628
  81.3 0.6 collective-permute-start.19
  81.9 1.6 %collective-permute-start.20 = (f32[8,128]{1,0:T(8,128)S(1)}, f32[8,128]{1,0:T(8,128)S(1)}, u32[]{:S(2)}, u32[]{:S(2)}) collective-permute-start(f32[8,128]{1,0:T(8,128)S(1)} %get-tuple-element.95._.lines), channel_id=1, source_target_pairs={{0,2},{1,3},{2,0},{3,1},{4,6},{5,7},{6,4},{7,5},{8,10},{9,11},{10,... | collective-permute-start | bytes 12296 | tf_op jit(solution)/shard_map/ppermute | solution.py:635
  83.9 1.6 %collective-permute-done.20.got_lines = f32[8,128]{1,0:T(8,128)S(1)} collective-permute-done((f32[8,128]{1,0:T(8,128)S(1)}, f32[8,128]{1,0:T(8,128)S(1)}, u32[]{:S(2)}, u32[]{:S(2)}) %collective-permute-start.20) | collective-permute-done | bytes 4128 | tf_op jit(solution)/shard_map/ppermute | solution.py:635
  85.5 0.9 %last.1 = (f32[8,32,64]{2,1,0:T(8,128)}, f32[8,32,64]{2,1,0:T(8,128)}) custom-call(f32[3,4,40,128]{3,2,1,0:T(8,128)S(1)} %get-tuple-element.92.tiles, f32[40,128]{1,0:T(8,128)S(1)} %collective-permute-done.18.got_first, f32[40,128]{1,0:T(8,128)S(1)} %collective-permute-done.19.got_second, f32[8,128]{1,0:T(8,128)S(1)} %get-tuple-element.95._.lines, ...), custom_call_target="tpu_custom_call" | custom-call | flops 1000000000 | bytes 20000000 | tf_op jit(solution)/shard_map/last/pallas_call | solution.py:595
  (47 shorter events, 3.4 us)
Async XLA Ops:
  1.8 9.1 %collective-permute-start = (f32[4,8,128]{2,1,0:T(8,128)S(1)}, f32[4,8,128]{2,1,0:T(8,128)S(1)}, u32[]{:S(2)}, u32[]{:S(2)}) collective-permute-start(f32[4,8,128]{2,1,0:T(8,128)S(1)} %get-tuple-element.55._), channel_id=1, source_target_pairs={{0,112},{16,32},{32,16},{48,64},{64,48},{80,96},{96,80},{112,0},{1... | collective-permute-start | bytes 49160 | tf_op jit(solution)/shard_map/ppermute | solution.py:585
  7.4 5.2 %collective-permute-start.1 = (f32[4,8,128]{2,1,0:T(8,128)S(1)}, f32[4,8,128]{2,1,0:T(8,128)S(1)}, u32[]{:S(2)}, u32[]{:S(2)}) collective-permute-start(f32[4,8,128]{2,1,0:T(8,128)S(1)} %get-tuple-element.56), channel_id=1, source_target_pairs={{0,16},{16,0},{32,48},{48,32},{64,80},{80,64},{96,112},{112,96},{1... | collective-permute-start | bytes 49160 | tf_op jit(solution)/shard_map/ppermute | solution.py:585
  12.6 8.1 %copy-start = (bf16[384,384]{1,0:T(8,128)(2,1)S(1)}, bf16[384,384]{1,0:T(8,128)(2,1)}, u32[]{:S(2)}) copy-start(bf16[384,384]{1,0:T(8,128)(2,1)} %constant.40.lon_up) | copy-start | bytes 884740
  12.6 8.1 %copy-start.1 = (bf16[384,256]{1,0:T(8,128)(2,1)S(1)}, bf16[384,256]{1,0:T(8,128)(2,1)}, u32[]{:S(2)}) copy-start(bf16[384,256]{1,0:T(8,128)(2,1)} %constant.43.lon_down) | copy-start | bytes 589828
  12.6 8.1 %copy-start.2 = (bf16[2,80,336]{2,1,0:T(8,128)(2,1)S(1)}, bf16[2,80,336]{2,1,0:T(8,128)(2,1)}, u32[]{:S(2)}) copy-start(bf16[2,80,336]{2,1,0:T(8,128)(2,1)} %constant.35.lat_down) | copy-start | bytes 322564
  12.6 8.1 %copy-start.3 = (bf16[224,240]{1,0:T(8,128)(2,1)S(1)}, bf16[224,240]{1,0:T(8,128)(2,1)}, u32[]{:S(2)}) copy-start(bf16[224,240]{1,0:T(8,128)(2,1)} %constant.30.lat_up) | copy-start | bytes 322564
  12.7 3.5 %collective-permute-start.2 = (f32[2,40,128]{2,1,0:T(8,128)S(1)}, f32[2,40,128]{2,1,0:T(8,128)S(1)}, u32[]{:S(2)}, u32[]{:S(2)}) collective-permute-start(f32[2,40,128]{2,1,0:T(8,128)S(1)} %get-tuple-element.59), channel_id=1, source_target_pairs={{0,3},{1,2},{2,1},{3,0},{4,7},{5,6},{6,5},{7,4},{8,11},{9,10},{10,... | collective-permute-start | bytes 122888 | tf_op jit(solution)/shard_map/ppermute | solution.py:585
  12.8 3.4 %collective-permute-start.3 = (f32[2,40,128]{2,1,0:T(8,128)S(1)}, f32[2,40,128]{2,1,0:T(8,128)S(1)}, u32[]{:S(2)}, u32[]{:S(2)}) collective-permute-start(f32[2,40,128]{2,1,0:T(8,128)S(1)} %get-tuple-element.60), channel_id=1, source_target_pairs={{0,1},{1,0},{2,3},{3,2},{4,5},{5,4},{6,7},{7,6},{8,9},{9,8},{10,11... | collective-permute-start | bytes 122888 | tf_op jit(solution)/shard_map/ppermute | solution.py:585
  16.5 8.4 %collective-permute-start.4 = (f32[8,512]{1,0:T(8,128)S(1)}, f32[8,512]{1,0:T(8,128)S(1)}, u32[]{:S(2)}, u32[]{:S(2)}) collective-permute-start(f32[8,512]{1,0:T(8,128)S(1)} %get-tuple-element.62), channel_id=1, source_target_pairs={{0,12},{4,8},{8,4},{12,0},{1,13},{5,9},{9,5},{13,1},{2,14},{6,10},... | collective-permute-start | bytes 49160 | tf_op jit(solution)/shard_map/ppermute | solution.py:585
  20.6 4.3 %collective-permute-start.5 = (f32[8,512]{1,0:T(8,128)S(1)}, f32[8,512]{1,0:T(8,128)S(1)}, u32[]{:S(2)}, u32[]{:S(2)}) collective-permute-start(f32[8,512]{1,0:T(8,128)S(1)} %get-tuple-element.63), channel_id=1, source_target_pairs={{0,4},{4,0},{8,12},{12,8},{1,5},{5,1},{9,13},{13,9},{2,6},{6,2},{1... | collective-permute-start | bytes 49160 | tf_op jit(solution)/shard_map/ppermute | solution.py:585
  20.8 4.3 %copy-start.4 = (bf16[1,80,96]{2,1,0:T(8,128)(2,1)S(1)}, bf16[1,80,96]{2,1,0:T(8,128)(2,1)}, u32[]{:S(2)}) copy-start(bf16[1,80,96]{2,1,0:T(8,128)(2,1)} %constant.55.lat_down) | copy-start | bytes 46084
  20.8 4.2 %copy-start.5 = (bf16[32,240]{1,0:T(8,128)(2,1)S(1)}, bf16[32,240]{1,0:T(8,128)(2,1)}, u32[]{:S(2)}) copy-start(bf16[32,240]{1,0:T(8,128)(2,1)} %constant.50.lat_up) | copy-start | bytes 46084
  26.2 7.5 %collective-permute-start.6 = (f32[3,2,8,128]{3,2,1,0:T(8,128)S(1)}, f32[3,2,8,128]{3,2,1,0:T(8,128)S(1)}, u32[]{:S(2)}, u32[]{:S(2)}) collective-permute-start(f32[3,2,8,128]{3,2,1,0:T(8,128)S(1)} %get-tuple-element.69), channel_id=1, source_target_pairs={{0,112},{16,32},{32,16},{48,64},{64,48},{80,96},{96,80},{112,0},{1... | collective-permute-start | bytes 73736 | tf_op jit(solution)/shard_map/ppermute | solution.py:585
  28.8 5.3 %collective-permute-start.7 = (f32[3,2,8,128]{3,2,1,0:T(8,128)S(1)}, f32[3,2,8,128]{3,2,1,0:T(8,128)S(1)}, u32[]{:S(2)}, u32[]{:S(2)}) collective-permute-start(f32[3,2,8,128]{3,2,1,0:T(8,128)S(1)} %get-tuple-element.70), channel_id=1, source_target_pairs={{0,16},{16,0},{32,48},{48,32},{64,80},{80,64},{96,112},{112,96},{1... | collective-permute-start | bytes 73736 | tf_op jit(solution)/shard_map/ppermute | solution.py:585
  34.2 3.7 %collective-permute-start.8 = (f32[3,40,128]{2,1,0:T(8,128)S(1)}, f32[3,40,128]{2,1,0:T(8,128)S(1)}, u32[]{:S(2)}, u32[]{:S(2)}) collective-permute-start(f32[3,40,128]{2,1,0:T(8,128)S(1)} %get-tuple-element.72), channel_id=1, source_target_pairs={{0,3},{1,2},{2,1},{3,0},{4,7},{5,6},{6,5},{7,4},{8,11},{9,10},{10,... | collective-permute-start | bytes 184328 | tf_op jit(solution)/shard_map/ppermute | solution.py:585
  34.3 3.6 %collective-permute-start.9 = (f32[3,40,128]{2,1,0:T(8,128)S(1)}, f32[3,40,128]{2,1,0:T(8,128)S(1)}, u32[]{:S(2)}, u32[]{:S(2)}) collective-permute-start(f32[3,40,128]{2,1,0:T(8,128)S(1)} %get-tuple-element.73), channel_id=1, source_target_pairs={{0,1},{1,0},{2,3},{3,2},{4,5},{5,4},{6,7},{7,6},{8,9},{9,8},{10,11... | collective-permute-start | bytes 184328 | tf_op jit(solution)/shard_map/ppermute | solution.py:585
  38.2 5.3 %collective-permute-start.10 = (f32[8,512]{1,0:T(8,128)S(1)}, f32[8,512]{1,0:T(8,128)S(1)}, u32[]{:S(2)}, u32[]{:S(2)}) collective-permute-start(f32[8,512]{1,0:T(8,128)S(1)} %get-tuple-element.75), channel_id=1, source_target_pairs={{0,12},{4,8},{8,4},{12,0},{1,13},{5,9},{9,5},{13,1},{2,14},{6,10},... | collective-permute-start | bytes 49160 | tf_op jit(solution)/shard_map/ppermute | solution.py:585
  38.9 4.6 %collective-permute-start.11 = (f32[8,512]{1,0:T(8,128)S(1)}, f32[8,512]{1,0:T(8,128)S(1)}, u32[]{:S(2)}, u32[]{:S(2)}) collective-permute-start(f32[8,512]{1,0:T(8,128)S(1)} %get-tuple-element.76), channel_id=1, source_target_pairs={{0,4},{4,0},{8,12},{12,8},{1,5},{5,1},{9,13},{13,9},{2,6},{6,2},{1... | collective-permute-start | bytes 49160 | tf_op jit(solution)/shard_map/ppermute | solution.py:585
  44.5 7.5 %collective-permute-start.12 = (f32[3,2,8,128]{3,2,1,0:T(8,128)S(1)}, f32[3,2,8,128]{3,2,1,0:T(8,128)S(1)}, u32[]{:S(2)}, u32[]{:S(2)}) collective-permute-start(f32[3,2,8,128]{3,2,1,0:T(8,128)S(1)} %get-tuple-element.81), channel_id=1, source_target_pairs={{0,112},{16,32},{32,16},{48,64},{64,48},{80,96},{96,80},{112,0},{1... | collective-permute-start | bytes 73736 | tf_op jit(solution)/shard_map/ppermute | solution.py:585
  48.3 5.3 %collective-permute-start.13 = (f32[3,2,8,128]{3,2,1,0:T(8,128)S(1)}, f32[3,2,8,128]{3,2,1,0:T(8,128)S(1)}, u32[]{:S(2)}, u32[]{:S(2)}) collective-permute-start(f32[3,2,8,128]{3,2,1,0:T(8,128)S(1)} %get-tuple-element.82), channel_id=1, source_target_pairs={{0,16},{16,0},{32,48},{48,32},{64,80},{80,64},{96,112},{112,96},{1... | collective-permute-start | bytes 73736 | tf_op jit(solution)/shard_map/ppermute | solution.py:585
  53.8 3.7 %collective-permute-start.14 = (f32[3,40,128]{2,1,0:T(8,128)S(1)}, f32[3,40,128]{2,1,0:T(8,128)S(1)}, u32[]{:S(2)}, u32[]{:S(2)}) collective-permute-start(f32[3,40,128]{2,1,0:T(8,128)S(1)} %get-tuple-element.84), channel_id=1, source_target_pairs={{0,3},{1,2},{2,1},{3,0},{4,7},{5,6},{6,5},{7,4},{8,11},{9,10},{10,... | collective-permute-start | bytes 184328 | tf_op jit(solution)/shard_map/ppermute | solution.py:585
  53.9 3.6 %collective-permute-start.15 = (f32[3,40,128]{2,1,0:T(8,128)S(1)}, f32[3,40,128]{2,1,0:T(8,128)S(1)}, u32[]{:S(2)}, u32[]{:S(2)}) collective-permute-start(f32[3,40,128]{2,1,0:T(8,128)S(1)} %get-tuple-element.85), channel_id=1, source_target_pairs={{0,1},{1,0},{2,3},{3,2},{4,5},{5,4},{6,7},{7,6},{8,9},{9,8},{10,11... | collective-permute-start | bytes 184328 | tf_op jit(solution)/shard_map/ppermute | solution.py:585
  57.7 5.6 %collective-permute-start.16 = (f32[8,512]{1,0:T(8,128)S(1)}, f32[8,512]{1,0:T(8,128)S(1)}, u32[]{:S(2)}, u32[]{:S(2)}) collective-permute-start(f32[8,512]{1,0:T(8,128)S(1)} %get-tuple-element.87), channel_id=1, source_target_pairs={{0,12},{4,8},{8,4},{12,0},{1,13},{5,9},{9,5},{13,1},{2,14},{6,10},... | collective-permute-start | bytes 49160 | tf_op jit(solution)/shard_map/ppermute | solution.py:585
  60.1 3.7 %collective-permute-start.17 = (f32[8,512]{1,0:T(8,128)S(1)}, f32[8,512]{1,0:T(8,128)S(1)}, u32[]{:S(2)}, u32[]{:S(2)}) collective-permute-start(f32[8,512]{1,0:T(8,128)S(1)} %get-tuple-element.88), channel_id=1, source_target_pairs={{0,4},{4,0},{8,12},{12,8},{1,5},{5,1},{9,13},{13,9},{2,6},{6,2},{1... | collective-permute-start | bytes 49160 | tf_op jit(solution)/shard_map/ppermute | solution.py:585
  81.2 4.3 %collective-permute-start.18 = (f32[40,128]{1,0:T(8,128)S(1)}, f32[40,128]{1,0:T(8,128)S(1)}, u32[]{:S(2)}, u32[]{:S(2)}) collective-permute-start(f32[40,128]{1,0:T(8,128)S(1)} %get-tuple-element.93), channel_id=1, source_target_pairs={{0,3},{1,2},{2,1},{3,0},{4,7},{5,6},{6,5},{7,4},{8,11},{9,10},{10,... | collective-permute-start | bytes 61448 | tf_op jit(solution)/shard_map/ppermute | solution.py:585
  81.3 4.2 %collective-permute-start.19 = (f32[40,128]{1,0:T(8,128)S(1)}, f32[40,128]{1,0:T(8,128)S(1)}, u32[]{:S(2)}, u32[]{:S(2)}) collective-permute-start(f32[40,128]{1,0:T(8,128)S(1)} %get-tuple-element.94), channel_id=1, source_target_pairs={{0,1},{1,0},{2,3},{3,2},{4,5},{5,4},{6,7},{7,6},{8,9},{9,8},{10,11... | collective-permute-start | bytes 61448 | tf_op jit(solution)/shard_map/ppermute | solution.py:585
  81.9 3.6 %collective-permute-start.20 = (f32[8,128]{1,0:T(8,128)S(1)}, f32[8,128]{1,0:T(8,128)S(1)}, u32[]{:S(2)}, u32[]{:S(2)}) collective-permute-start(f32[8,128]{1,0:T(8,128)S(1)} %get-tuple-element.95._.lines), channel_id=1, source_target_pairs={{0,2},{1,3},{2,0},{3,1},{4,6},{5,7},{6,4},{7,5},{8,10},{9,11},{10,... | collective-permute-start | bytes 12296 | tf_op jit(solution)/shard_map/ppermute | solution.py:635

commit v4 on v3

--- a/solution.py
+++ b/solution.py
@@ -246,17 +246,41 @@
     return sums, [[turned[g][r * SEG : (r + 1) * SEG] for g in range(4)] for r in range(3)]
 
 
+def rolled(values, amount, axis):
+    amount %= values.shape[axis]
+    return pltpu.roll(values, amount, axis) if amount else values
+
+
+def pack_lanes(parts):
+    lane = lax.broadcasted_iota(jnp.int32, parts[0].shape, 1)
+    rest = pltpu.roll(parts[0], 64, 1)
+    for i in range(1, len(parts)):
+        rest = jnp.where(lane < 4 * i, rest, pltpu.roll(parts[i], 64 + 4 * i, 1))
+    pairs = [jnp.where(lane < 64, parts[i], pltpu.roll(parts[i + 1], 64, 1)) for i in range(0, len(parts), 2)]
+    return pairs + [rest]
+
+
+def unpack_lanes(packs, i):
+    lane = lax.broadcasted_iota(jnp.int32, packs[0].shape, 1)
+    main, rest = rolled(packs[i // 2], -64 * (i % 2), 1), rolled(packs[-1], 64 - 4 * i, 1)
+    return jnp.where(lane < 64, main, jnp.where(lane < LAT_OWN + 4, rest, 0.0))
+
+
 def write_ends(segs, place, tiles, first, second):
     lower = lax.broadcasted_iota(jnp.int32, (8, 128), 0) < 4
+    sides = []
+    for at in (0, 32):
+        parts = []
+        for r in range(3):
+            for h in range(2):
+                pair = (segs[r][2 * h + i][at : at + 8] for i in range(2))
+                parts.append(jnp.where(lower, next(pair), pltpu.roll(next(pair), 4, 0)))
+        sides.append(pack_lanes(parts))
     for r in range(3):
         for g in range(4):
             tiles[r, g] = segs[r][g]
-        for h in range(2):
-            packed = [
-                jnp.where(lower, segs[r][2 * h][at : at + 8], pltpu.roll(segs[r][2 * h + 1][at : at + 8], 4, 0))
-                for at in (0, 32)
-            ]
-            first[r, h], second[r, h] = place.messages("lon", *packed)
+    for i, pair in enumerate(zip(*sides)):
+        first[i], second[i] = place.messages("lon", *pair)
 
 
 def start_of(area, offset, precip, weight):
@@ -348,11 +372,6 @@
     lon_count, lat_count = lax.axis_size("lon"), lax.axis_size("lat")
     lon = lax.rem(lax.axis_index("lon") + (lon_count + lon_step), lon_count)
     return lon * lat_count + lax.rem(lax.axis_index("lat") + (lat_count + lat_step), lat_count)
-
-
-def rolled(values, amount, axis):
-    amount %= values.shape[axis]
-    return pltpu.roll(values, amount, axis) if amount else values
 
 
 def row_of(shape=(8, 128)):
@@ -435,24 +454,17 @@
 def join_kernel(tiles, got_first, got_second, joined, first, second):
     place = Place()
     lower = lax.broadcasted_iota(jnp.int32, (8, 128), 0) < 4
+    lefts, rights = zip(*(place.received("lon", got_first[i], got_second[i]) for i in range(4)))
     for r in range(3):
-        for g in range(4):
-            left, right = place.received("lon", got_first[r, g // 2], got_second[r, g // 2])
-            if g % 2:
-                left, right = pltpu.roll(left, 4, 0), pltpu.roll(right, 4, 0)
-            joined[r, g, 0:8] = tiles[r, g, 0:8] + jnp.where(lower, left, 0.0)
-            joined[r, g, 8:32] = tiles[r, g, 8:32]
-            joined[r, g, 32:40] = tiles[r, g, 32:40] + jnp.where(lower, right, 0.0)
-    lane = lax.broadcasted_iota(jnp.int32, (SEG, 128), 1)
-
-    def packed(r):
-        rest = pltpu.roll(joined[r, 0], 64, 1)
-        for g in range(1, 4):
-            rest = jnp.where(lane < 4 * g, rest, pltpu.roll(joined[r, g], 64 + 4 * g, 1))
-        return [jnp.where(lane < 64, joined[r, g], pltpu.roll(joined[r, g + 1], 64, 1)) for g in (0, 2)] + [rest]
-
-    for i, (low_side, high_side) in enumerate(zip(packed(0), packed(2))):
-        first[i], second[i] = place.messages("tm", low_side, high_side)
+        for h in range(2):
+            pair_left, pair_right = unpack_lanes(lefts, 2 * r + h), unpack_lanes(rights, 2 * r + h)
+            for g in (2 * h, 2 * h + 1):
+                left, right = rolled(pair_left, 4 * (g % 2), 0), rolled(pair_right, 4 * (g % 2), 0)
+                joined[r, g, 0:8] = tiles[r, g, 0:8] + jnp.where(lower, left, 0.0)
+                joined[r, g, 8:32] = tiles[r, g, 8:32]
+                joined[r, g, 32:40] = tiles[r, g, 32:40] + jnp.where(lower, right, 0.0)
+    for i, pair in enumerate(zip(*(pack_lanes([joined[r, g] for g in range(4)]) for r in (0, 2)))):
+        first[i], second[i] = place.messages("tm", *pair)
 
 
 def turned_rows(tiles, g, left=0.0, right=0.0):
@@ -462,16 +474,9 @@
 
 def turn_kernel(tiles, got_first, got_second, rows, first, second):
     place = Place()
-    lane = lax.broadcasted_iota(jnp.int32, (SEG, 128), 1)
-    sides = [place.received("tm", got_first[i], got_second[i]) for i in range(3)]
-
-    def unpacked(g, side):
-        main = rolled(sides[g // 2][side], -64 * (g % 2), 1)
-        rest = rolled(sides[2][side], 64 - 4 * g, 1)
-        return jnp.where(lane < 64, main, jnp.where(lane < LAT_OWN + 4, rest, 0.0))
-
+    lefts, rights = zip(*(place.received("tm", got_first[i], got_second[i]) for i in range(3)))
     for g in range(4):
-        block = turned_rows(tiles, g, unpacked(g, 0), unpacked(g, 1))
+        block = turned_rows(tiles, g, unpack_lanes(lefts, g), unpack_lanes(rights, g))
         lanes = slice(g * 128, (g + 1) * 128)
         rows[:, lanes] = block[:ROWS]
         first[:, lanes], second[:, lanes] = place.messages("lat", block[0:8], block[64:72])
@@ -558,11 +563,16 @@
 def last_kernel(tiles, got_first, got_second, lines, got_lines, residual, scaled, image, image_scaled, step_out, residual_out):
     place = Place()
     total = lines[...] + got_lines[...] + got_first[32:40] + got_second[32:40]
-    norm, curvature, image_norm, image_curvature = (jnp.sum(total[i : i + 1], axis=1, keepdims=True) for i in range(4, 8))
-    step_size = norm / curvature
-    next_norm = step_size * step_size * image_norm - norm
+    norms, curvatures, image_norms, image_curvatures = (total[i : i + 1] for i in range(4, 8))
+
+    def all_lanes(values):
+        return jnp.sum(values, axis=1, keepdims=True)
+
+    norm = all_lanes(norms)
+    step_size = norm / all_lanes(curvatures)
+    next_norm = all_lanes(norms + step_size * (step_size * image_norms - 2.0 * curvatures))
+    next_curvature = all_lanes(curvatures + step_size * (step_size * image_curvatures - 2.0 * image_norms))
     ratio = next_norm / norm
-    next_curvature = curvature - 2.0 * step_size * image_norm + step_size * step_size * image_curvature
     step_next = next_norm / (next_curvature - ratio * next_norm / step_size)
     left, right = place.received("tm", got_first[...], got_second[...])
     for t in range(T_OWN):
@@ -604,7 +614,7 @@
     )(*args)
 
 
-LON_MESSAGE, TM_MESSAGE, LAT_MESSAGE = (3, 2, 8, 128), (3, SEG, 128), (8, LANES)
+LON_MESSAGE, TM_MESSAGE, LAT_MESSAGE = (4, 8, 128), (3, SEG, 128), (8, LANES)
 TILES = (3, 4, SEG, 128)
 VECTOR = (ROWS, LANES)
 MID_SCRATCH, EDGE_SCRATCH = ([pltpu.VMEM((4 * n, 384), jnp.float32)] * m for n, m in ((CHUNK, 4), (EDGE_CELLS, 2)))
@@ -632,7 +642,8 @@
     )
     first, second = swap(first, second, "tm")
     count = lax.axis_size("tm")
-    return tiles, first, second, lines, lax.ppermute(lines, "tm", [(i, (i + 2) % count) for i in range(count)])
+    got_lines = lax.ppermute(lines, "tm", [(i, (i + 2) % count) for i in range(count)])
+    return tiles, first, second, lines, got_lines
 
 
 def expand(coefficients, inverse_diag, offset, precip):

time: 86.5 us -> 86.7 us (level)
  no operation moved by 1% of the time
where the time goes in v4:
time: 86.7 us; the launch traced here: 86.5 us
  starting transfers between devices  26.2 us (30%)
  waiting for transfers between devices  22.3 us (26%)
  Pallas kernels  19.9 us (23%)
  blocking collectives  15.7 us (18%)
  other arithmetic  1.12 us (1%)
  between operations  0.9 us (1%)
    pallas_call x17, Pallas kernels, call(): pl.pallas_call(kernel, in_specs=[hbm if i in far else vmem for i in range...  19.9 us
    ppermute x10, starting transfers between devices, swap(): lax.ppermute(first, axis, first_pairs)  19.5 us
    ppermute x10, waiting for transfers between devices, swap(): lax.ppermute(first, axis, first_pairs)  16.4 us
    all_to_all x1, blocking collectives, fold_and_sum(): slots = lax.all_to_all(slots, ('lon', 'lat'), 0, 0, tiled=True)  15.7 us
    ppermute x10, starting transfers between devices, swap(): lax.ppermute(second, axis, second_pairs)  5.38 us
    ppermute x10, waiting for transfers between devices, swap(): lax.ppermute(second, axis, second_pairs)  4.19 us
  transfers between devices with their start and end apart: 21, of which 10 were waited for; matrix products, arithmetic and copies ran while one was open for 0% of the time, Pallas kernels for 16%

profile of v4, /device:TPU:0, one launch (start us, length us, event | category | flops | bytes accessed | tf_op | source)
XLA Modules:
  0.0 86.5 jit_solution(6621578728910933456)
XLA Ops:
  0.6 1.0 %pad_maximum_fusion.own_both = f32[2,8,32,64]{3,2,1,0:T(8,128)S(1)} fusion(f32[1,8,32,64]{3,2,1,0:T(8,128)} %bitcast.13, f32[1,8,32,64]{3,2,1,0:T(8,128)} %bitcast.14), kind=kLoop, calls=%fused_computation | loop fusion | flops 32768 | bytes 262144 | tf_op jit(solution)/shard_map/stack | solution.py:652
  1.8 5.6 %collective-permute-start = (f32[4,8,128]{2,1,0:T(8,128)S(1)}, f32[4,8,128]{2,1,0:T(8,128)S(1)}, u32[]{:S(2)}, u32[]{:S(2)}) collective-permute-start(f32[4,8,128]{2,1,0:T(8,128)S(1)} %get-tuple-element.55._), channel_id=1, source_target_pairs={{0,112},{16,32},{32,16},{48,64},{64,48},{80,96},{96,80},{112,0},{1... | collective-permute-start | bytes 49160 | tf_op jit(solution)/shard_map/ppermute | solution.py:595
  7.5 3.4 %load.1 = (f32[32,224,128]{2,1,0:T(8,128)S(1)}, f32[32,224,128]{2,1,0:T(8,128)S(1)}, f32[32,32,128]{2,1,0:T(8,128)S(1)}, f32[32,32,128]{2,1,0:T(8,128)S(1)}) custom-call(f32[4,8,128]{2,1,0:T(8,128)S(1)} %get-tuple-element.55._, f32[32,256,128]{2,1,0:T(8,128)} %offset_far.1, f32[32,256,128]{2,1,0:T(8,128)} %precip_far.1), custom_call_target="tpu_custom_call" | custom-call | flops 1000000000 | bytes 20000000 | tf_op jit(solution)/shard_map/load/pallas_call | solution.py:605
  10.9 1.7 %collective-permute-done.1.got_second = f32[4,8,128]{2,1,0:T(8,128)S(1)} collective-permute-done((f32[4,8,128]{2,1,0:T(8,128)S(1)}, f32[4,8,128]{2,1,0:T(8,128)S(1)}, u32[]{:S(2)}, u32[]{:S(2)}) %collective-permute-start.1) | collective-permute-done | bytes 16416 | tf_op jit(solution)/shard_map/ppermute | solution.py:595
  12.8 0.8 collective-permute-start.3
  13.8 2.5 %collective-permute-done.2.got_first = f32[2,40,128]{2,1,0:T(8,128)S(1)} collective-permute-done((f32[2,40,128]{2,1,0:T(8,128)S(1)}, f32[2,40,128]{2,1,0:T(8,128)S(1)}, u32[]{:S(2)}, u32[]{:S(2)}) %collective-permute-start.2) | collective-permute-done | bytes 40992 | tf_op jit(solution)/shard_map/ppermute | solution.py:595
  16.5 4.1 %collective-permute-start.4 = (f32[8,512]{1,0:T(8,128)S(1)}, f32[8,512]{1,0:T(8,128)S(1)}, u32[]{:S(2)}, u32[]{:S(2)}) collective-permute-start(f32[8,512]{1,0:T(8,128)S(1)} %get-tuple-element.62), channel_id=1, source_target_pairs={{0,12},{4,8},{8,4},{12,0},{1,13},{5,9},{9,5},{13,1},{2,14},{6,10},... | collective-permute-start | bytes 49160 | tf_op jit(solution)/shard_map/ppermute | solution.py:595
  20.8 4.1 %start_middle.1 = (f32[32,224,128]{2,1,0:T(8,128)S(1)}, f32[80,512]{1,0:T(8,128)S(1)}) custom-call(f32[2,80,512]{2,1,0:T(8,128)S(1)} %get-tuple-element.61.both, f32[224,128]{1,0:T(8,128)S(1)} %broadcast_in_dim.10.area, f32[32,224,128]{2,1,0:T(8,128)S(1)} %get-tuple-element.64.offset, f32[32,224,128]{2,1,0:T(8,128)S(1)} %get-tuple-element.65.precip, ...), custom_call_target="tpu_custom_call" | custom-call | flops 1000000000 | bytes 20000000 | tf_op jit(solution)/shard_map/start_middle/pallas_call | solution.py:605
  25.0 1.3 %start.1 = (f32[32,32,128]{2,1,0:T(8,128)S(1)}, f32[80,512]{1,0:T(8,128)S(1)}, f32[3,4,40,128]{3,2,1,0:T(8,128)S(1)}, f32[4,8,128]{2,1,0:T(8,128)S(1)}, f32[4,8,128]{2,1,0:T(8,128)S(1)}) custom-call(f32[2,80,512]{2,1,0:T(8,128)S(1)} %get-tuple-element.61.both, f32[8,512]{1,0:T(8,128)S(1)} %collective-permute-done.4.got_first, ...), custom_call_target="tpu_custom_call" | custom-call | flops 1000000000 | bytes 20000000 | tf_op jit(solution)/shard_map/start/pallas_call | solution.py:605
  26.3 2.5 %collective-permute-start.6 = (f32[4,8,128]{2,1,0:T(8,128)S(1)}, f32[4,8,128]{2,1,0:T(8,128)S(1)}, u32[]{:S(2)}, u32[]{:S(2)}) collective-permute-start(f32[4,8,128]{2,1,0:T(8,128)S(1)} %get-tuple-element.69), channel_id=1, source_target_pairs={{0,112},{16,32},{32,16},{48,64},{64,48},{80,96},{96,80},{112,0},{1... | collective-permute-start | bytes 49160 | tf_op jit(solution)/shard_map/ppermute | solution.py:595
  28.9 4.9 %collective-permute-done.6.got_first = f32[4,8,128]{2,1,0:T(8,128)S(1)} collective-permute-done((f32[4,8,128]{2,1,0:T(8,128)S(1)}, f32[4,8,128]{2,1,0:T(8,128)S(1)}, u32[]{:S(2)}, u32[]{:S(2)}) %collective-permute-start.6) | collective-permute-done | bytes 16416 | tf_op jit(solution)/shard_map/ppermute | solution.py:595
  34.4 0.8 collective-permute-start.9
  35.1 2.8 %collective-permute-done.8.got_first = f32[3,40,128]{2,1,0:T(8,128)S(1)} collective-permute-done((f32[3,40,128]{2,1,0:T(8,128)S(1)}, f32[3,40,128]{2,1,0:T(8,128)S(1)}, u32[]{:S(2)}, u32[]{:S(2)}) %collective-permute-start.8) | collective-permute-done | bytes 61472 | tf_op jit(solution)/shard_map/ppermute | solution.py:595
  38.2 0.7 collective-permute-start.10
  38.9 1.7 %collective-permute-start.11 = (f32[8,512]{1,0:T(8,128)S(1)}, f32[8,512]{1,0:T(8,128)S(1)}, u32[]{:S(2)}, u32[]{:S(2)}) collective-permute-start(f32[8,512]{1,0:T(8,128)S(1)} %get-tuple-element.76), channel_id=1, source_target_pairs={{0,4},{4,0},{8,12},{12,8},{1,5},{5,1},{9,13},{13,9},{2,6},{6,2},{1... | collective-permute-start | bytes 49160 | tf_op jit(solution)/shard_map/ppermute | solution.py:595
  40.6 2.9 %hessian_middle.2.total = f32[80,512]{1,0:T(8,128)S(1)} custom-call(f32[80,512]{1,0:T(8,128)S(1)} %get-tuple-element.74.partial_rows, f32[80,512]{1,0:T(8,128)S(1)} %get-tuple-element.77.diag, f32[32,224,128]{2,1,0:T(8,128)S(1)} %get-tuple-element.78.weight, bf16[224,240]{1,0:T(8,128)(2,1)S(1)} %copy-done.3, bf16[2,80,336]{2,1,0:T(8,128)(2,1)S(1)} %copy-done.2, ...), custom_call_target="tpu_custom_call" | custom-call | flops 1000000000 | bytes 20000000 | tf_op jit(solution)/shard_map/hessian_middle/pallas_call | solution.py:605
  43.5 1.1 %hessian.2 = (f32[80,512]{1,0:T(8,128)S(1)}, f32[80,512]{1,0:T(8,128)S(1)}, f32[3,4,40,128]{3,2,1,0:T(8,128)S(1)}, f32[4,8,128]{2,1,0:T(8,128)S(1)}, f32[4,8,128]{2,1,0:T(8,128)S(1)}, /*index=5*/f32[8,128]{1,0:T(8,128)S(1)}) custom-call(f32[80,512]{1,0:T(8,128)S(1)} %get-tuple-element.74.partial_rows, f32[8,512]{1,0:T(8,128)S(1)} %collective-permute-done.10.got_first, ...), custom_call_target="tpu_custom_call" | custom-call | flops 1000000000 | bytes 20000000 | tf_op jit(solution)/shard_map/hessian/pallas_call | solution.py:605
  44.6 3.7 %collective-permute-start.12 = (f32[4,8,128]{2,1,0:T(8,128)S(1)}, f32[4,8,128]{2,1,0:T(8,128)S(1)}, u32[]{:S(2)}, u32[]{:S(2)}) collective-permute-start(f32[4,8,128]{2,1,0:T(8,128)S(1)} %get-tuple-element.81), channel_id=1, source_target_pairs={{0,112},{16,32},{32,16},{48,64},{64,48},{80,96},{96,80},{112,0},{1... | collective-permute-start | bytes 49160 | tf_op jit(solution)/shard_map/ppermute | solution.py:595
  48.4 0.5 collective-permute-start.13
  48.9 3.2 %collective-permute-done.12.got_first = f32[4,8,128]{2,1,0:T(8,128)S(1)} collective-permute-done((f32[4,8,128]{2,1,0:T(8,128)S(1)}, f32[4,8,128]{2,1,0:T(8,128)S(1)}, u32[]{:S(2)}, u32[]{:S(2)}) %collective-permute-start.12) | collective-permute-done | bytes 16416 | tf_op jit(solution)/shard_map/ppermute | solution.py:595
  52.0 1.6 %collective-permute-done.13.got_second = f32[4,8,128]{2,1,0:T(8,128)S(1)} collective-permute-done((f32[4,8,128]{2,1,0:T(8,128)S(1)}, f32[4,8,128]{2,1,0:T(8,128)S(1)}, u32[]{:S(2)}, u32[]{:S(2)}) %collective-permute-start.13) | collective-permute-done | bytes 16416 | tf_op jit(solution)/shard_map/ppermute | solution.py:595
  53.9 0.7 collective-permute-start.15
  54.5 3.0 %collective-permute-done.14.got_first = f32[3,40,128]{2,1,0:T(8,128)S(1)} collective-permute-done((f32[3,40,128]{2,1,0:T(8,128)S(1)}, f32[3,40,128]{2,1,0:T(8,128)S(1)}, u32[]{:S(2)}, u32[]{:S(2)}) %collective-permute-start.14) | collective-permute-done | bytes 61472 | tf_op jit(solution)/shard_map/ppermute | solution.py:595
  57.7 2.4 %collective-permute-start.16 = (f32[8,512]{1,0:T(8,128)S(1)}, f32[8,512]{1,0:T(8,128)S(1)}, u32[]{:S(2)}, u32[]{:S(2)}) collective-permute-start(f32[8,512]{1,0:T(8,128)S(1)} %get-tuple-element.87), channel_id=1, source_target_pairs={{0,12},{4,8},{8,4},{12,0},{1,13},{5,9},{9,5},{13,1},{2,14},{6,10},... | collective-permute-start | bytes 49160 | tf_op jit(solution)/shard_map/ppermute | solution.py:595
  60.4 2.9 %hessian_middle.3.total = f32[80,512]{1,0:T(8,128)S(1)} custom-call(f32[80,512]{1,0:T(8,128)S(1)} %get-tuple-element.86.partial_rows, f32[80,512]{1,0:T(8,128)S(1)} %get-tuple-element.77.diag, f32[32,224,128]{2,1,0:T(8,128)S(1)} %get-tuple-element.78.weight, bf16[224,240]{1,0:T(8,128)(2,1)S(1)} %copy-done.3, bf16[2,80,336]{2,1,0:T(8,128)(2,1)S(1)} %copy-done.2, ...), custom_call_target="tpu_custom_call" | custom-call | flops 1000000000 | bytes 20000000 | tf_op jit(solution)/shard_map/hessian_middle/pallas_call | solution.py:605
  63.3 0.6 collective-permute-done.17.got_second
  63.9 1.1 %hessian.3 = (f32[80,512]{1,0:T(8,128)S(1)}, f32[80,512]{1,0:T(8,128)S(1)}, f32[3,4,40,128]{3,2,1,0:T(8,128)S(1)}, f32[32,16,128]{2,1,0:T(8,128)S(1)}) custom-call(f32[80,512]{1,0:T(8,128)S(1)} %get-tuple-element.86.partial_rows, f32[8,512]{1,0:T(8,128)S(1)} %collective-permute-done.16.got_first, f32[8,512]{1,0:T(8,128)S(1)} %collective-permute-done.17.got_second, ...), custom_call_target="tpu_custom_call" | custom-call | flops 1000000000 | bytes 20000000 | tf_op jit(solution)/shard_map/hessian/pallas_call | solution.py:605
  65.0 15.7 %all_to_all.5.slots = f32[32,16,128]{2,1,0:T(8,128)S(1)} all-to-all(f32[32,16,128]{2,1,0:T(8,128)S(1)} %get-tuple-element.91), channel_id=1, replica_groups=mesh['lon'=8,'lat'=4,'tm'=4] {'lon','lat'}, dimensions={0} | all-to-all | bytes 524288 | tf_op jit(solution)/shard_map/all_to_all | solution.py:638
  81.2 0.7 collective-permute-start.19
  81.9 1.4 %collective-permute-start.20 = (f32[8,128]{1,0:T(8,128)S(1)}, f32[8,128]{1,0:T(8,128)S(1)}, u32[]{:S(2)}, u32[]{:S(2)}) collective-permute-start(f32[8,128]{1,0:T(8,128)S(1)} %get-tuple-element.95._.lines), channel_id=1, source_target_pairs={{0,2},{1,3},{2,0},{3,1},{4,6},{5,7},{6,4},{7,5},{8,10},{9,11},{10,... | collective-permute-start | bytes 12296 | tf_op jit(solution)/shard_map/ppermute | solution.py:645
  83.8 1.7 %collective-permute-done.20.got_lines = f32[8,128]{1,0:T(8,128)S(1)} collective-permute-done((f32[8,128]{1,0:T(8,128)S(1)}, f32[8,128]{1,0:T(8,128)S(1)}, u32[]{:S(2)}, u32[]{:S(2)}) %collective-permute-start.20) | collective-permute-done | bytes 4128 | tf_op jit(solution)/shard_map/ppermute | solution.py:645
  85.5 1.0 %last.1 = (f32[8,32,64]{2,1,0:T(8,128)}, f32[8,32,64]{2,1,0:T(8,128)}) custom-call(f32[3,4,40,128]{3,2,1,0:T(8,128)S(1)} %get-tuple-element.92.tiles, f32[40,128]{1,0:T(8,128)S(1)} %collective-permute-done.18.got_first, f32[40,128]{1,0:T(8,128)S(1)} %collective-permute-done.19.got_second, f32[8,128]{1,0:T(8,128)S(1)} %get-tuple-element.95._.lines, ...), custom_call_target="tpu_custom_call" | custom-call | flops 1000000000 | bytes 20000000 | tf_op jit(solution)/shard_map/last/pallas_call | solution.py:605
  (47 shorter events, 3.5 us)
Async XLA Ops:
  1.8 9.1 %collective-permute-start = (f32[4,8,128]{2,1,0:T(8,128)S(1)}, f32[4,8,128]{2,1,0:T(8,128)S(1)}, u32[]{:S(2)}, u32[]{:S(2)}) collective-permute-start(f32[4,8,128]{2,1,0:T(8,128)S(1)} %get-tuple-element.55._), channel_id=1, source_target_pairs={{0,112},{16,32},{32,16},{48,64},{64,48},{80,96},{96,80},{112,0},{1... | collective-permute-start | bytes 49160 | tf_op jit(solution)/shard_map/ppermute | solution.py:595
  7.4 5.2 %collective-permute-start.1 = (f32[4,8,128]{2,1,0:T(8,128)S(1)}, f32[4,8,128]{2,1,0:T(8,128)S(1)}, u32[]{:S(2)}, u32[]{:S(2)}) collective-permute-start(f32[4,8,128]{2,1,0:T(8,128)S(1)} %get-tuple-element.56), channel_id=1, source_target_pairs={{0,16},{16,0},{32,48},{48,32},{64,80},{80,64},{96,112},{112,96},{1... | collective-permute-start | bytes 49160 | tf_op jit(solution)/shard_map/ppermute | solution.py:595
  12.6 8.1 %copy-start = (bf16[384,384]{1,0:T(8,128)(2,1)S(1)}, bf16[384,384]{1,0:T(8,128)(2,1)}, u32[]{:S(2)}) copy-start(bf16[384,384]{1,0:T(8,128)(2,1)} %constant.40.lon_up) | copy-start | bytes 884740
  12.6 8.1 %copy-start.1 = (bf16[384,256]{1,0:T(8,128)(2,1)S(1)}, bf16[384,256]{1,0:T(8,128)(2,1)}, u32[]{:S(2)}) copy-start(bf16[384,256]{1,0:T(8,128)(2,1)} %constant.43.lon_down) | copy-start | bytes 589828
  12.6 8.1 %copy-start.2 = (bf16[2,80,336]{2,1,0:T(8,128)(2,1)S(1)}, bf16[2,80,336]{2,1,0:T(8,128)(2,1)}, u32[]{:S(2)}) copy-start(bf16[2,80,336]{2,1,0:T(8,128)(2,1)} %constant.35.lat_down) | copy-start | bytes 322564
  12.6 8.1 %copy-start.3 = (bf16[224,240]{1,0:T(8,128)(2,1)S(1)}, bf16[224,240]{1,0:T(8,128)(2,1)}, u32[]{:S(2)}) copy-start(bf16[224,240]{1,0:T(8,128)(2,1)} %constant.30.lat_up) | copy-start | bytes 322564
  12.7 3.5 %collective-permute-start.2 = (f32[2,40,128]{2,1,0:T(8,128)S(1)}, f32[2,40,128]{2,1,0:T(8,128)S(1)}, u32[]{:S(2)}, u32[]{:S(2)}) collective-permute-start(f32[2,40,128]{2,1,0:T(8,128)S(1)} %get-tuple-element.59), channel_id=1, source_target_pairs={{0,3},{1,2},{2,1},{3,0},{4,7},{5,6},{6,5},{7,4},{8,11},{9,10},{10,... | collective-permute-start | bytes 122888 | tf_op jit(solution)/shard_map/ppermute | solution.py:595
  12.8 3.4 %collective-permute-start.3 = (f32[2,40,128]{2,1,0:T(8,128)S(1)}, f32[2,40,128]{2,1,0:T(8,128)S(1)}, u32[]{:S(2)}, u32[]{:S(2)}) collective-permute-start(f32[2,40,128]{2,1,0:T(8,128)S(1)} %get-tuple-element.60), channel_id=1, source_target_pairs={{0,1},{1,0},{2,3},{3,2},{4,5},{5,4},{6,7},{7,6},{8,9},{9,8},{10,11... | collective-permute-start | bytes 122888 | tf_op jit(solution)/shard_map/ppermute | solution.py:595
  16.5 8.4 %collective-permute-start.4 = (f32[8,512]{1,0:T(8,128)S(1)}, f32[8,512]{1,0:T(8,128)S(1)}, u32[]{:S(2)}, u32[]{:S(2)}) collective-permute-start(f32[8,512]{1,0:T(8,128)S(1)} %get-tuple-element.62), channel_id=1, source_target_pairs={{0,12},{4,8},{8,4},{12,0},{1,13},{5,9},{9,5},{13,1},{2,14},{6,10},... | collective-permute-start | bytes 49160 | tf_op jit(solution)/shard_map/ppermute | solution.py:595
  20.6 4.3 %collective-permute-start.5 = (f32[8,512]{1,0:T(8,128)S(1)}, f32[8,512]{1,0:T(8,128)S(1)}, u32[]{:S(2)}, u32[]{:S(2)}) collective-permute-start(f32[8,512]{1,0:T(8,128)S(1)} %get-tuple-element.63), channel_id=1, source_target_pairs={{0,4},{4,0},{8,12},{12,8},{1,5},{5,1},{9,13},{13,9},{2,6},{6,2},{1... | collective-permute-start | bytes 49160 | tf_op jit(solution)/shard_map/ppermute | solution.py:595
  20.8 4.3 %copy-start.4 = (bf16[1,80,96]{2,1,0:T(8,128)(2,1)S(1)}, bf16[1,80,96]{2,1,0:T(8,128)(2,1)}, u32[]{:S(2)}) copy-start(bf16[1,80,96]{2,1,0:T(8,128)(2,1)} %constant.55.lat_down) | copy-start | bytes 46084
  20.8 4.2 %copy-start.5 = (bf16[32,240]{1,0:T(8,128)(2,1)S(1)}, bf16[32,240]{1,0:T(8,128)(2,1)}, u32[]{:S(2)}) copy-start(bf16[32,240]{1,0:T(8,128)(2,1)} %constant.50.lat_up) | copy-start | bytes 46084
  26.3 7.4 %collective-permute-start.6 = (f32[4,8,128]{2,1,0:T(8,128)S(1)}, f32[4,8,128]{2,1,0:T(8,128)S(1)}, u32[]{:S(2)}, u32[]{:S(2)}) collective-permute-start(f32[4,8,128]{2,1,0:T(8,128)S(1)} %get-tuple-element.69), channel_id=1, source_target_pairs={{0,112},{16,32},{32,16},{48,64},{64,48},{80,96},{96,80},{112,0},{1... | collective-permute-start | bytes 49160 | tf_op jit(solution)/shard_map/ppermute | solution.py:595
  28.8 5.2 %collective-permute-start.7 = (f32[4,8,128]{2,1,0:T(8,128)S(1)}, f32[4,8,128]{2,1,0:T(8,128)S(1)}, u32[]{:S(2)}, u32[]{:S(2)}) collective-permute-start(f32[4,8,128]{2,1,0:T(8,128)S(1)} %get-tuple-element.70), channel_id=1, source_target_pairs={{0,16},{16,0},{32,48},{48,32},{64,80},{80,64},{96,112},{112,96},{1... | collective-permute-start | bytes 49160 | tf_op jit(solution)/shard_map/ppermute | solution.py:595
  34.3 3.7 %collective-permute-start.8 = (f32[3,40,128]{2,1,0:T(8,128)S(1)}, f32[3,40,128]{2,1,0:T(8,128)S(1)}, u32[]{:S(2)}, u32[]{:S(2)}) collective-permute-start(f32[3,40,128]{2,1,0:T(8,128)S(1)} %get-tuple-element.72), channel_id=1, source_target_pairs={{0,3},{1,2},{2,1},{3,0},{4,7},{5,6},{6,5},{7,4},{8,11},{9,10},{10,... | collective-permute-start | bytes 184328 | tf_op jit(solution)/shard_map/ppermute | solution.py:595
  34.4 3.6 %collective-permute-start.9 = (f32[3,40,128]{2,1,0:T(8,128)S(1)}, f32[3,40,128]{2,1,0:T(8,128)S(1)}, u32[]{:S(2)}, u32[]{:S(2)}) collective-permute-start(f32[3,40,128]{2,1,0:T(8,128)S(1)} %get-tuple-element.73), channel_id=1, source_target_pairs={{0,1},{1,0},{2,3},{3,2},{4,5},{5,4},{6,7},{7,6},{8,9},{9,8},{10,11... | collective-permute-start | bytes 184328 | tf_op jit(solution)/shard_map/ppermute | solution.py:595
  38.2 5.3 %collective-permute-start.10 = (f32[8,512]{1,0:T(8,128)S(1)}, f32[8,512]{1,0:T(8,128)S(1)}, u32[]{:S(2)}, u32[]{:S(2)}) collective-permute-start(f32[8,512]{1,0:T(8,128)S(1)} %get-tuple-element.75), channel_id=1, source_target_pairs={{0,12},{4,8},{8,4},{12,0},{1,13},{5,9},{9,5},{13,1},{2,14},{6,10},... | collective-permute-start | bytes 49160 | tf_op jit(solution)/shard_map/ppermute | solution.py:595
  38.9 4.6 %collective-permute-start.11 = (f32[8,512]{1,0:T(8,128)S(1)}, f32[8,512]{1,0:T(8,128)S(1)}, u32[]{:S(2)}, u32[]{:S(2)}) collective-permute-start(f32[8,512]{1,0:T(8,128)S(1)} %get-tuple-element.76), channel_id=1, source_target_pairs={{0,4},{4,0},{8,12},{12,8},{1,5},{5,1},{9,13},{13,9},{2,6},{6,2},{1... | collective-permute-start | bytes 49160 | tf_op jit(solution)/shard_map/ppermute | solution.py:595
  44.6 7.4 %collective-permute-start.12 = (f32[4,8,128]{2,1,0:T(8,128)S(1)}, f32[4,8,128]{2,1,0:T(8,128)S(1)}, u32[]{:S(2)}, u32[]{:S(2)}) collective-permute-start(f32[4,8,128]{2,1,0:T(8,128)S(1)} %get-tuple-element.81), channel_id=1, source_target_pairs={{0,112},{16,32},{32,16},{48,64},{64,48},{80,96},{96,80},{112,0},{1... | collective-permute-start | bytes 49160 | tf_op jit(solution)/shard_map/ppermute | solution.py:595
  48.4 5.2 %collective-permute-start.13 = (f32[4,8,128]{2,1,0:T(8,128)S(1)}, f32[4,8,128]{2,1,0:T(8,128)S(1)}, u32[]{:S(2)}, u32[]{:S(2)}) collective-permute-start(f32[4,8,128]{2,1,0:T(8,128)S(1)} %get-tuple-element.82), channel_id=1, source_target_pairs={{0,16},{16,0},{32,48},{48,32},{64,80},{80,64},{96,112},{112,96},{1... | collective-permute-start | bytes 49160 | tf_op jit(solution)/shard_map/ppermute | solution.py:595
  53.8 3.7 %collective-permute-start.14 = (f32[3,40,128]{2,1,0:T(8,128)S(1)}, f32[3,40,128]{2,1,0:T(8,128)S(1)}, u32[]{:S(2)}, u32[]{:S(2)}) collective-permute-start(f32[3,40,128]{2,1,0:T(8,128)S(1)} %get-tuple-element.84), channel_id=1, source_target_pairs={{0,3},{1,2},{2,1},{3,0},{4,7},{5,6},{6,5},{7,4},{8,11},{9,10},{10,... | collective-permute-start | bytes 184328 | tf_op jit(solution)/shard_map/ppermute | solution.py:595
  53.9 3.6 %collective-permute-start.15 = (f32[3,40,128]{2,1,0:T(8,128)S(1)}, f32[3,40,128]{2,1,0:T(8,128)S(1)}, u32[]{:S(2)}, u32[]{:S(2)}) collective-permute-start(f32[3,40,128]{2,1,0:T(8,128)S(1)} %get-tuple-element.85), channel_id=1, source_target_pairs={{0,1},{1,0},{2,3},{3,2},{4,5},{5,4},{6,7},{7,6},{8,9},{9,8},{10,11... | collective-permute-start | bytes 184328 | tf_op jit(solution)/shard_map/ppermute | solution.py:595
  57.7 5.6 %collective-permute-start.16 = (f32[8,512]{1,0:T(8,128)S(1)}, f32[8,512]{1,0:T(8,128)S(1)}, u32[]{:S(2)}, u32[]{:S(2)}) collective-permute-start(f32[8,512]{1,0:T(8,128)S(1)} %get-tuple-element.87), channel_id=1, source_target_pairs={{0,12},{4,8},{8,4},{12,0},{1,13},{5,9},{9,5},{13,1},{2,14},{6,10},... | collective-permute-start | bytes 49160 | tf_op jit(solution)/shard_map/ppermute | solution.py:595
  60.2 3.7 %collective-permute-start.17 = (f32[8,512]{1,0:T(8,128)S(1)}, f32[8,512]{1,0:T(8,128)S(1)}, u32[]{:S(2)}, u32[]{:S(2)}) collective-permute-start(f32[8,512]{1,0:T(8,128)S(1)} %get-tuple-element.88), channel_id=1, source_target_pairs={{0,4},{4,0},{8,12},{12,8},{1,5},{5,1},{9,13},{13,9},{2,6},{6,2},{1... | collective-permute-start | bytes 49160 | tf_op jit(solution)/shard_map/ppermute | solution.py:595
  81.1 4.4 %collective-permute-start.18 = (f32[40,128]{1,0:T(8,128)S(1)}, f32[40,128]{1,0:T(8,128)S(1)}, u32[]{:S(2)}, u32[]{:S(2)}) collective-permute-start(f32[40,128]{1,0:T(8,128)S(1)} %get-tuple-element.93), channel_id=1, source_target_pairs={{0,3},{1,2},{2,1},{3,0},{4,7},{5,6},{6,5},{7,4},{8,11},{9,10},{10,... | collective-permute-start | bytes 61448 | tf_op jit(solution)/shard_map/ppermute | solution.py:595
  81.2 4.4 %collective-permute-start.19 = (f32[40,128]{1,0:T(8,128)S(1)}, f32[40,128]{1,0:T(8,128)S(1)}, u32[]{:S(2)}, u32[]{:S(2)}) collective-permute-start(f32[40,128]{1,0:T(8,128)S(1)} %get-tuple-element.94), channel_id=1, source_target_pairs={{0,1},{1,0},{2,3},{3,2},{4,5},{5,4},{6,7},{7,6},{8,9},{9,8},{10,11... | collective-permute-start | bytes 61448 | tf_op jit(solution)/shard_map/ppermute | solution.py:595
  81.9 3.6 %collective-permute-start.20 = (f32[8,128]{1,0:T(8,128)S(1)}, f32[8,128]{1,0:T(8,128)S(1)}, u32[]{:S(2)}, u32[]{:S(2)}) collective-permute-start(f32[8,128]{1,0:T(8,128)S(1)} %get-tuple-element.95._.lines), channel_id=1, source_target_pairs={{0,2},{1,3},{2,0},{3,1},{4,6},{5,7},{6,4},{7,5},{8,10},{9,11},{10,... | collective-permute-start | bytes 12296 | tf_op jit(solution)/shard_map/ppermute | solution.py:645

commit v5 on v4

--- a/solution.py
+++ b/solution.py
@@ -311,8 +311,21 @@
         copy.wait()
 
 
-def start_middle_kernel(both, area, offset, precip, lat_up, lat_down, lon_up, lon_down, weight, total, *scratch):
-    w_of = start_of(area, offset, precip, weight)
+def offset_kernel(_, area, offset, precip, rate, loss):
+    def hour(h, carry):
+        rate[h] = area[...] * jnp.exp((2.0 - tweedie_power) * offset[h])
+        loss[h] = area[...] * precip[h] * jnp.exp((1.0 - tweedie_power) * offset[h])
+        return carry
+
+    lax.fori_loop(0, HOURS, hour, 0)
+
+
+def start_middle_kernel(both, rate, loss, lat_up, lat_down, lon_up, lon_down, weight, total, *scratch):
+    def w_of(hour, rows, value):
+        w = rate[hour, rows, :] * jnp.exp((2.0 - tweedie_power) * value)
+        weight[hour, rows, :] = w
+        return w - loss[hour, rows, :] * jnp.exp((1.0 - tweedie_power) * value)
+
     total[...] = apply_cells(both[0], w_of, lat_up, lat_down, lon_up, lon_down, *scratch)
 
 
@@ -527,7 +540,7 @@
         first[i], second[i] = place.messages("tm", beside(0, 2 + i), beside(2, i))
 
 
-def embed_turn_kernel(tiles, got_first, got_second, rows, first, second):
+def embed_turn_kernel(tiles, got_first, got_second, _, rows, first, second):
     place = Place()
     lane = lax.broadcasted_iota(jnp.int32, (SEG, 128), 1)
     own = (lane >= 2) & (lane < LAT_OWN + 2)
@@ -646,7 +659,7 @@
     return tiles, first, second, lines, got_lines
 
 
-def expand(coefficients, inverse_diag, offset, precip):
+def expand(coefficients, inverse_diag, offset, precip, area):
     tiles, message = shaped(2, *TILES), shaped(4, 8, 128)
     tiles_here, first, second = call(
         embed_kernel, (tiles, message, message), "embed", jnp.stack([coefficients, inverse_diag])
@@ -658,10 +671,11 @@
     first, second = swap(first, second, "lon")
     message = shaped(2, SEG, 128)
     tiles_here, first, second = call(embed_join_kernel, (tiles, message, message), "embed_join", tiles_here, first, second, cells[2])
+    shares = call(offset_kernel, (shaped(*MID), shaped(*MID)), "offset", first, middle(area), *cells[:2])
     first, second = swap(first, second, "tm")
     shapes = (shaped(2, *VECTOR), shaped(*LAT_MESSAGE), shaped(*LAT_MESSAGE))
-    both, first, second = call(embed_turn_kernel, shapes, "embed_turn", tiles_here, first, second)
-    return both, *swap(first, second, "lat"), cells
+    both, first, second = call(embed_turn_kernel, shapes, "embed_turn", tiles_here, first, second, shares[0])
+    return both, *swap(first, second, "lat"), cells, shares
 
 
 def per_device(precip, offset, coefficients, inverse_diag):
@@ -673,9 +687,9 @@
     ends = (shaped(*TILES), shaped(*LON_MESSAGE), shaped(*LON_MESSAGE))
     vector = shaped(*VECTOR)
 
-    both, *got, cells = expand(coefficients.transpose(0, 2, 1), inverse_diag.transpose(0, 2, 1), offset, precip)
+    both, *got, cells, shares = expand(coefficients.transpose(0, 2, 1), inverse_diag.transpose(0, 2, 1), offset, precip, area)
     weight, total = call(
-        start_middle_kernel, (shaped(*MID), vector), "start_middle", both, middle(area), *cells[:2], *mid_tabs, scratch=MID_SCRATCH
+        start_middle_kernel, (shaped(*MID), vector), "start_middle", both, *shares, *mid_tabs, scratch=MID_SCRATCH
     )
     edge_weight, diag, *sent = call(
         start_kernel, (shaped(*ENDS), vector, *ends), "start", both, *got, total, edges(area), *cells[2:],

time: 86.7 us -> 86.5 us (level)
  waiting for transfers between devices: 22.3 us -> 20.7 us
  Pallas kernels: 19.9 us -> 21.2 us
    ppermute x10, waiting for transfers between devices: 16.4 us -> 14.9 us  [swap(): lax.ppermute(first, axis, first_pairs)]
    pallas_call x17 -> x18, Pallas kernels: 19.9 us -> 21.2 us  [call(): pl.pallas_call(kernel, in_specs=[hbm if i in far else vmem for i in range...]
  transfers between devices with their start and end apart: 21 -> 21, of which waited for: 10 -> 10; matrix products, arithmetic and copies ran while one was open for 0% -> 0% of each run, Pallas kernels for 16% -> 17%
where the time goes in v5:
time: 86.5 us; the launch traced here: 86.3 us
  starting transfers between devices  26.2 us (30%)
  Pallas kernels  21.2 us (25%)
  waiting for transfers between devices  20.7 us (24%)
  blocking collectives  15.8 us (18%)
  other arithmetic  1.12 us (1%)
  between operations  0.91 us (1%)
    pallas_call x18, Pallas kernels, call(): pl.pallas_call(kernel, in_specs=[hbm if i in far else vmem for i in range...  21.2 us
    ppermute x10, starting transfers between devices, swap(): lax.ppermute(first, axis, first_pairs)  19.8 us
    all_to_all x1, blocking collectives, fold_and_sum(): slots = lax.all_to_all(slots, ('lon', 'lat'), 0, 0, tiled=True)  15.8 us
    ppermute x10, waiting for transfers between devices, swap(): lax.ppermute(first, axis, first_pairs)  14.9 us
    ppermute x10, starting transfers between devices, swap(): lax.ppermute(second, axis, second_pairs)  5.07 us
    ppermute x10, waiting for transfers between devices, swap(): lax.ppermute(second, axis, second_pairs)  4.03 us
  transfers between devices with their start and end apart: 21, of which 10 were waited for; matrix products, arithmetic and copies ran while one was open for 0% of the time, Pallas kernels for 17%

profile of v5, /device:TPU:0, one launch (start us, length us, event | category | flops | bytes accessed | tf_op | source)
XLA Modules:
  0.0 86.3 jit_solution(947663175183105472)
XLA Ops:
  0.6 1.0 %pad_maximum_fusion.own_both = f32[2,8,32,64]{3,2,1,0:T(8,128)S(1)} fusion(f32[1,8,32,64]{3,2,1,0:T(8,128)} %bitcast.13, f32[1,8,32,64]{3,2,1,0:T(8,128)} %bitcast.14), kind=kLoop, calls=%fused_computation | loop fusion | flops 32768 | bytes 262144 | tf_op jit(solution)/shard_map/stack | solution.py:665
  1.8 5.6 %collective-permute-start = (f32[4,8,128]{2,1,0:T(8,128)S(1)}, f32[4,8,128]{2,1,0:T(8,128)S(1)}, u32[]{:S(2)}, u32[]{:S(2)}) collective-permute-start(f32[4,8,128]{2,1,0:T(8,128)S(1)} %get-tuple-element.57._), channel_id=1, source_target_pairs={{0,112},{16,32},{32,16},{48,64},{64,48},{80,96},{96,80},{112,0},{1... | collective-permute-start | bytes 49160 | tf_op jit(solution)/shard_map/ppermute | solution.py:608
  7.6 3.4 %load.1 = (f32[32,224,128]{2,1,0:T(8,128)S(1)}, f32[32,224,128]{2,1,0:T(8,128)S(1)}, f32[32,32,128]{2,1,0:T(8,128)S(1)}, f32[32,32,128]{2,1,0:T(8,128)S(1)}) custom-call(f32[4,8,128]{2,1,0:T(8,128)S(1)} %get-tuple-element.57._, f32[32,256,128]{2,1,0:T(8,128)} %offset_far.1, f32[32,256,128]{2,1,0:T(8,128)} %precip_far.1), custom_call_target="tpu_custom_call" | custom-call | flops 1000000000 | bytes 20000000 | tf_op jit(solution)/shard_map/load/pallas_call | solution.py:618
  11.1 1.5 %collective-permute-done.1.got_second = f32[4,8,128]{2,1,0:T(8,128)S(1)} collective-permute-done((f32[4,8,128]{2,1,0:T(8,128)S(1)}, f32[4,8,128]{2,1,0:T(8,128)S(1)}, u32[]{:S(2)}, u32[]{:S(2)}) %collective-permute-start.1) | collective-permute-done | bytes 16416 | tf_op jit(solution)/shard_map/ppermute | solution.py:608
  12.8 0.8 collective-permute-start.3
  13.7 1.5 %offset.1 = (f32[32,224,128]{2,1,0:T(8,128)S(1)}, f32[32,224,128]{2,1,0:T(8,128)S(1)}) custom-call(f32[2,40,128]{2,1,0:T(8,128)S(1)} %get-tuple-element.61._, f32[224,128]{1,0:T(8,128)S(1)} %broadcast_in_dim.10.area, f32[32,224,128]{2,1,0:T(8,128)S(1)} %get-tuple-element.63.offset, f32[32,224,128]{2,1,0:T(8,128)S(1)} %get-tuple-element.64.precip), custom_call_target="tpu_custom_call" | custom-call | flops 1000000000 | bytes 20000000 | tf_op jit(solution)/shard_map/offset/pallas_call | solution.py:618
  15.2 1.0 %collective-permute-done.2.got_first = f32[2,40,128]{2,1,0:T(8,128)S(1)} collective-permute-done((f32[2,40,128]{2,1,0:T(8,128)S(1)}, f32[2,40,128]{2,1,0:T(8,128)S(1)}, u32[]{:S(2)}, u32[]{:S(2)}) %collective-permute-start.2) | collective-permute-done | bytes 40992 | tf_op jit(solution)/shard_map/ppermute | solution.py:608
  16.5 4.1 %collective-permute-start.4 = (f32[8,512]{1,0:T(8,128)S(1)}, f32[8,512]{1,0:T(8,128)S(1)}, u32[]{:S(2)}, u32[]{:S(2)}) collective-permute-start(f32[8,512]{1,0:T(8,128)S(1)} %get-tuple-element.67), channel_id=1, source_target_pairs={{0,12},{4,8},{8,4},{12,0},{1,13},{5,9},{9,5},{13,1},{2,14},{6,10},... | collective-permute-start | bytes 49160 | tf_op jit(solution)/shard_map/ppermute | solution.py:608
  20.7 3.9 %start_middle.1 = (f32[32,224,128]{2,1,0:T(8,128)S(1)}, f32[80,512]{1,0:T(8,128)S(1)}) custom-call(f32[2,80,512]{2,1,0:T(8,128)S(1)} %get-tuple-element.66.both, f32[32,224,128]{2,1,0:T(8,128)S(1)} %get-tuple-element.65._.rate, f32[32,224,128]{2,1,0:T(8,128)S(1)} %get-tuple-element.69.loss, bf16[224,240]{1,0:T(8,128)(2,1)S(1)} %copy-done.3, ...), custom_call_target="tpu_custom_call" | custom-call | flops 1000000000 | bytes 20000000 | tf_op jit(solution)/shard_map/start_middle/pallas_call | solution.py:618
  24.7 1.3 %start.1 = (f32[32,32,128]{2,1,0:T(8,128)S(1)}, f32[80,512]{1,0:T(8,128)S(1)}, f32[3,4,40,128]{3,2,1,0:T(8,128)S(1)}, f32[4,8,128]{2,1,0:T(8,128)S(1)}, f32[4,8,128]{2,1,0:T(8,128)S(1)}) custom-call(f32[2,80,512]{2,1,0:T(8,128)S(1)} %get-tuple-element.66.both, f32[8,512]{1,0:T(8,128)S(1)} %collective-permute-done.4.got_first, ...), custom_call_target="tpu_custom_call" | custom-call | flops 1000000000 | bytes 20000000 | tf_op jit(solution)/shard_map/start/pallas_call | solution.py:618
  26.0 2.6 %collective-permute-start.6 = (f32[4,8,128]{2,1,0:T(8,128)S(1)}, f32[4,8,128]{2,1,0:T(8,128)S(1)}, u32[]{:S(2)}, u32[]{:S(2)}) collective-permute-start(f32[4,8,128]{2,1,0:T(8,128)S(1)} %get-tuple-element.73), channel_id=1, source_target_pairs={{0,112},{16,32},{32,16},{48,64},{64,48},{80,96},{96,80},{112,0},{1... | collective-permute-start | bytes 49160 | tf_op jit(solution)/shard_map/ppermute | solution.py:608
  28.6 4.8 %collective-permute-done.6.got_first = f32[4,8,128]{2,1,0:T(8,128)S(1)} collective-permute-done((f32[4,8,128]{2,1,0:T(8,128)S(1)}, f32[4,8,128]{2,1,0:T(8,128)S(1)}, u32[]{:S(2)}, u32[]{:S(2)}) %collective-permute-start.6) | collective-permute-done | bytes 16416 | tf_op jit(solution)/shard_map/ppermute | solution.py:608
  34.1 0.7 collective-permute-start.9
  34.8 2.9 %collective-permute-done.8.got_first = f32[3,40,128]{2,1,0:T(8,128)S(1)} collective-permute-done((f32[3,40,128]{2,1,0:T(8,128)S(1)}, f32[3,40,128]{2,1,0:T(8,128)S(1)}, u32[]{:S(2)}, u32[]{:S(2)}) %collective-permute-start.8) | collective-permute-done | bytes 61472 | tf_op jit(solution)/shard_map/ppermute | solution.py:608
  38.0 1.0 %collective-permute-start.10 = (f32[8,512]{1,0:T(8,128)S(1)}, f32[8,512]{1,0:T(8,128)S(1)}, u32[]{:S(2)}, u32[]{:S(2)}) collective-permute-start(f32[8,512]{1,0:T(8,128)S(1)} %get-tuple-element.79), channel_id=1, source_target_pairs={{0,12},{4,8},{8,4},{12,0},{1,13},{5,9},{9,5},{13,1},{2,14},{6,10},... | collective-permute-start | bytes 49160 | tf_op jit(solution)/shard_map/ppermute | solution.py:608
  39.0 1.3 %collective-permute-start.11 = (f32[8,512]{1,0:T(8,128)S(1)}, f32[8,512]{1,0:T(8,128)S(1)}, u32[]{:S(2)}, u32[]{:S(2)}) collective-permute-start(f32[8,512]{1,0:T(8,128)S(1)} %get-tuple-element.80), channel_id=1, source_target_pairs={{0,4},{4,0},{8,12},{12,8},{1,5},{5,1},{9,13},{13,9},{2,6},{6,2},{1... | collective-permute-start | bytes 49160 | tf_op jit(solution)/shard_map/ppermute | solution.py:608
  40.4 2.9 %hessian_middle.2.total = f32[80,512]{1,0:T(8,128)S(1)} custom-call(f32[80,512]{1,0:T(8,128)S(1)} %get-tuple-element.78.partial_rows, f32[80,512]{1,0:T(8,128)S(1)} %get-tuple-element.81.diag, f32[32,224,128]{2,1,0:T(8,128)S(1)} %get-tuple-element.82.weight, bf16[224,240]{1,0:T(8,128)(2,1)S(1)} %copy-done.3, bf16[2,80,336]{2,1,0:T(8,128)(2,1)S(1)} %copy-done.2, ...), custom_call_target="tpu_custom_call" | custom-call | flops 1000000000 | bytes 20000000 | tf_op jit(solution)/shard_map/hessian_middle/pallas_call | solution.py:618
  43.3 1.1 %hessian.2 = (f32[80,512]{1,0:T(8,128)S(1)}, f32[80,512]{1,0:T(8,128)S(1)}, f32[3,4,40,128]{3,2,1,0:T(8,128)S(1)}, f32[4,8,128]{2,1,0:T(8,128)S(1)}, f32[4,8,128]{2,1,0:T(8,128)S(1)}, /*index=5*/f32[8,128]{1,0:T(8,128)S(1)}) custom-call(f32[80,512]{1,0:T(8,128)S(1)} %get-tuple-element.78.partial_rows, f32[8,512]{1,0:T(8,128)S(1)} %collective-permute-done.10.got_first, ...), custom_call_target="tpu_custom_call" | custom-call | flops 1000000000 | bytes 20000000 | tf_op jit(solution)/shard_map/hessian/pallas_call | solution.py:618
  44.4 3.6 %collective-permute-start.12 = (f32[4,8,128]{2,1,0:T(8,128)S(1)}, f32[4,8,128]{2,1,0:T(8,128)S(1)}, u32[]{:S(2)}, u32[]{:S(2)}) collective-permute-start(f32[4,8,128]{2,1,0:T(8,128)S(1)} %get-tuple-element.85), channel_id=1, source_target_pairs={{0,112},{16,32},{32,16},{48,64},{64,48},{80,96},{96,80},{112,0},{1... | collective-permute-start | bytes 49160 | tf_op jit(solution)/shard_map/ppermute | solution.py:608
  48.6 3.2 %collective-permute-done.12.got_first = f32[4,8,128]{2,1,0:T(8,128)S(1)} collective-permute-done((f32[4,8,128]{2,1,0:T(8,128)S(1)}, f32[4,8,128]{2,1,0:T(8,128)S(1)}, u32[]{:S(2)}, u32[]{:S(2)}) %collective-permute-start.12) | collective-permute-done | bytes 16416 | tf_op jit(solution)/shard_map/ppermute | solution.py:608
  51.8 1.4 %collective-permute-done.13.got_second = f32[4,8,128]{2,1,0:T(8,128)S(1)} collective-permute-done((f32[4,8,128]{2,1,0:T(8,128)S(1)}, f32[4,8,128]{2,1,0:T(8,128)S(1)}, u32[]{:S(2)}, u32[]{:S(2)}) %collective-permute-start.13) | collective-permute-done | bytes 16416 | tf_op jit(solution)/shard_map/ppermute | solution.py:608
  53.5 0.7 collective-permute-start.15
  54.2 3.0 %collective-permute-done.14.got_first = f32[3,40,128]{2,1,0:T(8,128)S(1)} collective-permute-done((f32[3,40,128]{2,1,0:T(8,128)S(1)}, f32[3,40,128]{2,1,0:T(8,128)S(1)}, u32[]{:S(2)}, u32[]{:S(2)}) %collective-permute-start.14) | collective-permute-done | bytes 61472 | tf_op jit(solution)/shard_map/ppermute | solution.py:608
  57.4 2.4 %collective-permute-start.16 = (f32[8,512]{1,0:T(8,128)S(1)}, f32[8,512]{1,0:T(8,128)S(1)}, u32[]{:S(2)}, u32[]{:S(2)}) collective-permute-start(f32[8,512]{1,0:T(8,128)S(1)} %get-tuple-element.91), channel_id=1, source_target_pairs={{0,12},{4,8},{8,4},{12,0},{1,13},{5,9},{9,5},{13,1},{2,14},{6,10},... | collective-permute-start | bytes 49160 | tf_op jit(solution)/shard_map/ppermute | solution.py:608
  60.1 2.9 %hessian_middle.3.total = f32[80,512]{1,0:T(8,128)S(1)} custom-call(f32[80,512]{1,0:T(8,128)S(1)} %get-tuple-element.90.partial_rows, f32[80,512]{1,0:T(8,128)S(1)} %get-tuple-element.81.diag, f32[32,224,128]{2,1,0:T(8,128)S(1)} %get-tuple-element.82.weight, bf16[224,240]{1,0:T(8,128)(2,1)S(1)} %copy-done.3, bf16[2,80,336]{2,1,0:T(8,128)(2,1)S(1)} %copy-done.2, ...), custom_call_target="tpu_custom_call" | custom-call | flops 1000000000 | bytes 20000000 | tf_op jit(solution)/shard_map/hessian_middle/pallas_call | solution.py:618
  63.0 0.6 collective-permute-done.17.got_second
  63.6 1.1 %hessian.3 = (f32[80,512]{1,0:T(8,128)S(1)}, f32[80,512]{1,0:T(8,128)S(1)}, f32[3,4,40,128]{3,2,1,0:T(8,128)S(1)}, f32[32,16,128]{2,1,0:T(8,128)S(1)}) custom-call(f32[80,512]{1,0:T(8,128)S(1)} %get-tuple-element.90.partial_rows, f32[8,512]{1,0:T(8,128)S(1)} %collective-permute-done.16.got_first, f32[8,512]{1,0:T(8,128)S(1)} %collective-permute-done.17.got_second, ...), custom_call_target="tpu_custom_call" | custom-call | flops 1000000000 | bytes 20000000 | tf_op jit(solution)/shard_map/hessian/pallas_call | solution.py:618
  64.7 15.8 %all_to_all.5.slots = f32[32,16,128]{2,1,0:T(8,128)S(1)} all-to-all(f32[32,16,128]{2,1,0:T(8,128)S(1)} %get-tuple-element.95), channel_id=1, replica_groups=mesh['lon'=8,'lat'=4,'tm'=4] {'lon','lat'}, dimensions={0} | all-to-all | bytes 524288 | tf_op jit(solution)/shard_map/all_to_all | solution.py:651
  80.9 0.7 collective-permute-start.19
  81.7 1.4 %collective-permute-start.20 = (f32[8,128]{1,0:T(8,128)S(1)}, f32[8,128]{1,0:T(8,128)S(1)}, u32[]{:S(2)}, u32[]{:S(2)}) collective-permute-start(f32[8,128]{1,0:T(8,128)S(1)} %get-tuple-element.99._.lines), channel_id=1, source_target_pairs={{0,2},{1,3},{2,0},{3,1},{4,6},{5,7},{6,4},{7,5},{8,10},{9,11},{10,... | collective-permute-start | bytes 12296 | tf_op jit(solution)/shard_map/ppermute | solution.py:658
  83.5 1.7 %collective-permute-done.20.got_lines = f32[8,128]{1,0:T(8,128)S(1)} collective-permute-done((f32[8,128]{1,0:T(8,128)S(1)}, f32[8,128]{1,0:T(8,128)S(1)}, u32[]{:S(2)}, u32[]{:S(2)}) %collective-permute-start.20) | collective-permute-done | bytes 4128 | tf_op jit(solution)/shard_map/ppermute | solution.py:658
  85.3 1.0 %last.1 = (f32[8,32,64]{2,1,0:T(8,128)}, f32[8,32,64]{2,1,0:T(8,128)}) custom-call(f32[3,4,40,128]{3,2,1,0:T(8,128)S(1)} %get-tuple-element.96.tiles, f32[40,128]{1,0:T(8,128)S(1)} %collective-permute-done.18.got_first, f32[40,128]{1,0:T(8,128)S(1)} %collective-permute-done.19.got_second, f32[8,128]{1,0:T(8,128)S(1)} %get-tuple-element.99._.lines, ...), custom_call_target="tpu_custom_call" | custom-call | flops 1000000000 | bytes 20000000 | tf_op jit(solution)/shard_map/last/pallas_call | solution.py:618
  (48 shorter events, 4.2 us)
Async XLA Ops:
  1.8 9.3 %collective-permute-start = (f32[4,8,128]{2,1,0:T(8,128)S(1)}, f32[4,8,128]{2,1,0:T(8,128)S(1)}, u32[]{:S(2)}, u32[]{:S(2)}) collective-permute-start(f32[4,8,128]{2,1,0:T(8,128)S(1)} %get-tuple-element.57._), channel_id=1, source_target_pairs={{0,112},{16,32},{32,16},{48,64},{64,48},{80,96},{96,80},{112,0},{1... | collective-permute-start | bytes 49160 | tf_op jit(solution)/shard_map/ppermute | solution.py:608
  7.4 5.2 %collective-permute-start.1 = (f32[4,8,128]{2,1,0:T(8,128)S(1)}, f32[4,8,128]{2,1,0:T(8,128)S(1)}, u32[]{:S(2)}, u32[]{:S(2)}) collective-permute-start(f32[4,8,128]{2,1,0:T(8,128)S(1)} %get-tuple-element.58), channel_id=1, source_target_pairs={{0,16},{16,0},{32,48},{48,32},{64,80},{80,64},{96,112},{112,96},{1... | collective-permute-start | bytes 49160 | tf_op jit(solution)/shard_map/ppermute | solution.py:608
  12.7 3.5 %collective-permute-start.2 = (f32[2,40,128]{2,1,0:T(8,128)S(1)}, f32[2,40,128]{2,1,0:T(8,128)S(1)}, u32[]{:S(2)}, u32[]{:S(2)}) collective-permute-start(f32[2,40,128]{2,1,0:T(8,128)S(1)} %get-tuple-element.61._), channel_id=1, source_target_pairs={{0,3},{1,2},{2,1},{3,0},{4,7},{5,6},{6,5},{7,4},{8,11},{9,10},{10,... | collective-permute-start | bytes 122888 | tf_op jit(solution)/shard_map/ppermute | solution.py:608
  12.8 3.4 %collective-permute-start.3 = (f32[2,40,128]{2,1,0:T(8,128)S(1)}, f32[2,40,128]{2,1,0:T(8,128)S(1)}, u32[]{:S(2)}, u32[]{:S(2)}) collective-permute-start(f32[2,40,128]{2,1,0:T(8,128)S(1)} %get-tuple-element.62), channel_id=1, source_target_pairs={{0,1},{1,0},{2,3},{3,2},{4,5},{5,4},{6,7},{7,6},{8,9},{9,8},{10,11... | collective-permute-start | bytes 122888 | tf_op jit(solution)/shard_map/ppermute | solution.py:608
  15.2 5.5 %copy-start = (bf16[384,384]{1,0:T(8,128)(2,1)S(1)}, bf16[384,384]{1,0:T(8,128)(2,1)}, u32[]{:S(2)}) copy-start(bf16[384,384]{1,0:T(8,128)(2,1)} %constant.40.lon_up) | copy-start | bytes 884740
  15.2 5.5 %copy-start.1 = (bf16[384,256]{1,0:T(8,128)(2,1)S(1)}, bf16[384,256]{1,0:T(8,128)(2,1)}, u32[]{:S(2)}) copy-start(bf16[384,256]{1,0:T(8,128)(2,1)} %constant.43.lon_down) | copy-start | bytes 589828
  15.2 5.5 %copy-start.2 = (bf16[2,80,336]{2,1,0:T(8,128)(2,1)S(1)}, bf16[2,80,336]{2,1,0:T(8,128)(2,1)}, u32[]{:S(2)}) copy-start(bf16[2,80,336]{2,1,0:T(8,128)(2,1)} %constant.35.lat_down) | copy-start | bytes 322564
  15.2 5.5 %copy-start.3 = (bf16[224,240]{1,0:T(8,128)(2,1)S(1)}, bf16[224,240]{1,0:T(8,128)(2,1)}, u32[]{:S(2)}) copy-start(bf16[224,240]{1,0:T(8,128)(2,1)} %constant.30.lat_up) | copy-start | bytes 322564
  16.5 8.1 %collective-permute-start.4 = (f32[8,512]{1,0:T(8,128)S(1)}, f32[8,512]{1,0:T(8,128)S(1)}, u32[]{:S(2)}, u32[]{:S(2)}) collective-permute-start(f32[8,512]{1,0:T(8,128)S(1)} %get-tuple-element.67), channel_id=1, source_target_pairs={{0,12},{4,8},{8,4},{12,0},{1,13},{5,9},{9,5},{13,1},{2,14},{6,10},... | collective-permute-start | bytes 49160 | tf_op jit(solution)/shard_map/ppermute | solution.py:608
  20.6 4.0 %collective-permute-start.5 = (f32[8,512]{1,0:T(8,128)S(1)}, f32[8,512]{1,0:T(8,128)S(1)}, u32[]{:S(2)}, u32[]{:S(2)}) collective-permute-start(f32[8,512]{1,0:T(8,128)S(1)} %get-tuple-element.68), channel_id=1, source_target_pairs={{0,4},{4,0},{8,12},{12,8},{1,5},{5,1},{9,13},{13,9},{2,6},{6,2},{1... | collective-permute-start | bytes 49160 | tf_op jit(solution)/shard_map/ppermute | solution.py:608
  20.7 4.1 %copy-start.4 = (bf16[1,80,96]{2,1,0:T(8,128)(2,1)S(1)}, bf16[1,80,96]{2,1,0:T(8,128)(2,1)}, u32[]{:S(2)}) copy-start(bf16[1,80,96]{2,1,0:T(8,128)(2,1)} %constant.55.lat_down) | copy-start | bytes 46084
  20.7 4.0 %copy-start.5 = (bf16[32,240]{1,0:T(8,128)(2,1)S(1)}, bf16[32,240]{1,0:T(8,128)(2,1)}, u32[]{:S(2)}) copy-start(bf16[32,240]{1,0:T(8,128)(2,1)} %constant.50.lat_up) | copy-start | bytes 46084
  26.0 7.4 %collective-permute-start.6 = (f32[4,8,128]{2,1,0:T(8,128)S(1)}, f32[4,8,128]{2,1,0:T(8,128)S(1)}, u32[]{:S(2)}, u32[]{:S(2)}) collective-permute-start(f32[4,8,128]{2,1,0:T(8,128)S(1)} %get-tuple-element.73), channel_id=1, source_target_pairs={{0,112},{16,32},{32,16},{48,64},{64,48},{80,96},{96,80},{112,0},{1... | collective-permute-start | bytes 49160 | tf_op jit(solution)/shard_map/ppermute | solution.py:608
  28.6 5.2 %collective-permute-start.7 = (f32[4,8,128]{2,1,0:T(8,128)S(1)}, f32[4,8,128]{2,1,0:T(8,128)S(1)}, u32[]{:S(2)}, u32[]{:S(2)}) collective-permute-start(f32[4,8,128]{2,1,0:T(8,128)S(1)} %get-tuple-element.74), channel_id=1, source_target_pairs={{0,16},{16,0},{32,48},{48,32},{64,80},{80,64},{96,112},{112,96},{1... | collective-permute-start | bytes 49160 | tf_op jit(solution)/shard_map/ppermute | solution.py:608
  34.0 3.7 %collective-permute-start.8 = (f32[3,40,128]{2,1,0:T(8,128)S(1)}, f32[3,40,128]{2,1,0:T(8,128)S(1)}, u32[]{:S(2)}, u32[]{:S(2)}) collective-permute-start(f32[3,40,128]{2,1,0:T(8,128)S(1)} %get-tuple-element.76), channel_id=1, source_target_pairs={{0,3},{1,2},{2,1},{3,0},{4,7},{5,6},{6,5},{7,4},{8,11},{9,10},{10,... | collective-permute-start | bytes 184328 | tf_op jit(solution)/shard_map/ppermute | solution.py:608
  34.1 3.6 %collective-permute-start.9 = (f32[3,40,128]{2,1,0:T(8,128)S(1)}, f32[3,40,128]{2,1,0:T(8,128)S(1)}, u32[]{:S(2)}, u32[]{:S(2)}) collective-permute-start(f32[3,40,128]{2,1,0:T(8,128)S(1)} %get-tuple-element.77), channel_id=1, source_target_pairs={{0,1},{1,0},{2,3},{3,2},{4,5},{5,4},{6,7},{7,6},{8,9},{9,8},{10,11... | collective-permute-start | bytes 184328 | tf_op jit(solution)/shard_map/ppermute | solution.py:608
  38.0 5.3 %collective-permute-start.10 = (f32[8,512]{1,0:T(8,128)S(1)}, f32[8,512]{1,0:T(8,128)S(1)}, u32[]{:S(2)}, u32[]{:S(2)}) collective-permute-start(f32[8,512]{1,0:T(8,128)S(1)} %get-tuple-element.79), channel_id=1, source_target_pairs={{0,12},{4,8},{8,4},{12,0},{1,13},{5,9},{9,5},{13,1},{2,14},{6,10},... | collective-permute-start | bytes 49160 | tf_op jit(solution)/shard_map/ppermute | solution.py:608
  39.0 4.2 %collective-permute-start.11 = (f32[8,512]{1,0:T(8,128)S(1)}, f32[8,512]{1,0:T(8,128)S(1)}, u32[]{:S(2)}, u32[]{:S(2)}) collective-permute-start(f32[8,512]{1,0:T(8,128)S(1)} %get-tuple-element.80), channel_id=1, source_target_pairs={{0,4},{4,0},{8,12},{12,8},{1,5},{5,1},{9,13},{13,9},{2,6},{6,2},{1... | collective-permute-start | bytes 49160 | tf_op jit(solution)/shard_map/ppermute | solution.py:608
  44.4 7.4 %collective-permute-start.12 = (f32[4,8,128]{2,1,0:T(8,128)S(1)}, f32[4,8,128]{2,1,0:T(8,128)S(1)}, u32[]{:S(2)}, u32[]{:S(2)}) collective-permute-start(f32[4,8,128]{2,1,0:T(8,128)S(1)} %get-tuple-element.85), channel_id=1, source_target_pairs={{0,112},{16,32},{32,16},{48,64},{64,48},{80,96},{96,80},{112,0},{1... | collective-permute-start | bytes 49160 | tf_op jit(solution)/shard_map/ppermute | solution.py:608
  48.0 5.2 %collective-permute-start.13 = (f32[4,8,128]{2,1,0:T(8,128)S(1)}, f32[4,8,128]{2,1,0:T(8,128)S(1)}, u32[]{:S(2)}, u32[]{:S(2)}) collective-permute-start(f32[4,8,128]{2,1,0:T(8,128)S(1)} %get-tuple-element.86), channel_id=1, source_target_pairs={{0,16},{16,0},{32,48},{48,32},{64,80},{80,64},{96,112},{112,96},{1... | collective-permute-start | bytes 49160 | tf_op jit(solution)/shard_map/ppermute | solution.py:608
  53.4 3.7 %collective-permute-start.14 = (f32[3,40,128]{2,1,0:T(8,128)S(1)}, f32[3,40,128]{2,1,0:T(8,128)S(1)}, u32[]{:S(2)}, u32[]{:S(2)}) collective-permute-start(f32[3,40,128]{2,1,0:T(8,128)S(1)} %get-tuple-element.88), channel_id=1, source_target_pairs={{0,3},{1,2},{2,1},{3,0},{4,7},{5,6},{6,5},{7,4},{8,11},{9,10},{10,... | collective-permute-start | bytes 184328 | tf_op jit(solution)/shard_map/ppermute | solution.py:608
  53.5 3.6 %collective-permute-start.15 = (f32[3,40,128]{2,1,0:T(8,128)S(1)}, f32[3,40,128]{2,1,0:T(8,128)S(1)}, u32[]{:S(2)}, u32[]{:S(2)}) collective-permute-start(f32[3,40,128]{2,1,0:T(8,128)S(1)} %get-tuple-element.89), channel_id=1, source_target_pairs={{0,1},{1,0},{2,3},{3,2},{4,5},{5,4},{6,7},{7,6},{8,9},{9,8},{10,11... | collective-permute-start | bytes 184328 | tf_op jit(solution)/shard_map/ppermute | solution.py:608
  57.4 5.6 %collective-permute-start.16 = (f32[8,512]{1,0:T(8,128)S(1)}, f32[8,512]{1,0:T(8,128)S(1)}, u32[]{:S(2)}, u32[]{:S(2)}) collective-permute-start(f32[8,512]{1,0:T(8,128)S(1)} %get-tuple-element.91), channel_id=1, source_target_pairs={{0,12},{4,8},{8,4},{12,0},{1,13},{5,9},{9,5},{13,1},{2,14},{6,10},... | collective-permute-start | bytes 49160 | tf_op jit(solution)/shard_map/ppermute | solution.py:608
  59.8 3.7 %collective-permute-start.17 = (f32[8,512]{1,0:T(8,128)S(1)}, f32[8,512]{1,0:T(8,128)S(1)}, u32[]{:S(2)}, u32[]{:S(2)}) collective-permute-start(f32[8,512]{1,0:T(8,128)S(1)} %get-tuple-element.92), channel_id=1, source_target_pairs={{0,4},{4,0},{8,12},{12,8},{1,5},{5,1},{9,13},{13,9},{2,6},{6,2},{1... | collective-permute-start | bytes 49160 | tf_op jit(solution)/shard_map/ppermute | solution.py:608
  80.8 4.5 %collective-permute-start.18 = (f32[40,128]{1,0:T(8,128)S(1)}, f32[40,128]{1,0:T(8,128)S(1)}, u32[]{:S(2)}, u32[]{:S(2)}) collective-permute-start(f32[40,128]{1,0:T(8,128)S(1)} %get-tuple-element.97), channel_id=1, source_target_pairs={{0,3},{1,2},{2,1},{3,0},{4,7},{5,6},{6,5},{7,4},{8,11},{9,10},{10,... | collective-permute-start | bytes 61448 | tf_op jit(solution)/shard_map/ppermute | solution.py:608
  80.9 4.4 %collective-permute-start.19 = (f32[40,128]{1,0:T(8,128)S(1)}, f32[40,128]{1,0:T(8,128)S(1)}, u32[]{:S(2)}, u32[]{:S(2)}) collective-permute-start(f32[40,128]{1,0:T(8,128)S(1)} %get-tuple-element.98), channel_id=1, source_target_pairs={{0,1},{1,0},{2,3},{3,2},{4,5},{5,4},{6,7},{7,6},{8,9},{9,8},{10,11... | collective-permute-start | bytes 61448 | tf_op jit(solution)/shard_map/ppermute | solution.py:608
  81.7 3.6 %collective-permute-start.20 = (f32[8,128]{1,0:T(8,128)S(1)}, f32[8,128]{1,0:T(8,128)S(1)}, u32[]{:S(2)}, u32[]{:S(2)}) collective-permute-start(f32[8,128]{1,0:T(8,128)S(1)} %get-tuple-element.99._.lines), channel_id=1, source_target_pairs={{0,2},{1,3},{2,0},{3,1},{4,6},{5,7},{6,4},{7,5},{8,10},{9,11},{10,... | collective-permute-start | bytes 12296 | tf_op jit(solution)/shard_map/ppermute | solution.py:658
